TPU v7x, 32 devices: a whole 2x2x4 slice. The times are simulated.
32 devices in a mesh: grp: 2 (over y), gz: 4 (over z), gx: 2 (over x), row: 2 (over core).
Axes of the slice: x: 2, y: 2, z: 4, core: 2. Of those that a mesh axis runs over, the one named last changes fastest.
Arguments:
- volume: float32 [32, 512, 512], P(('grp', 'gz'), 'gx', 'row'), parts along dimension 0, may hold values from -6 to 6
- tile_table: bfloat16 [64, 128, 128], replicated, may hold values from -0.09375 to 0.09375
- tile_ids: int32 [4, 2, 2, 4, 32], P('gz', 'gx', 'row'), may hold values from 0 to 63
- block_ids: int32 [4, 2, 2, 4, 768], P('gz', 'gx', 'row'), may hold values from 0 to 2047
- live_slots: int32 [4, 2, 2, 4], P('gz', 'gx', 'row'), may hold values from 4 to 32, as said below
- measured: float32 [8, 512, 16], P(('grp', 'gz'), ('gx', 'row')), parts along dimension 0, may hold values from -12 to 12
- row_norm: float32 [4, 512, 16], P('gz', ('gx', 'row')), may hold values from 0.2 to 1
- col_norm: float32 [16, 512, 512], P('gz', 'gx', 'row'), may hold values from 0.5 to 2
Outputs:
- new_volume: float32 [32, 512, 512], P(('grp', 'gz'), 'gx', 'row'), parts along dimension 0
There are 2 independent parts, one for each index of `grp`. A program takes and returns all parts, laid end to end along the dimension named above; an argument that names none is the same for every part. Nothing has to cross between parts.
Inputs may be any that keep to these rules, and one draw needn't show every extreme that they name: `block_ids`: indices of voxel blocks of the piece itself. `live_slots`: 32 is reached by some angle of some piece in every draw.
All inputs are finite; a program needn't handle non-finite values.
Results may differ from a plain program's by a relative error of at most 0.004.
Values may be sent and summed in bfloat16 or wider, within the bound.
No kernel may reach another device: no remote copies, remote signals or barrier semaphores. Data moves between devices by JAX's collectives and lax.ppermute only.
A program may use at most 64 MiB of HBM per device.

v0:
```python
import math

import jax
import jax.numpy as jnp
from jax import lax
from jax.sharding import PartitionSpec as P


def extended_2(cells, sides, width):
    for axis, dim in sides:
        count = lax.axis_size(axis)
        ends = count - 1
        head = lax.slice_in_dim(cells, 0, width, axis=dim)
        tail = lax.slice_in_dim(cells, cells.shape[dim] - width, cells.shape[dim], axis=dim)
        cells = jnp.concatenate(
            [
                lax.ppermute(tail, axis, [(i, (i + 1) % count) for i in range(ends)]),
                cells,
                lax.ppermute(head, axis, [((i + 1) % count, i) for i in range(ends)]),
            ],
            axis=dim,
        )
    return cells


def slot_loop(slot_step, initial, tile_rows, block_rows, live_rows):
    slot_count = tile_rows.shape[1]
    position = jnp.arange(slot_count, dtype=jnp.int32)
    in_use = position[None, :] < live_rows[:, None]
    return slot_step(initial, tile_rows, block_rows, in_use)


def to_windows(row_data, slab_count, slab_depth):
    angles, columns, total_rows = row_data.shape
    padded = jnp.pad(row_data, ((0, 0), (0, 0), (1, 1)))
    head_rows = padded[:, :, :total_rows].reshape(angles, columns, slab_count, slab_depth)
    tail_rows = padded[:, :, 2:].reshape(angles, columns, slab_count, slab_depth)[
        :, :, :, slab_depth - 2 :
    ]
    joined = jnp.concatenate([head_rows, tail_rows], axis=3)
    return joined.transpose(0, 2, 1, 3)


def on_device(volume, tile_table, tile_ids, block_ids, live_slots, measured, row_norm, col_norm):
    slab_depth, column_width, half_width = volume.shape
    tile_count, tile_size = (tile_table.shape[0], tile_table.shape[1])
    angle_count = tile_ids.shape[3]
    slot_count = tile_ids.shape[4]
    window = slab_depth + 2
    block_cols = block_ids.shape[4] // (slot_count * window)
    det_width = block_cols * tile_size
    block_count = slab_depth * column_width * half_width // tile_size
    voxel_rows = volume.astype(jnp.bfloat16).reshape(block_count, tile_size)
    angle_block = math.gcd(angle_count, 2)
    step_count = angle_count // angle_block
    tile_steps = tile_ids.reshape(step_count, angle_block, slot_count)
    block_steps = block_ids.reshape(step_count, angle_block, slot_count, window, block_cols)
    live_steps = live_slots.reshape(step_count, angle_block)
    tile_numbers = jnp.arange(tile_count, dtype=jnp.int32)
    block_numbers = jnp.arange(block_count, dtype=jnp.int32)

    def pick_tiles(tile_part):
        tile_hot = (tile_part[:, :, None] == tile_numbers[None, None, :]).astype(jnp.bfloat16)
        picked = jnp.einsum(
            "akt,tdv->akdv", tile_hot, tile_table, preferred_element_type=jnp.float32
        )
        return picked.astype(jnp.bfloat16)

    def block_table(block_part, in_use):
        matches = block_part[:, :, :, :, None] == block_numbers[None, None, None, None, :]
        return (matches & in_use[:, :, None, None, None]).astype(jnp.bfloat16)

    slab_count = lax.axis_size("gz")
    own_angles, local_cols = (measured.shape[0], measured.shape[1])
    measured_win = to_windows(measured, slab_count, slab_depth).reshape(
        own_angles, slab_count, local_cols * window
    )
    norm_win = to_windows(row_norm, slab_count, slab_depth).reshape(
        own_angles, slab_count, local_cols * window
    )
    arrived = (
        lax.all_to_all(measured_win, "gz", split_axis=1, concat_axis=0, tiled=True),
        lax.all_to_all(norm_win, "gz", split_axis=1, concat_axis=0, tiled=True),
    )
    spread_out = (
        lax.all_gather(
            arrived[0].reshape(angle_count, local_cols * window), ("gx", "row"), axis=1, tiled=True
        ),
        lax.all_gather(
            arrived[1].reshape(angle_count, local_cols * window), ("gx", "row"), axis=1, tiled=True
        ),
    )
    target = spread_out[0].reshape(angle_count, det_width, window).transpose(0, 2, 1)
    weights = spread_out[1].reshape(angle_count, det_width, window).transpose(0, 2, 1)
    out_shape = (window, block_cols, tile_size)

    def project_angle_step(unused, inputs):
        tile_rows, block_rows, live_rows = inputs

        def slot_step(running, tile_part, block_part, in_use):
            picked = pick_tiles(tile_part)
            block_hot = block_table(block_part, in_use)
            voxels = jnp.einsum(
                "akwqn,nv->akwqv", block_hot, voxel_rows, preferred_element_type=jnp.float32
            )
            voxels = voxels.astype(jnp.bfloat16)
            return jnp.einsum(
                "akdv,akwqv->awqd", picked, voxels, preferred_element_type=jnp.float32
            )

        initial = jnp.zeros((angle_block,) + out_shape, jnp.float32)
        return (unused, slot_loop(slot_step, initial, tile_rows, block_rows, live_rows))

    ignored, stacked = lax.scan(
        project_angle_step, jnp.int32(0), (tile_steps, block_steps, live_steps)
    )
    partial_value = stacked.reshape((angle_count,) + out_shape).reshape(
        angle_count, window, det_width
    )
    total_proj = lax.psum(partial_value, ("gx", "row"))
    extended = extended_2(total_proj, (("gz", 1),), 2)
    folded = (
        total_proj.at[:, :2].add(extended[:, :2]).at[:, window - 2 :].add(extended[:, window + 2 :])
    )
    residual = (weights * (target - folded)).astype(jnp.bfloat16)
    res_steps = residual.reshape(step_count, angle_block, window, block_cols, tile_size)

    def back_angle_step(running_sum, inputs):
        tile_rows, block_rows, live_rows, res_rows = inputs

        def slot_step(running, tile_part, block_part, in_use):
            picked = pick_tiles(tile_part)
            block_hot = block_table(block_part, in_use)
            spread = jnp.einsum(
                "akdv,awqd->akwqv", picked, res_rows, preferred_element_type=jnp.float32
            )
            upper_part = spread.astype(jnp.bfloat16)
            lower_part = (spread - upper_part.astype(jnp.float32)).astype(jnp.bfloat16)
            added = jnp.einsum(
                "akwqn,akwqv->nv", block_hot, upper_part, preferred_element_type=jnp.float32
            )
            added = added + jnp.einsum(
                "akwqn,akwqv->nv", block_hot, lower_part, preferred_element_type=jnp.float32
            )
            return running + added

        return (slot_loop(slot_step, running_sum, tile_rows, block_rows, live_rows), None)

    initial = jnp.zeros((block_count, tile_size), jnp.float32)
    result, ignored = lax.scan(
        back_angle_step, initial, (tile_steps, block_steps, live_steps, res_steps)
    )
    return volume + col_norm * result.reshape(slab_depth, column_width, half_width)


def solution(mesh):
    placed = (
        P(("grp", "gz"), "gx", "row"),
        P(),
        P("gz", "gx", "row", None, None),
        P("gz", "gx", "row", None, None),
        P("gz", "gx", "row", None),
        P(("grp", "gz"), ("gx", "row"), None),
        P("gz", ("gx", "row"), None),
        P("gz", "gx", "row"),
    )
    return jax.shard_map(
        on_device,
        mesh=mesh,
        in_specs=placed,
        out_specs=P(("grp", "gz"), "gx", "row"),
        check_vma=False,
    )
```

profile of v0, /device:TPU:9, one launch (start us, length us, event | category | flops | bytes accessed | tf_op | source)
XLA Modules:
  0.0 90.5 jit_solution(14383756225101299012)
XLA Ops:
  0.0 3.0 %copy.90 = bf16[64,128,128]{2,0,1:T(8,128)(2,1)S(1)} copy(bf16[64,128,128]{2,1,0:T(8,128)(2,1)} %param.17) | data formatting | bytes 4194304
  4.7 1.3 %convert_element_type.31 = bf16[4,256,256]{2,1,0:T(8,128)(2,1)S(1)} convert(f32[4,256,256]{2,1,0:T(8,128)} %param.16) | non-fusion elementwise | flops 262144 | bytes 1572864 | tf_op jit(solution)/shard_map/convert_element_type | solution.py:53
  6.0 1.0 %reshape.190 = bf16[2048,128]{1,0:T(8,128)(2,1)} reshape(bf16[4,256,256]{2,1,0:T(8,128)(2,1)S(1)} %convert_element_type.31) | data formatting | bytes 1048576 | tf_op jit(solution)/shard_map/reshape | solution.py:53
  7.0 12.0 %while.24 = (s32[]{:T(128)}, f32[2,2,6,4,128]{4,3,1,0,2:T(4,128)S(1)}, s32[2,2,32,6,4]{2,4,3,1,0:T(4,128)S(1)}, s32[2,2]{1,0:T(2,128)S(1)}, bf16[2048,128]{1,0:T...) while((s32[]{:T(128)}, ...), condition=%wide.region_1.2_spmd.clone, body=%wide.region_0.1_spmd.clone.sunk | while | flops 997396544 | bytes 7703549 | solution.py:114
  7.0 3.8 %fusion.102 = bf16[2,32,6,4,128]{4,1,3,2,0:T(8,128)(2,1)S(1)} fusion(s32[2,32,6,4]{1,3,2,0:T(4,128)S(1)} %dynamic-slice_bitcast_fusion.6, pred[2,32]{1,0:T(4,128)(4,1)S(1)} %iota_compare_fusion.8, bf16[2048,128]{1,0:T(8,128)(2,1)} %get-tuple-element.373), kind=kOutput, calls=%fused_computation.14.clone.1 | convolution fusion | flops 811794432 | bytes 923712 | tf_op jit(solution)/shard_map/while/body/eval_jaxpr/akwqn,nv->akwqv/dot_general | solution.py:103
  10.8 0.8 convert_bitcast_fusion.4
  11.6 1.3 %fusion.103 = f32[1,2,6,4,128]{4,2,3,1,0:T(8,128)S(1)} fusion(bf16[2,32,128,128,1]{3,1,2,0,4:T(8,128)(2,1)S(1)} %convert_bitcast_fusion.4, bf16[2,32,6,4,128]{4,1,3,2,0:T(8,128)(2,1)S(1)} %fusion.102), kind=kOutput, calls=%fused_computation.15.clone.1 | convolution fusion | flops 50331648 | bytes 2514944 | tf_op jit(solution)/shard_map/while/body/eval_jaxpr/akdv,akwqv->awqd/dot_general | solution.py:107
  13.1 3.8 %fusion.102 = bf16[2,32,6,4,128]{4,1,3,2,0:T(8,128)(2,1)S(1)} fusion(s32[2,32,6,4]{1,3,2,0:T(4,128)S(1)} %dynamic-slice_bitcast_fusion.6, pred[2,32]{1,0:T(4,128)(4,1)S(1)} %iota_compare_fusion.8, bf16[2048,128]{1,0:T(8,128)(2,1)} %get-tuple-element.373), kind=kOutput, calls=%fused_computation.14.clone.1 | convolution fusion | flops 811794432 | bytes 923712 | tf_op jit(solution)/shard_map/while/body/eval_jaxpr/akwqn,nv->akwqv/dot_general | solution.py:103
  16.9 0.8 convert_bitcast_fusion.4
  17.6 1.3 %fusion.103 = f32[1,2,6,4,128]{4,2,3,1,0:T(8,128)S(1)} fusion(bf16[2,32,128,128,1]{3,1,2,0,4:T(8,128)(2,1)S(1)} %convert_bitcast_fusion.4, bf16[2,32,6,4,128]{4,1,3,2,0:T(8,128)(2,1)S(1)} %fusion.102), kind=kOutput, calls=%fused_computation.15.clone.1 | convolution fusion | flops 50331648 | bytes 2514944 | tf_op jit(solution)/shard_map/while/body/eval_jaxpr/akdv,akwqv->awqd/dot_general | solution.py:107
  19.0 10.7 %psum.7 = f32[4,6,512]{2,0,1:T(4,128)S(1)} all-reduce(f32[4,6,512]{2,0,1:T(4,128)S(1)} %reshape_reshape.3), channel_id=1, replica_groups=mesh['grp'=2,'gz'=4,'gx'=2,'row'=2] {'gx','row'}, use_global_device_ids=true, to_apply=%region_2.3 | all-reduce | flops 12288 | bytes 98304 | tf_op jit(solution)/shard_map/psum | solution.py:120
  29.7 3.2 %collective-permute-start = (f32[4,2,512]{2,0,1:T(4,128)S(1)}, f32[4,2,512]{2,0,1:T(4,128)S(1)}, u32[]{:S(2)}, u32[]{:S(2)}) collective-permute-start(f32[4,2,512]{2,0,1:T(4,128)S(1)} %slice.82), channel_id=1, source_target_pairs={{0,4},{4,8},{8,12},{1,5},{5,9},{9,13},{2,6},{6,10},{10,14},{3,7},{... | collective-permute-start | bytes 49160 | tf_op jit(solution)/shard_map/ppermute | solution.py:17
  33.2 0.8 reshape.209
  34.0 3.7 %all-to-all-start = ((f32[1,4,768]{2,0,1:T(1,128)}), f32[1,4,768]{2,0,1:T(1,128)S(1)}, u32[]{:S(2)}, u32[]{:S(2)}) async-start(f32[1,4,768]{2,0,1:T(1,128)} %reshape.209), calls=%async_computation | async-start | bytes 24576 | tf_op jit(solution)/shard_map/all_to_all | solution.py:83
  38.2 0.8 reshape.210
  39.0 1.9 %collective-permute-start.1 = (f32[4,2,512]{2,0,1:T(4,128)S(1)}, f32[4,2,512]{2,0,1:T(4,128)S(1)}, u32[]{:S(2)}, u32[]{:S(2)}) collective-permute-start(f32[4,2,512]{2,0,1:T(4,128)S(1)} %get-tuple-element.261), channel_id=1, source_target_pairs={{4,0},{8,4},{12,8},{5,1},{9,5},{13,9},{6,2},{10,6},{14,10},{7,3},{... | collective-permute-start | bytes 49160 | tf_op jit(solution)/shard_map/ppermute | solution.py:19
  41.0 4.7 %all-to-all-start.1 = ((f32[1,4,768]{2,0,1:T(1,128)}), f32[1,4,768]{2,0,1:T(1,128)S(1)}, u32[]{:S(2)}, u32[]{:S(2)}) async-start(f32[1,4,768]{2,0,1:T(1,128)} %reshape.210), calls=%async_computation.1 | async-start | bytes 24576 | tf_op jit(solution)/shard_map/all_to_all | solution.py:82
  45.7 8.4 %all-gather = f32[1,4,3072]{2,0,1:T(1,128)S(1)} all-gather(f32[1,4,768]{2,0,1:T(1,128)S(1)} %all-to-all-done), channel_id=2, replica_groups=mesh['grp'=2,'gz'=4,'gx'=2,'row'=2] {'gx','row'}, dimensions={2}, use_global_device_ids=true | all-gather | bytes 61440 | tf_op jit(solution)/shard_map/all_gather | solution.py:89
  54.3 1.0 %reshape.184 = f32[4,512,6]{2,1,0:T(8,128)S(1)} reshape(f32[4,3072]{1,0:T(4,128)S(1)} %reduce.5) | data formatting | bytes 98304 | tf_op jit(solution)/shard_map/reshape | solution.py:94
  55.7 5.4 %all-gather.1 = f32[1,4,3072]{2,0,1:T(1,128)S(1)} all-gather(f32[1,4,768]{2,0,1:T(1,128)S(1)} %all-to-all-done.1), channel_id=3, replica_groups=mesh['grp'=2,'gz'=4,'gx'=2,'row'=2] {'gx','row'}, dimensions={2}, use_global_device_ids=true | all-gather | bytes 61440 | tf_op jit(solution)/shard_map/all_gather | solution.py:86
  61.2 1.0 %reshape.189 = f32[4,512,6]{2,1,0:T(8,128)S(1)} reshape(f32[4,3072]{1,0:T(4,128)S(1)} %reduce.6) | data formatting | bytes 98304 | tf_op jit(solution)/shard_map/reshape | solution.py:93
  62.7 24.8 %while.25 = (s32[]{:T(128)}, f32[2048,128]{1,0:T(8,128)}, s32[2,2,32,6,4]{2,3,4,1,0:T(8,128)S(1)}, s32[2,2]{1,0:T(2,128)S(1)}, bf16[2,2,6,4,128]{4,3,1,0,2:T(4,1...) while((s32[]{:T(128)}, f32[2048,128]{1,0:T(8,128)}, ...), condition=%wide.region_4.5_spmd.clone, body=%wide.region_3.4_spmd.clone.sunk | while | flops 1810370560 | bytes 12907599 | solution.py:150
  62.7 0.7 convert_bitcast_fusion.5
  63.5 0.7 fusion.113
  64.3 4.7 %fusion.114 = f32[2048,128]{1,0:T(8,128)} fusion(s32[2,32,6,4]{1,2,3,0:T(8,128)S(1)} %dynamic-slice_bitcast_fusion.7, pred[2,32]{1,0:T(4,128)(4,1)S(1)} %iota_compare_fusion.9, f32[2,6,4,32,128]{4,1,3,2,0:T(8,128)S(1)} %fusion.113), kind=kOutput, calls=%fused_computation.36.clone.1 | convolution fusion | flops 811597824 | bytes 1841216 | tf_op jit(solution)/shard_map/while/body/eval_jaxpr/akwqn,akwqv->nv/dot_general | solution.py:139
  69.0 5.9 %fusion.115 = f32[2048,128]{1,0:T(8,128)} fusion(f32[2048,128]{1,0:T(8,128)} %fusion.114, s32[2,32,6,4]{1,2,3,0:T(8,128)S(1)} %dynamic-slice_bitcast_fusion.7, pred[2,32]{1,0:T(4,128)(4,1)S(1)} %iota_compare_fusion.9, f32[2048,128]{1,0:T(8,128)} %get-tuple-element.387, pred[]{:T(512)S(6)} %compare.16, f32[2,6,4,32,128]{4,1,3,2,0:T(8,128)S(1)} %fusion.113), kind=kOutput, calls=%fused_computation.39.clone.1 | convolution fusion | flops 813170688 | bytes 3938369 | tf_op jit(solution)/shard_map/while/body/eval_jaxpr/akwqn,akwqv->nv/dot_general | solution.py:142
  74.9 0.8 convert_bitcast_fusion.5
  75.7 0.7 fusion.113
  76.6 4.7 %fusion.114 = f32[2048,128]{1,0:T(8,128)} fusion(s32[2,32,6,4]{1,2,3,0:T(8,128)S(1)} %dynamic-slice_bitcast_fusion.7, pred[2,32]{1,0:T(4,128)(4,1)S(1)} %iota_compare_fusion.9, f32[2,6,4,32,128]{4,1,3,2,0:T(8,128)S(1)} %fusion.113), kind=kOutput, calls=%fused_computation.36.clone.1 | convolution fusion | flops 811597824 | bytes 1841216 | tf_op jit(solution)/shard_map/while/body/eval_jaxpr/akwqn,akwqv->nv/dot_general | solution.py:139
  81.3 6.2 %fusion.115 = f32[2048,128]{1,0:T(8,128)} fusion(f32[2048,128]{1,0:T(8,128)} %fusion.114, s32[2,32,6,4]{1,2,3,0:T(8,128)S(1)} %dynamic-slice_bitcast_fusion.7, pred[2,32]{1,0:T(4,128)(4,1)S(1)} %iota_compare_fusion.9, f32[2048,128]{1,0:T(8,128)} %get-tuple-element.387, pred[]{:T(512)S(6)} %compare.16, f32[2,6,4,32,128]{4,1,3,2,0:T(8,128)S(1)} %fusion.113), kind=kOutput, calls=%fused_computation.39.clone.1 | convolution fusion | flops 813170688 | bytes 3938369 | tf_op jit(solution)/shard_map/while/body/eval_jaxpr/akwqn,akwqv->nv/dot_general | solution.py:142
  87.5 1.7 %reshape.193 = f32[4,256,256]{2,1,0:T(8,128)S(1)} reshape(f32[2048,128]{1,0:T(8,128)} %get-tuple-element.124) | data formatting | bytes 2097152 | tf_op jit(solution)/shard_map/reshape | solution.py:153
  89.4 1.2 %multiply_add_fusion = f32[4,256,256]{2,1,0:T(8,128)} fusion(f32[4,256,256]{2,1,0:T(8,128)S(1)} %copy-done, f32[4,256,256]{2,1,0:T(8,128)S(1)} %copy-done.1, f32[4,256,256]{2,1,0:T(8,128)S(1)} %reshape.193), kind=kLoop, calls=%fused_computation.60 | loop fusion | flops 524288 | bytes 4194304 | tf_op jit(solution)/shard_map/add | solution.py:153
  (68 shorter events, 4.1 us)
Async XLA Ops:
  0.0 3.0 %copy-start.3 = (s32[1,1,1,4,768]{4,3,2,1,0:T(4,128)S(1)}, s32[1,1,1,4,768]{4,3,2,1,0:T(4,128)}, u32[]{:S(2)}) copy-start(s32[1,1,1,4,768]{4,3,2,1,0:T(4,128)} %param.19) | copy-start | bytes 36868
  0.0 3.9 %copy-start.6 = (s32[1,1,1,4]{3,2,1,0:T(1,128)S(1)}, s32[1,1,1,4]{3,2,1,0:T(1,128)}, u32[]{:S(2)}) copy-start(s32[1,1,1,4]{3,2,1,0:T(1,128)} %param.20) | copy-start | bytes 52
  3.0 4.0 %copy-start.2 = (s32[1,1,1,4,32]{4,3,2,1,0:T(4,128)S(1)}, s32[1,1,1,4,32]{4,3,2,1,0:T(4,128)}, u32[]{:S(2)}) copy-start(s32[1,1,1,4,32]{4,3,2,1,0:T(4,128)} %param.18) | copy-start | bytes 1540
  6.9 26.0 %copy-start.4 = (f32[1,128,16]{1,2,0:T(8,128)S(1)}, f32[1,128,16]{1,2,0:T(8,128)}, u32[]{:S(2)}) copy-start(f32[1,128,16]{1,2,0:T(8,128)} %param.22) | copy-start | bytes 24580
  6.9 30.7 %copy-start.5 = (f32[1,128,16]{1,2,0:T(8,128)S(1)}, f32[1,128,16]{1,2,0:T(8,128)}, u32[]{:S(2)}) copy-start(f32[1,128,16]{1,2,0:T(8,128)} %param.21) | copy-start | bytes 24580
  29.7 9.2 %collective-permute-start = (f32[4,2,512]{2,0,1:T(4,128)S(1)}, f32[4,2,512]{2,0,1:T(4,128)S(1)}, u32[]{:S(2)}, u32[]{:S(2)}) collective-permute-start(f32[4,2,512]{2,0,1:T(4,128)S(1)} %slice.82), channel_id=1, source_target_pairs={{0,4},{4,8},{8,12},{1,5},{5,9},{9,13},{2,6},{6,10},{10,14},{3,7},{... | collective-permute-start | bytes 49160 | tf_op jit(solution)/shard_map/ppermute | solution.py:17
  34.0 7.1 %all-to-all-start = ((f32[1,4,768]{2,0,1:T(1,128)}), f32[1,4,768]{2,0,1:T(1,128)S(1)}, u32[]{:S(2)}, u32[]{:S(2)}) async-start(f32[1,4,768]{2,0,1:T(1,128)} %reshape.209), calls=%async_computation | async-start | bytes 24576 | tf_op jit(solution)/shard_map/all_to_all | solution.py:83
  39.0 23.6 %collective-permute-start.1 = (f32[4,2,512]{2,0,1:T(4,128)S(1)}, f32[4,2,512]{2,0,1:T(4,128)S(1)}, u32[]{:S(2)}, u32[]{:S(2)}) collective-permute-start(f32[4,2,512]{2,0,1:T(4,128)S(1)} %get-tuple-element.261), channel_id=1, source_target_pairs={{4,0},{8,4},{12,8},{5,1},{9,5},{13,9},{6,2},{10,6},{14,10},{7,3},{... | collective-permute-start | bytes 49160 | tf_op jit(solution)/shard_map/ppermute | solution.py:19
  41.0 14.7 %all-to-all-start.1 = ((f32[1,4,768]{2,0,1:T(1,128)}), f32[1,4,768]{2,0,1:T(1,128)S(1)}, u32[]{:S(2)}, u32[]{:S(2)}) async-start(f32[1,4,768]{2,0,1:T(1,128)} %reshape.210), calls=%async_computation.1 | async-start | bytes 24576 | tf_op jit(solution)/shard_map/all_to_all | solution.py:82
  87.5 1.7 %copy-start = (f32[4,256,256]{2,1,0:T(8,128)S(1)}, f32[4,256,256]{2,1,0:T(8,128)}, u32[]{:S(2)}) copy-start(f32[4,256,256]{2,1,0:T(8,128)} %param.16) | copy-start | bytes 3145732
  87.5 1.9 %copy-start.1 = (f32[4,256,256]{2,1,0:T(8,128)S(1)}, f32[4,256,256]{2,1,0:T(8,128)}, u32[]{:S(2)}) copy-start(f32[4,256,256]{2,1,0:T(8,128)} %param.23) | copy-start | bytes 3145732
where the time goes:
time: 91.6 us; the launch traced here: 90.5 us
  matrix products  36.2 us (40%)
  blocking collectives  24.5 us (27%)
  starting transfers between devices  13.6 us (15%)
  local copies, waits for them, and re-layouts  12 us (13%)
  other arithmetic  3.73 us (4%)
    dot_general x2, matrix products, slot_step(): jnp.einsum('akwqn,akwqv->nv', block_hot, lower_part, preferred_element_ty...  12.2 us
    psum x1, blocking collectives, on_device(): total_proj = lax.psum(partial_value, ('gx', 'row'))  10.7 us
    dot_general x2, matrix products, slot_step(): jnp.einsum('akwqn,akwqv->nv', block_hot, upper_part, preferred_element_ty...  9.4 us
    all_gather x1, blocking collectives, on_device(): lax.all_gather(arrived[1].reshape(angle_count, local_cols * window), ('gx...  8.43 us
    dot_general x2, matrix products, slot_step(): jnp.einsum('akwqn,nv->akwqv', block_hot, voxel_rows, preferred_element_ty...  7.55 us
    all_gather x1, blocking collectives, on_device(): lax.all_gather(arrived[0].reshape(angle_count, local_cols * window), ('gx...  5.38 us
    all_to_all x1, starting transfers between devices, on_device(): lax.all_to_all(measured_win, 'gz', split_axis=1, concat_axis=0, tiled=True)  4.71 us
    unnamed x18, local copies, waits for them, and re-layouts  4.17 us
  transfers between devices with their start and end apart: 4, of which 1 were waited for; matrix products, arithmetic and copies ran while one was open for 6% of the time, Pallas kernels for 0%

commit v1 on v0

v1 whole, which is shorter than its diff:
```python
import functools

import jax
import jax.numpy as jnp
from jax import lax
from jax.experimental import pallas as pl
from jax.experimental.pallas import tpu as pltpu
from jax.sharding import PartitionSpec as P

ONE_HOT = 256
GROUP = 8
VMEM_LIMIT = 32 * 1024 * 1024


def forward_kernel(rows, live, tid, bid, vol, tiles, out, vox, picked):
    angles, slots = tid.shape
    tile = tiles.shape[1]
    lines, width = vol.shape
    runs = width // tile
    step = 8
    for run in range(runs):
        for line in range(0, lines, step):
            vox[pl.ds(line * runs + run, step, stride=runs), :] = vol[
                line : line + step, run * tile : (run + 1) * tile
            ]

    def gather_angle(a, carry):
        def pair(i, inner):
            for u in range(2):
                k = i * 2 + u
                base = (a * slots + k) * rows
                for r in range(rows):
                    picked[pl.ds(base + r, 1), :] = vox[pl.ds(bid[a, k * rows + r], 1), :]
            return inner

        return lax.fori_loop(0, (live[a] + 1) // 2, pair, carry)

    lax.fori_loop(0, angles, gather_angle, 0)

    def project_angle(a, carry):
        count = live[a]

        def group(g, total):
            left, right = [], []
            for u in range(GROUP):
                k = g * GROUP + u
                part = picked[pl.ds(pl.multiple_of((a * slots + k) * rows, 8), rows), :]
                left.append(jnp.where(k < count, part, 0.0).astype(jnp.bfloat16))
                right.append(tiles[tid[a, k]])
            return total + lax.dot_general(
                jnp.concatenate(left, axis=1),
                jnp.concatenate(right, axis=1),
                (((1,), (1,)), ((), ())),
                preferred_element_type=jnp.float32,
            )

        total = lax.fori_loop(
            0, (count + GROUP - 1) // GROUP, group, jnp.zeros((rows, tile), jnp.float32)
        )
        out[pl.ds(pl.multiple_of(a * rows, 8), rows), :] = total
        return carry

    lax.fori_loop(0, angles, project_angle, 0)


def index_kernel(rows, runs, live, bid, hot, code):
    angles, length = bid.shape
    tile = code.shape[1]
    place = lax.broadcasted_iota(jnp.int32, (ONE_HOT, length), 0)
    position = lax.broadcasted_iota(jnp.int32, (1, length), 1)
    for a in range(angles):
        block = bid[a : a + 1, :]
        line = block // runs
        hot[a] = jnp.where(place == line % ONE_HOT, 1.0, 0.0).astype(jnp.bfloat16)
        group = (line // ONE_HOT) * runs + block % runs
        group = jnp.where(position < live[a] * rows, group, -1).astype(jnp.float32)
        for c in range(length // tile):
            wide = jnp.broadcast_to(group[:, c * tile : (c + 1) * tile], (tile, tile))
            code[a * length + c * tile : a * length + (c + 1) * tile, :] = wide.T.astype(
                jnp.bfloat16
            )


def backward_kernel(
    rows, live, tid, base, up, down, weight, tiles, hot, code, vol, col, out, res, spread, total
):
    angles, slots = tid.shape
    tile = tiles.shape[1]
    lines, width = vol.shape
    runs = width // tile
    rim = up.shape[0] // angles
    length = slots * rows
    for a in range(angles):
        own = base[a * rows : (a + 1) * rows, :]
        whole = jnp.concatenate(
            [
                own[:rim] + up[a * rim : (a + 1) * rim, :],
                own[rim : rows - rim],
                own[rows - rim :] + down[a * rim : (a + 1) * rim, :],
            ],
            axis=0,
        )
        res[a] = (weight[a * rows : (a + 1) * rows, :] * whole).astype(jnp.bfloat16)

    def spread_angle(a, carry):
        values = res[a]

        def group(g, inner):
            for u in range(0, GROUP, 2):
                k = g * GROUP + u
                pair = jnp.concatenate([tiles[tid[a, k]], tiles[tid[a, k + 1]]], axis=1)
                made = jnp.dot(values, pair, preferred_element_type=jnp.float32)
                both = jnp.concatenate([made[:, :tile], made[:, tile:]], axis=0)
                at = pl.multiple_of((a * slots + k) * rows, 16)
                spread[pl.ds(at, 2 * rows), :] = both.astype(jnp.bfloat16)
            return inner

        return lax.fori_loop(0, (live[a] + GROUP - 1) // GROUP, group, carry)

    lax.fori_loop(0, angles, spread_angle, 0)

    for chunk in range(lines // ONE_HOT):

        def add_angle(a, carry):
            at = pl.multiple_of(a * length, 128)
            values = spread[pl.ds(at, length), :]
            groups = code[pl.ds(at, length), :]
            right = jnp.concatenate(
                [
                    jnp.where(groups == jnp.bfloat16(chunk * runs + run), values, jnp.bfloat16(0))
                    for run in range(runs)
                ],
                axis=1,
            )
            made = jnp.dot(hot[a], right, preferred_element_type=jnp.float32)

            @pl.when(a == 0)
            def _():
                total[...] = made

            @pl.when(a > 0)
            def _():
                total[...] += made

            return carry

        lax.fori_loop(0, angles, add_angle, 0)
        here = slice(chunk * ONE_HOT, (chunk + 1) * ONE_HOT)
        out[here, :] = vol[here, :] + col[here, :] * total[...]


def swap(values, axis, bit):
    return lax.ppermute(values, axis, [(i, i ^ bit) for i in range(lax.axis_size(axis))])


def bits(axis):
    return [1 << i for i in range((lax.axis_size(axis) - 1).bit_length())]


def windows(data, slab_count, slab_depth, edge):
    padded = jnp.pad(data, ((0, 0), (1, 1), (0, 0)))
    parts = []
    for s in range(slab_count):
        part = padded[:, s * slab_depth : s * slab_depth + slab_depth + 2]
        if not edge:
            part = jnp.pad(part[:, 1:-1], ((0, 0), (1, 1), (0, 0)))
        parts.append(part)
    return jnp.stack(parts)


def on_device(volume, tile_table, tile_ids, block_ids, live_slots, measured, row_norm, col_norm):
    slab_depth, column_width, half_width = volume.shape
    tile_count, tile_size = (tile_table.shape[0], tile_table.shape[1])
    angle_count, slot_count = tile_ids.shape[3:]
    window = slab_depth + 2
    block_cols = block_ids.shape[4] // (slot_count * window)
    rows = window * block_cols
    rim = 2 * block_cols
    length = slot_count * rows
    lines = slab_depth * column_width
    runs = half_width // tile_size
    slab_count = lax.axis_size("gz")
    own_angles, local_cols = (measured.shape[0], measured.shape[1])

    tid = tile_ids.reshape(angle_count, slot_count)
    bid = block_ids.reshape(angle_count, length)
    live = live_slots.reshape(angle_count)
    vol = volume.reshape(lines, half_width)
    col = col_norm.reshape(lines, half_width)

    smem = pl.BlockSpec(memory_space=pltpu.SMEM)
    vmem = pl.BlockSpec(memory_space=pltpu.VMEM)
    params = pltpu.CompilerParams(vmem_limit_bytes=VMEM_LIMIT)

    me_z = lax.axis_index("gz")
    sends = jnp.concatenate(
        [
            windows(measured.transpose(0, 2, 1), slab_count, slab_depth, False),
            windows(row_norm.transpose(0, 2, 1), slab_count, slab_depth, True),
        ],
        axis=2,
    )
    got = [lax.dynamic_index_in_dim(sends, me_z, 0, False)]
    for step in range(1, slab_count):
        got.append(swap(lax.dynamic_index_in_dim(sends, me_z ^ step, 0, False), "gz", step))
    got = jnp.stack(got)
    arrived = jnp.concatenate(
        [lax.dynamic_index_in_dim(got, me_z ^ i, 0, False) for i in range(slab_count)], axis=0
    )
    target = arrived[:, :window]
    weight = arrived[:, window:][None]

    partial = pl.pallas_call(
        functools.partial(forward_kernel, rows),
        out_shape=jax.ShapeDtypeStruct((angle_count * rows, tile_size), jnp.float32),
        in_specs=[smem, smem, smem, vmem, vmem],
        out_specs=vmem,
        scratch_shapes=[
            pltpu.VMEM((lines * runs, tile_size), jnp.float32),
            pltpu.VMEM((angle_count * length, tile_size), jnp.float32),
        ],
        compiler_params=params,
        name="forward",
    )(live, tid, bid, vol, tile_table)

    hot, code = pl.pallas_call(
        functools.partial(index_kernel, rows, runs),
        out_shape=(
            jax.ShapeDtypeStruct((angle_count, ONE_HOT, length), jnp.bfloat16),
            jax.ShapeDtypeStruct((angle_count * length, tile_size), jnp.bfloat16),
        ),
        in_specs=[smem, vmem],
        out_specs=(vmem, vmem),
        compiler_params=params,
        name="index",
    )(live, bid)

    place = lax.axis_index("gx") * lax.axis_size("row") + lax.axis_index("row")
    if local_cols == tile_size:
        mine = lax.broadcasted_iota(jnp.int32, (1, 1, block_cols, 1), 2) == place
        spot = jnp.where(mine, target[:, :, None, :], 0.0)
    else:
        spot = jnp.zeros((angle_count, window, block_cols * tile_size), jnp.float32)
        spot = lax.dynamic_update_slice_in_dim(spot, target, place * local_cols, 2)
        spot = spot.reshape(angle_count, window, block_cols, tile_size)
    total = spot.reshape(angle_count * rows, tile_size) - partial
    for axis in ("row", "gx"):
        here = lax.axis_index(axis)
        for bit in bits(axis):
            other = swap(total, axis, bit)
            other_weight = swap(weight, axis, bit)
            total = total + other
            high = (here & bit) != 0
            weight = jnp.concatenate(
                [jnp.where(high, other_weight, weight), jnp.where(high, weight, other_weight)],
                axis=0,
            )
    weight = weight.transpose(1, 2, 0, 3).reshape(angle_count * rows, tile_size)
    blocks = total.reshape(angle_count, rows, tile_size)
    head = blocks[:, :rim].reshape(angle_count * rim, tile_size)
    tail = blocks[:, rows - rim :].reshape(angle_count * rim, tile_size)
    odd = (me_z & 1) == 1
    first = [(i, i ^ 1) for i in range(slab_count)]
    second = [(i, ((i + 1) ^ 1) - 1) for i in range(1, slab_count - 1)]
    one = lax.ppermute(jnp.where(odd, head, tail), "gz", first)
    two = lax.ppermute(jnp.where(odd, tail, head), "gz", second)
    up = jnp.where(odd, one, two)
    down = jnp.where(odd, two, one)

    made = pl.pallas_call(
        functools.partial(backward_kernel, rows),
        out_shape=jax.ShapeDtypeStruct((lines, half_width), jnp.float32),
        in_specs=[smem, smem] + [vmem] * 9,
        out_specs=vmem,
        scratch_shapes=[
            pltpu.VMEM((angle_count, rows, tile_size), jnp.bfloat16),
            pltpu.VMEM((angle_count * length, tile_size), jnp.bfloat16),
            pltpu.VMEM((ONE_HOT, half_width), jnp.float32),
        ],
        compiler_params=params,
        name="backward",
    )(live, tid, total, up, down, weight, tile_table, hot, code, vol, col)
    return made.reshape(slab_depth, column_width, half_width)


def solution(mesh):
    placed = (
        P(("grp", "gz"), "gx", "row"),
        P(),
        P("gz", "gx", "row", None, None),
        P("gz", "gx", "row", None, None),
        P("gz", "gx", "row", None),
        P(("grp", "gz"), ("gx", "row"), None),
        P("gz", ("gx", "row"), None),
        P("gz", "gx", "row"),
    )
    return jax.shard_map(
        on_device,
        mesh=mesh,
        in_specs=placed,
        out_specs=P(("grp", "gz"), "gx", "row"),
        check_vma=False,
    )
```

time: 91.6 us -> 51.7 us (0.56)
  the two profiles are of different devices: /device:TPU:9 before, /device:TPU:0 now
where the time goes in v1:
time: 51.7 us; the launch traced here: 51.6 us
  Pallas kernels  19.3 us (37%)
  starting transfers between devices  14.3 us (28%)
  local copies, waits for them, and re-layouts  12.5 us (24%)
  waiting for transfers between devices  5.06 us (10%)
    unnamed x30, local copies, waits for them, and re-layouts  10.7 us
    pallas_call x1, Pallas kernels, on_device(): pl.pallas_call(functools.partial(backward_kernel, rows), out_shape=jax.Sh...  8.96 us
    pallas_call x1, Pallas kernels, on_device(): pl.pallas_call(functools.partial(forward_kernel, rows), out_shape=jax.Sha...  8.9 us
    ppermute x7, starting transfers between devices, swap(): lax.ppermute(values, axis, [(i, i ^ bit) for i in range(lax.axis_size(axi...  8.57 us
    ppermute x1, starting transfers between devices, on_device(): one = lax.ppermute(jnp.where(odd, head, tail), 'gz', first)  5.1 us
    ppermute x7, waiting for transfers between devices, swap(): lax.ppermute(values, axis, [(i, i ^ bit) for i in range(lax.axis_size(axi...  3.39 us
    ppermute x1, waiting for transfers between devices, on_device(): one = lax.ppermute(jnp.where(odd, head, tail), 'gz', first)  1.67 us
    pallas_call x1, Pallas kernels, on_device(): pl.pallas_call(functools.partial(index_kernel, rows, runs), out_shape=(ja...  1.42 us
  transfers between devices with their start and end apart: 9, of which 3 were waited for; matrix products, arithmetic and copies ran while one was open for 1% of the time, Pallas kernels for 20%

profile of v1, /device:TPU:0, one launch (start us, length us, event | category | flops | bytes accessed | tf_op | source)
XLA Modules:
  0.0 51.6 jit_solution(17936001869765001037)
XLA Ops:
  0.0 0.8 %fusion.2 = (f32[1,4,128]{2,1,0:T(4,128)S(1)}, f32[1,4,128]{2,1,0:T(4,128)S(1)}, f32[1,4,128]{2,1,0:T(4,128)S(1)}, f32[1,4,128]{2,1,0:T(4,128)S(1)}) fusion(f32[1,16,128]{2,1,0:T(8,128)} %bitcast.62), kind=kLoop, calls=%fused_computation.34 | loop fusion | bytes 16384 | tf_op jit(solution)/shard_map/slice | solution.py:166
  0.8 0.8 %fusion = (f32[1,1,6,128]{3,2,1,0:T(8,128)S(1)}, f32[1,1,6,128]{3,2,1,0:T(8,128)S(1)}, f32[1,1,6,128]{3,2,1,0:T(8,128)S(1)}, f32[1,1,6,128]{3,2,1,0:T(8,128)S(1)}) fusion(f32[1,16,128]{2,1,0:T(8,128)} %bitcast.61), kind=kLoop, calls=%fused_computation.20 | loop fusion | bytes 28672 | tf_op jit(solution)/shard_map/stack | solution.py:168
  1.7 5.1 %collective-permute-start.2 = (f32[1,12,128]{2,1,0:T(8,128)S(1)}, f32[1,12,128]{2,1,0:T(8,128)S(1)}, u32[]{:S(2)}, u32[]{:S(2)}) collective-permute-start(f32[1,12,128]{2,1,0:T(8,128)S(1)} %get-tuple-element.22), channel_id=1, source_target_pairs={{0,12},{4,8},{8,4},{12,0},{1,13},{5,9},{9,5},{13,1},{2,14},{6,10},... | collective-permute-start | bytes 18440 | tf_op jit(solution)/shard_map/ppermute | solution.py:153
  6.8 0.6 %collective-permute-start = (f32[1,12,128]{2,1,0:T(8,128)S(1)}, f32[1,12,128]{2,1,0:T(8,128)S(1)}, u32[]{:S(2)}, u32[]{:S(2)}) collective-permute-start(f32[1,12,128]{2,1,0:T(8,128)S(1)} %get-tuple-element.24), channel_id=1, source_target_pairs={{0,4},{4,0},{8,12},{12,8},{1,5},{5,1},{9,13},{13,9},{2,6},{6,2},{1... | collective-permute-start | bytes 18440 | tf_op jit(solution)/shard_map/ppermute | solution.py:153
  7.5 0.1 broadcast_in_dim.31
  7.6 0.0 copy-start
  7.6 1.6 %copy-done = bf16[64,128,128]{2,1,0:T(8,128)(2,1)S(1)} copy-done((bf16[64,128,128]{2,1,0:T(8,128)(2,1)S(1)}, bf16[64,128,128]{2,1,0:T(8,128)(2,1)}, u32[]{:S(2)}) %copy-start) | copy-done | bytes 2097176
  9.2 1.2 %copy-done.2 = f32[4,256,256]{2,1,0:T(8,128)S(1)} copy-done((f32[4,256,256]{2,1,0:T(8,128)S(1)}, f32[4,256,256]{2,1,0:T(8,128)}, u32[]{:S(2)}) %copy-start.2) | copy-done | bytes 1048600
  10.4 0.7 %copy-done.9 = s32[1,1,1,4,768]{4,3,2,1,0:T(4,128)S(1)} copy-done((s32[1,1,1,4,768]{4,3,2,1,0:T(4,128)S(1)}, s32[1,1,1,4,768]{4,3,2,1,0:T(4,128)}, u32[]{:S(2)}) %copy-start.9) | copy-done | bytes 12312
  11.1 0.7 %copy-done.11 = s32[1,1,1,4,32]{4,3,2,1,0:T(4,128)S(1)} copy-done((s32[1,1,1,4,32]{4,3,2,1,0:T(4,128)S(1)}, s32[1,1,1,4,32]{4,3,2,1,0:T(4,128)}, u32[]{:S(2)}) %copy-start.11) | copy-done | bytes 536
  11.8 0.7 %copy-done.13 = s32[1,1,1,4]{3,2,1,0:T(1,128)S(1)} copy-done((s32[1,1,1,4]{3,2,1,0:T(1,128)S(1)}, s32[1,1,1,4]{3,2,1,0:T(1,128)}, u32[]{:S(2)}) %copy-start.13) | copy-done | bytes 40
  12.4 8.9 %forward.1 = f32[96,128]{1,0:T(8,128)S(1)} custom-call(s32[4]{0:T(128)S(1)} %bitcast.57, s32[4,32]{1,0:T(4,128)S(1)} %bitcast.55, s32[4,768]{1,0:T(4,128)S(1)} %bitcast.53, f32[1024,256]{1,0:T(8,128)S(1)} %bitcast.48, bf16[64,128,128]{2,1,0:T(8,128)(2,1)S(1)} %copy-done), custom_call_target="tpu_custom_call" | custom-call | tf_op jit(solution)/shard_map/forward/pallas_call | solution.py:213
  21.4 0.0 collective-permute-done.1
  21.4 0.0 collective-permute-done
  21.5 0.1 collective-permute-start.7
  21.6 0.1 select_subtract_fusion
  21.7 0.6 %collective-permute-start.3 = (f32[96,128]{1,0:T(8,128)S(1)}, f32[96,128]{1,0:T(8,128)S(1)}, u32[]{:S(2)}, u32[]{:S(2)}) collective-permute-start(f32[96,128]{1,0:T(8,128)S(1)} %select_subtract_fusion), channel_id=1, source_target_pairs={{0,1},{1,0},{2,3},{3,2},{4,5},{5,4},{6,7},{7,6},{8,9},{9,8},{10,11... | collective-permute-start | bytes 147464 | tf_op jit(solution)/shard_map/ppermute | solution.py:153
  22.3 0.5 collective-permute-done.7
  22.8 0.9 %collective-permute-start.8 = (f32[2,4,6,128]{3,1,2,0:T(4,128)S(1)}, f32[2,4,6,128]{3,1,2,0:T(4,128)S(1)}, u32[]{:S(2)}, u32[]{:S(2)}) collective-permute-start(f32[2,4,6,128]{3,1,2,0:T(4,128)S(1)} %pad_maximum_fusion.2), channel_id=1, source_target_pairs={{0,2},{2,0},{1,3},{3,1},{4,6},{6,4},{5,7},{7,5},{8,10},{10,8},{9,1... | collective-permute-start | bytes 73736 | tf_op jit(solution)/shard_map/ppermute | solution.py:153
  23.7 1.4 %index.1 = (bf16[4,256,768]{2,1,0:T(8,128)(2,1)S(1)}, bf16[3072,128]{1,0:T(8,128)(2,1)S(1)}) custom-call(s32[4]{0:T(128)S(1)} %bitcast.58, s32[4,768]{1,0:T(4,128)S(1)} %bitcast.54), custom_call_target="tpu_custom_call" | custom-call | tf_op jit(solution)/shard_map/index/pallas_call | solution.py:226
  25.1 1.2 %copy-done.4 = bf16[4,256,768]{2,1,0:T(8,128)(2,1)} copy-done((bf16[4,256,768]{2,1,0:T(8,128)(2,1)}, bf16[4,256,768]{2,1,0:T(8,128)(2,1)S(1)}, u32[]{:S(2)}) %copy-start.4) | copy-done | bytes 1572888
  26.3 0.9 %copy-done.7 = bf16[3072,128]{1,0:T(8,128)(2,1)} copy-done((bf16[3072,128]{1,0:T(8,128)(2,1)}, bf16[3072,128]{1,0:T(8,128)(2,1)S(1)}, u32[]{:S(2)}) %copy-start.7) | copy-done | bytes 786456
  27.2 0.0 collective-permute-done.3
  27.2 1.3 %collective-permute-start.4 = (f32[96,128]{1,0:T(8,128)S(1)}, f32[96,128]{1,0:T(8,128)S(1)}, u32[]{:S(2)}, u32[]{:S(2)}) collective-permute-start(f32[96,128]{1,0:T(8,128)S(1)} %add.41), channel_id=1, source_target_pairs={{0,2},{2,0},{1,3},{3,1},{4,6},{6,4},{5,7},{7,5},{8,10},{10,8},{9,1... | collective-permute-start | bytes 147464 | tf_op jit(solution)/shard_map/ppermute | solution.py:153
  28.5 2.9 %collective-permute-done.4 = f32[96,128]{1,0:T(8,128)S(1)} collective-permute-done((f32[96,128]{1,0:T(8,128)S(1)}, f32[96,128]{1,0:T(8,128)S(1)}, u32[]{:S(2)}, u32[]{:S(2)}) %collective-permute-start.4) | collective-permute-done | bytes 49184 | tf_op jit(solution)/shard_map/ppermute | solution.py:153
  31.4 0.7 %collective-permute-start.6 = (f32[32,128]{1,0:T(8,128)S(1)}, f32[32,128]{1,0:T(8,128)S(1)}, u32[]{:S(2)}, u32[]{:S(2)}) collective-permute-start(f32[32,128]{1,0:T(8,128)S(1)} %get-tuple-element.11), channel_id=1, source_target_pairs={{4,8},{8,4},{5,9},{9,5},{6,10},{10,6},{7,11},{11,7},{20,24},{24,20... | collective-permute-start | bytes 49160 | tf_op jit(solution)/shard_map/ppermute | solution.py:266
  32.0 5.1 %collective-permute-start.5 = (f32[32,128]{1,0:T(8,128)S(1)}, f32[32,128]{1,0:T(8,128)S(1)}, u32[]{:S(2)}, u32[]{:S(2)}) collective-permute-start(f32[32,128]{1,0:T(8,128)S(1)} %get-tuple-element.12), channel_id=1, source_target_pairs={{0,4},{4,0},{8,12},{12,8},{1,5},{5,1},{9,13},{13,9},{2,6},{6,2},{1... | collective-permute-start | bytes 49160 | tf_op jit(solution)/shard_map/ppermute | solution.py:265
  37.2 1.7 %collective-permute-done.5 = f32[32,128]{1,0:T(8,128)S(1)} collective-permute-done((f32[32,128]{1,0:T(8,128)S(1)}, f32[32,128]{1,0:T(8,128)S(1)}, u32[]{:S(2)}, u32[]{:S(2)}) %collective-permute-start.5) | collective-permute-done | bytes 16416 | tf_op jit(solution)/shard_map/ppermute | solution.py:265
  38.9 1.4 %copy-done.5 = bf16[4,256,768]{2,1,0:T(8,128)(2,1)S(1)} copy-done((bf16[4,256,768]{2,1,0:T(8,128)(2,1)S(1)}, bf16[4,256,768]{2,1,0:T(8,128)(2,1)}, u32[]{:S(2)}) %copy-start.5) | copy-done | bytes 1572888
  40.3 1.2 %copy-done.6 = f32[4,256,256]{2,1,0:T(8,128)S(1)} copy-done((f32[4,256,256]{2,1,0:T(8,128)S(1)}, f32[4,256,256]{2,1,0:T(8,128)}, u32[]{:S(2)}) %copy-start.6) | copy-done | bytes 1048600
  41.5 1.1 %copy-done.8 = bf16[3072,128]{1,0:T(8,128)(2,1)S(1)} copy-done((bf16[3072,128]{1,0:T(8,128)(2,1)S(1)}, bf16[3072,128]{1,0:T(8,128)(2,1)}, u32[]{:S(2)}) %copy-start.8) | copy-done | bytes 786456
  42.7 9.0 %backward.1 = f32[1024,256]{1,0:T(8,128)} custom-call(s32[4]{0:T(128)S(1)} %bitcast.59, s32[4,32]{1,0:T(4,128)S(1)} %bitcast.56, f32[96,128]{1,0:T(8,128)S(1)} %add.42.base, f32[32,128]{1,0:T(8,128)S(1)} %get-tuple-element.16.up, f32[32,128]{1,0:T(8,128)S(1)} %get-tuple-element.15.down, f32[96,128]{1,0:T(8,128)S(1)} %bitcast.52, ...), custom_call_target="tpu_custom_call" | custom-call | tf_op jit(solution)/shard_map/backward/pallas_call | solution.py:270
  (48 shorter events, 0.3 us)
Async XLA Ops:
  0.0 23.7 %copy-start.14 = (s32[1,1,1,4]{3,2,1,0:T(1,128)S(1)}, s32[1,1,1,4]{3,2,1,0:T(1,128)}, u32[]{:S(2)}) copy-start(s32[1,1,1,4]{3,2,1,0:T(1,128)} %param.12) | copy-start | bytes 52
  0.0 23.7 %copy-start.10 = (s32[1,1,1,4,768]{4,3,2,1,0:T(4,128)S(1)}, s32[1,1,1,4,768]{4,3,2,1,0:T(4,128)}, u32[]{:S(2)}) copy-start(s32[1,1,1,4,768]{4,3,2,1,0:T(4,128)} %param.11) | copy-start | bytes 36868
  1.7 19.7 %collective-permute-start.2 = (f32[1,12,128]{2,1,0:T(8,128)S(1)}, f32[1,12,128]{2,1,0:T(8,128)S(1)}, u32[]{:S(2)}, u32[]{:S(2)}) collective-permute-start(f32[1,12,128]{2,1,0:T(8,128)S(1)} %get-tuple-element.22), channel_id=1, source_target_pairs={{0,12},{4,8},{8,4},{12,0},{1,13},{5,9},{9,5},{13,1},{2,14},{6,10},... | collective-permute-start | bytes 18440 | tf_op jit(solution)/shard_map/ppermute | solution.py:153
  6.8 14.6 %collective-permute-start.1 = (f32[1,12,128]{2,1,0:T(8,128)S(1)}, f32[1,12,128]{2,1,0:T(8,128)S(1)}, u32[]{:S(2)}, u32[]{:S(2)}) collective-permute-start(f32[1,12,128]{2,1,0:T(8,128)S(1)} %get-tuple-element.23), channel_id=1, source_target_pairs={{0,8},{4,12},{8,0},{12,4},{1,9},{5,13},{9,1},{13,5},{2,10},{6,14},... | collective-permute-start | bytes 18440 | tf_op jit(solution)/shard_map/ppermute | solution.py:153
  6.8 14.6 %collective-permute-start = (f32[1,12,128]{2,1,0:T(8,128)S(1)}, f32[1,12,128]{2,1,0:T(8,128)S(1)}, u32[]{:S(2)}, u32[]{:S(2)}) collective-permute-start(f32[1,12,128]{2,1,0:T(8,128)S(1)} %get-tuple-element.24), channel_id=1, source_target_pairs={{0,4},{4,0},{8,12},{12,8},{1,5},{5,1},{9,13},{13,9},{2,6},{6,2},{1... | collective-permute-start | bytes 18440 | tf_op jit(solution)/shard_map/ppermute | solution.py:153
  7.6 1.6 %copy-start = (bf16[64,128,128]{2,1,0:T(8,128)(2,1)S(1)}, bf16[64,128,128]{2,1,0:T(8,128)(2,1)}, u32[]{:S(2)}) copy-start(bf16[64,128,128]{2,1,0:T(8,128)(2,1)} %tiles.3) | copy-start | bytes 6291460
  9.2 1.2 %copy-start.2 = (f32[4,256,256]{2,1,0:T(8,128)S(1)}, f32[4,256,256]{2,1,0:T(8,128)}, u32[]{:S(2)}) copy-start(f32[4,256,256]{2,1,0:T(8,128)} %param.8) | copy-start | bytes 3145732
  10.4 0.7 %copy-start.9 = (s32[1,1,1,4,768]{4,3,2,1,0:T(4,128)S(1)}, s32[1,1,1,4,768]{4,3,2,1,0:T(4,128)}, u32[]{:S(2)}) copy-start(s32[1,1,1,4,768]{4,3,2,1,0:T(4,128)} %param.11) | copy-start | bytes 36868
  11.1 0.7 %copy-start.11 = (s32[1,1,1,4,32]{4,3,2,1,0:T(4,128)S(1)}, s32[1,1,1,4,32]{4,3,2,1,0:T(4,128)}, u32[]{:S(2)}) copy-start(s32[1,1,1,4,32]{4,3,2,1,0:T(4,128)} %param.10) | copy-start | bytes 1540
  11.8 0.7 %copy-start.13 = (s32[1,1,1,4]{3,2,1,0:T(1,128)S(1)}, s32[1,1,1,4]{3,2,1,0:T(1,128)}, u32[]{:S(2)}) copy-start(s32[1,1,1,4]{3,2,1,0:T(1,128)} %param.12) | copy-start | bytes 52
  12.4 26.4 %copy-start.1 = (bf16[64,128,128]{2,1,0:T(8,128)(2,1)S(1)}, bf16[64,128,128]{2,1,0:T(8,128)(2,1)}, u32[]{:S(2)}) copy-start(bf16[64,128,128]{2,1,0:T(8,128)(2,1)} %tiles.3) | copy-start | bytes 6291460
  12.4 26.4 %copy-start.3 = (f32[4,256,256]{2,1,0:T(8,128)S(1)}, f32[4,256,256]{2,1,0:T(8,128)}, u32[]{:S(2)}) copy-start(f32[4,256,256]{2,1,0:T(8,128)} %param.8) | copy-start | bytes 3145732
  12.4 26.4 %copy-start.12 = (s32[1,1,1,4,32]{4,3,2,1,0:T(4,128)S(1)}, s32[1,1,1,4,32]{4,3,2,1,0:T(4,128)}, u32[]{:S(2)}) copy-start(s32[1,1,1,4,32]{4,3,2,1,0:T(4,128)} %param.10) | copy-start | bytes 1540
  21.5 1.2 %collective-permute-start.7 = (f32[1,4,6,128]{3,1,2,0:T(4,128)S(1)}, f32[1,4,6,128]{3,1,2,0:T(4,128)S(1)}, u32[]{:S(2)}, u32[]{:S(2)}) collective-permute-start(f32[1,4,6,128]{3,1,2,0:T(4,128)S(1)} %get-tuple-element.25), channel_id=1, source_target_pairs={{0,1},{1,0},{2,3},{3,2},{4,5},{5,4},{6,7},{7,6},{8,9},{9,8},{10,11... | collective-permute-start | bytes 36872 | tf_op jit(solution)/shard_map/ppermute | solution.py:153
  21.7 5.5 %collective-permute-start.3 = (f32[96,128]{1,0:T(8,128)S(1)}, f32[96,128]{1,0:T(8,128)S(1)}, u32[]{:S(2)}, u32[]{:S(2)}) collective-permute-start(f32[96,128]{1,0:T(8,128)S(1)} %select_subtract_fusion), channel_id=1, source_target_pairs={{0,1},{1,0},{2,3},{3,2},{4,5},{5,4},{6,7},{7,6},{8,9},{9,8},{10,11... | collective-permute-start | bytes 147464 | tf_op jit(solution)/shard_map/ppermute | solution.py:153
  22.8 5.7 %collective-permute-start.8 = (f32[2,4,6,128]{3,1,2,0:T(4,128)S(1)}, f32[2,4,6,128]{3,1,2,0:T(4,128)S(1)}, u32[]{:S(2)}, u32[]{:S(2)}) collective-permute-start(f32[2,4,6,128]{3,1,2,0:T(4,128)S(1)} %pad_maximum_fusion.2), channel_id=1, source_target_pairs={{0,2},{2,0},{1,3},{3,1},{4,6},{6,4},{5,7},{7,5},{8,10},{10,8},{9,1... | collective-permute-start | bytes 73736 | tf_op jit(solution)/shard_map/ppermute | solution.py:153
  25.1 1.2 %copy-start.4 = (bf16[4,256,768]{2,1,0:T(8,128)(2,1)}, bf16[4,256,768]{2,1,0:T(8,128)(2,1)S(1)}, u32[]{:S(2)}) copy-start(bf16[4,256,768]{2,1,0:T(8,128)(2,1)S(1)} %get-tuple-element.7.hot) | copy-start | bytes 4718596
  26.3 0.9 %copy-start.7 = (bf16[3072,128]{1,0:T(8,128)(2,1)}, bf16[3072,128]{1,0:T(8,128)(2,1)S(1)}, u32[]{:S(2)}) copy-start(bf16[3072,128]{1,0:T(8,128)(2,1)S(1)} %get-tuple-element.8.code) | copy-start | bytes 2359300
  27.2 4.2 %collective-permute-start.4 = (f32[96,128]{1,0:T(8,128)S(1)}, f32[96,128]{1,0:T(8,128)S(1)}, u32[]{:S(2)}, u32[]{:S(2)}) collective-permute-start(f32[96,128]{1,0:T(8,128)S(1)} %add.41), channel_id=1, source_target_pairs={{0,2},{2,0},{1,3},{3,1},{4,6},{6,4},{5,7},{7,5},{8,10},{10,8},{9,1... | collective-permute-start | bytes 147464 | tf_op jit(solution)/shard_map/ppermute | solution.py:153
  31.4 5.8 %collective-permute-start.6 = (f32[32,128]{1,0:T(8,128)S(1)}, f32[32,128]{1,0:T(8,128)S(1)}, u32[]{:S(2)}, u32[]{:S(2)}) collective-permute-start(f32[32,128]{1,0:T(8,128)S(1)} %get-tuple-element.11), channel_id=1, source_target_pairs={{4,8},{8,4},{5,9},{9,5},{6,10},{10,6},{7,11},{11,7},{20,24},{24,20... | collective-permute-start | bytes 49160 | tf_op jit(solution)/shard_map/ppermute | solution.py:266
  32.0 6.8 %collective-permute-start.5 = (f32[32,128]{1,0:T(8,128)S(1)}, f32[32,128]{1,0:T(8,128)S(1)}, u32[]{:S(2)}, u32[]{:S(2)}) collective-permute-start(f32[32,128]{1,0:T(8,128)S(1)} %get-tuple-element.12), channel_id=1, source_target_pairs={{0,4},{4,0},{8,12},{12,8},{1,5},{5,1},{9,13},{13,9},{2,6},{6,2},{1... | collective-permute-start | bytes 49160 | tf_op jit(solution)/shard_map/ppermute | solution.py:265
  38.9 1.4 %copy-start.5 = (bf16[4,256,768]{2,1,0:T(8,128)(2,1)S(1)}, bf16[4,256,768]{2,1,0:T(8,128)(2,1)}, u32[]{:S(2)}) copy-start(bf16[4,256,768]{2,1,0:T(8,128)(2,1)} %copy-done.4) | copy-start | bytes 4718596
  40.3 1.2 %copy-start.6 = (f32[4,256,256]{2,1,0:T(8,128)S(1)}, f32[4,256,256]{2,1,0:T(8,128)}, u32[]{:S(2)}) copy-start(f32[4,256,256]{2,1,0:T(8,128)} %param.15) | copy-start | bytes 3145732
  41.5 1.1 %copy-start.8 = (bf16[3072,128]{1,0:T(8,128)(2,1)S(1)}, bf16[3072,128]{1,0:T(8,128)(2,1)}, u32[]{:S(2)}) copy-start(bf16[3072,128]{1,0:T(8,128)(2,1)} %copy-done.7) | copy-start | bytes 2359300

commit v2 on v1

v2 whole, which is shorter than its diff:
```python
import functools
import math

import jax
import jax.numpy as jnp
from jax import lax
from jax.experimental import pallas as pl
from jax.experimental.pallas import tpu as pltpu
from jax.sharding import PartitionSpec as P

ONE_HOT = 512
GROUP = 8
VMEM_LIMIT = 16 * 1024 * 1024


def forward_kernel(
    rows, live_in, tid_in, bid_in, vol_in, tiles_in, out,
    live, tid, bid, vol, tiles, vox, picked, sems,
):
    angles, slots = tid.shape
    tile = tiles.shape[1]
    lines, width = vol.shape
    runs = width // tile
    pairs = ((bid_in, bid), (tid_in, tid), (live_in, live), (vol_in, vol), (tiles_in, tiles))
    copies = [pltpu.make_async_copy(a, b, sems.at[i]) for i, (a, b) in enumerate(pairs)]
    for copy in copies:
        copy.start()
    copies[3].wait()
    step = 8
    for run in range(runs):
        for line in range(0, lines, step):
            vox[pl.ds(line * runs + run, step, stride=runs), :] = vol[
                line : line + step, run * tile : (run + 1) * tile
            ]
    for copy in copies[:3] + copies[4:]:
        copy.wait()

    def project_angle(a, carry):
        count = live[a]
        total = jnp.zeros((rows, tile), jnp.float32)
        for g in range(0, slots, GROUP):
            left, right = [], []
            for k in range(g, g + GROUP):
                for r in range(rows):
                    j = k * rows + r
                    picked[j : j + 1, :] = vox[pl.ds(bid[a, j], 1), :]
            for k in range(g, g + GROUP):
                part = picked[k * rows : (k + 1) * rows, :]
                left.append(jnp.where(k < count, part, 0.0).astype(jnp.bfloat16))
                right.append(tiles[tid[a, k]])
            total += lax.dot_general(
                jnp.concatenate(left, axis=1),
                jnp.concatenate(right, axis=1),
                (((1,), (1,)), ((), ())),
                preferred_element_type=jnp.float32,
            )
        out[pl.ds(pl.multiple_of(a * rows, 8), rows), :] = total
        return carry

    lax.fori_loop(0, angles, project_angle, 0)


def index_kernel(rows, runs, live, bid, hot, code):
    angles, length = bid.shape
    tile = code.shape[1]
    high = hot.shape[0]
    place = lax.broadcasted_iota(jnp.int32, (high, length), 0)
    position = lax.broadcasted_iota(jnp.int32, (1, length), 1)
    for a in range(angles):
        block = bid[a : a + 1, :]
        line = block // runs
        hot[:, a * length : (a + 1) * length] = jnp.where(
            place == line % high, 1.0, 0.0
        ).astype(jnp.bfloat16)
        group = (line // high) * runs + block % runs
        group = jnp.where(position < live[a] * rows, group, -1).astype(jnp.float32)
        for c in range(length // tile):
            wide = jnp.broadcast_to(group[:, c * tile : (c + 1) * tile], (tile, tile))
            code[a * length + c * tile : a * length + (c + 1) * tile, :] = wide.T.astype(
                jnp.bfloat16
            )


def backward_kernel(
    rows, live, tid, base, up, down, weight, tiles, hot, code, vol_in, col_in, out_in,
    res, spread, vol, col, out, sems,
):
    angles, slots = tid.shape
    tile = tiles.shape[1]
    lines, width = vol.shape
    runs = width // tile
    rim = up.shape[0] // angles
    high = hot.shape[0]
    reads = [
        pltpu.make_async_copy(vol_in, vol, sems.at[0]),
        pltpu.make_async_copy(col_in, col, sems.at[1]),
    ]
    for copy in reads:
        copy.start()
    for a in range(angles):
        own = base[a * rows : (a + 1) * rows, :]
        whole = jnp.concatenate(
            [
                own[:rim] + up[a * rim : (a + 1) * rim, :],
                own[rim : rows - rim],
                own[rows - rim :] + down[a * rim : (a + 1) * rim, :],
            ],
            axis=0,
        )
        res[a] = (weight[a * rows : (a + 1) * rows, :] * whole).astype(jnp.bfloat16)

    def spread_angle(a, carry):
        values = res[a]

        def group(g, inner):
            for u in range(0, GROUP, 2):
                k = g * GROUP + u
                pair = jnp.concatenate([tiles[tid[a, k]], tiles[tid[a, k + 1]]], axis=1)
                made = jnp.dot(values, pair, preferred_element_type=jnp.float32)
                both = jnp.concatenate([made[:, :tile], made[:, tile:]], axis=0)
                at = pl.multiple_of((a * slots + k) * rows, 16)
                spread[pl.ds(at, 2 * rows), :] = both.astype(jnp.bfloat16)
            return inner

        return lax.fori_loop(0, (live[a] + GROUP - 1) // GROUP, group, carry)

    lax.fori_loop(0, angles, spread_angle, 0)
    for copy in reads:
        copy.wait()

    writes = []
    for chunk in range(lines // high):
        values = spread[...]
        groups = code[...]
        right = jnp.concatenate(
            [
                jnp.where(groups == jnp.bfloat16(chunk * runs + run), values, jnp.bfloat16(0))
                for run in range(runs)
            ],
            axis=1,
        )
        made = jnp.dot(hot[...], right, preferred_element_type=jnp.float32)
        here = pl.ds(chunk * high, high)
        out[here, :] = vol[here, :] + col[here, :] * made
        copy = pltpu.make_async_copy(out.at[here, :], out_in.at[here, :], sems.at[2 + chunk])
        copy.start()
        writes.append(copy)
    for copy in writes:
        copy.wait()


def swap(values, axis, bit):
    return lax.ppermute(values, axis, [(i, i ^ bit) for i in range(lax.axis_size(axis))])


def bits(axis):
    return [1 << i for i in range((lax.axis_size(axis) - 1).bit_length())]


def windows(data, slab_count, slab_depth, edge):
    padded = jnp.pad(data, ((0, 0), (1, 1), (0, 0)))
    parts = []
    for s in range(slab_count):
        part = padded[:, s * slab_depth : s * slab_depth + slab_depth + 2]
        if not edge:
            part = jnp.pad(part[:, 1:-1], ((0, 0), (1, 1), (0, 0)))
        parts.append(part)
    return jnp.stack(parts)


def ordered(mine_high, own, other, axis):
    return jnp.concatenate(
        [jnp.where(mine_high, other, own), jnp.where(mine_high, own, other)], axis=axis
    )


def to_slabs(sends):
    here = lax.axis_index("gz")
    for bit in bits("gz"):
        high = (here & bit) != 0
        halves = sends.reshape((sends.shape[0] // 2, 2) + sends.shape[1:])
        keep = jnp.where(high, halves[:, 1], halves[:, 0])
        give = jnp.where(high, halves[:, 0], halves[:, 1])
        sends = ordered(high, keep, swap(give, "gz", bit), 1)
    return sends[0]


def on_device(volume, tile_table, tile_ids, block_ids, live_slots, measured, row_norm, col_norm):
    slab_depth, column_width, half_width = volume.shape
    tile_size = tile_table.shape[1]
    angle_count, slot_count = tile_ids.shape[3:]
    window = slab_depth + 2
    block_cols = block_ids.shape[4] // (slot_count * window)
    rows = window * block_cols
    rim = 2 * block_cols
    length = slot_count * rows
    lines = slab_depth * column_width
    runs = half_width // tile_size
    high = math.gcd(lines, ONE_HOT)
    slab_count = lax.axis_size("gz")
    local_cols = measured.shape[1]

    tid = tile_ids.reshape(angle_count, slot_count)
    bid = block_ids.reshape(angle_count, length)
    live = live_slots.reshape(angle_count)
    vol = volume.reshape(lines, half_width)
    col = col_norm.reshape(lines, half_width)

    smem = pl.BlockSpec(memory_space=pltpu.SMEM)
    vmem = pl.BlockSpec(memory_space=pltpu.VMEM)
    hbm = pl.BlockSpec(memory_space=pltpu.HBM)
    params = pltpu.CompilerParams(vmem_limit_bytes=VMEM_LIMIT)

    arrived = to_slabs(
        jnp.concatenate(
            [
                windows(measured.transpose(0, 2, 1), slab_count, slab_depth, False),
                windows(row_norm.transpose(0, 2, 1), slab_count, slab_depth, True),
            ],
            axis=2,
        )
    )
    target = arrived[:, :window]
    weight = arrived[:, window:].reshape(angle_count * window, local_cols)[None]

    partial = pl.pallas_call(
        functools.partial(forward_kernel, rows),
        out_shape=jax.ShapeDtypeStruct((angle_count * rows, tile_size), jnp.float32),
        in_specs=[hbm] * 5,
        out_specs=vmem,
        scratch_shapes=[
            pltpu.SMEM((angle_count,), jnp.int32),
            pltpu.SMEM((angle_count, slot_count), jnp.int32),
            pltpu.SMEM((angle_count, length), jnp.int32),
            pltpu.VMEM((lines, half_width), jnp.float32),
            pltpu.VMEM(tile_table.shape, jnp.bfloat16),
            pltpu.VMEM((lines * runs, tile_size), jnp.float32),
            pltpu.VMEM((length, tile_size), jnp.float32),
            pltpu.SemaphoreType.DMA((5,)),
        ],
        compiler_params=params,
        name="forward",
    )(live, tid, bid, vol, tile_table)

    hot, code = pl.pallas_call(
        functools.partial(index_kernel, rows, runs),
        out_shape=(
            jax.ShapeDtypeStruct((high, angle_count * length), jnp.bfloat16),
            jax.ShapeDtypeStruct((angle_count * length, tile_size), jnp.bfloat16),
        ),
        in_specs=[smem, vmem],
        out_specs=(vmem, vmem),
        compiler_params=params,
        name="index",
    )(live, bid)

    row_count = lax.axis_size("row")
    at_row = lax.axis_index("row")
    place = lax.axis_index("gx") * row_count + at_row
    if local_cols == tile_size:
        mine = lax.broadcasted_iota(jnp.int32, (1, 1, block_cols, 1), 2) == place
        spot = jnp.where(mine, target[:, :, None, :], 0.0)
    else:
        spot = jnp.zeros((angle_count, window, block_cols * tile_size), jnp.float32)
        spot = lax.dynamic_update_slice_in_dim(spot, target, place * local_cols, 2)
        spot = spot.reshape(angle_count, window, block_cols, tile_size)
    total = spot.reshape(angle_count * rows, tile_size) - partial
    for bit in bits("row"):
        total = total + swap(total, "row", bit)
    for bit in bits("gx"):
        is_high = (lax.axis_index("gx") & bit) != 0
        if local_cols == tile_size:
            both = jnp.concatenate([total, weight.reshape(-1, tile_size)], axis=0)
            came = swap(both, "gx", bit)
            other_weight = came[total.shape[0] :].reshape(weight.shape)
            came = came[: total.shape[0]]
        else:
            came = swap(total, "gx", bit)
            other_weight = swap(weight, "gx", bit)
        total = total + came
        weight = ordered(is_high, weight, other_weight, 0)

    blocks = total.reshape(angle_count, rows, tile_size)
    head = blocks[:, :rim].reshape(angle_count * rim, tile_size)
    tail = blocks[:, rows - rim :].reshape(angle_count * rim, tile_size)
    last = slab_count - 1
    assert row_count == 2
    upper = at_row == 1
    hops = [((z + 1) * 2, z * 2) for z in range(last)]
    hops += [(z * 2 + 1, z * 2 + 3) for z in range(last)]
    came = lax.ppermute(jnp.where(upper, tail, head), ("gz", "row"), hops)
    if local_cols == tile_size:
        both = jnp.concatenate([came, weight.reshape(-1, tile_size)], axis=0)
        swapped = swap(both, "row", 1)
        other_came = swapped[: came.shape[0]]
        other_weight = swapped[came.shape[0] :].reshape(weight.shape)
    else:
        other_came = swap(came, "row", 1)
        other_weight = swap(weight, "row", 1)
    up = jnp.where(upper, came, other_came)
    down = jnp.where(upper, other_came, came)
    weight = ordered(upper, weight[:, None], other_weight[:, None], 1)
    weight = weight.reshape(-1, angle_count, window, local_cols)
    weight = weight.transpose(1, 2, 0, 3).reshape(angle_count * rows, tile_size)

    made = pl.pallas_call(
        functools.partial(backward_kernel, rows),
        out_shape=jax.ShapeDtypeStruct((lines, half_width), jnp.float32),
        in_specs=[smem, smem] + [vmem] * 7 + [hbm] * 2,
        out_specs=hbm,
        scratch_shapes=[
            pltpu.VMEM((angle_count, rows, tile_size), jnp.bfloat16),
            pltpu.VMEM((angle_count * length, tile_size), jnp.bfloat16),
            pltpu.VMEM((lines, half_width), jnp.float32),
            pltpu.VMEM((lines, half_width), jnp.float32),
            pltpu.VMEM((lines, half_width), jnp.float32),
            pltpu.SemaphoreType.DMA((2 + lines // high,)),
        ],
        compiler_params=params,
        name="backward",
    )(live, tid, total, up, down, weight, tile_table, hot, code, vol, col)
    return made.reshape(slab_depth, column_width, half_width)


def solution(mesh):
    placed = (
        P(("grp", "gz"), "gx", "row"),
        P(),
        P("gz", "gx", "row", None, None),
        P("gz", "gx", "row", None, None),
        P("gz", "gx", "row", None),
        P(("grp", "gz"), ("gx", "row"), None),
        P("gz", ("gx", "row"), None),
        P("gz", "gx", "row"),
    )
    return jax.shard_map(
        on_device,
        mesh=mesh,
        in_specs=placed,
        out_specs=P(("grp", "gz"), "gx", "row"),
        check_vma=False,
    )
```

time: 51.7 us -> 40.9 us (0.79)
  the two profiles are of different devices: /device:TPU:0 before, /device:TPU:1 now
where the time goes in v2:
time: 40.9 us; the launch traced here: 40.1 us
  starting transfers between devices  14.4 us (35%)
  Pallas kernels  12.7 us (31%)
  local copies, waits for them, and re-layouts  7.85 us (19%)
  waiting for transfers between devices  4.7 us (11%)
    ppermute x5, starting transfers between devices, swap(): lax.ppermute(values, axis, [(i, i ^ bit) for i in range(lax.axis_size(axi...  11.2 us
    unnamed x22, local copies, waits for them, and re-layouts  6.09 us
    pallas_call x1, Pallas kernels, on_device(): pl.pallas_call(functools.partial(forward_kernel, rows), out_shape=jax.Sha...  5.32 us
    pallas_call x1, Pallas kernels, on_device(): pl.pallas_call(functools.partial(backward_kernel, rows), out_shape=jax.Sh...  5.27 us
    ppermute x5, waiting for transfers between devices, swap(): lax.ppermute(values, axis, [(i, i ^ bit) for i in range(lax.axis_size(axi...  3.88 us
    ppermute x1, starting transfers between devices, on_device(): came = lax.ppermute(jnp.where(upper, tail, head), ('gz', 'row'), hops)  3.2 us
    pallas_call x1, Pallas kernels, on_device(): pl.pallas_call(functools.partial(index_kernel, rows, runs), out_shape=(ja...  2.13 us
    another operation x3, local copies, waits for them, and re-layouts, windows(): return jnp.stack(parts)  0.83 us
  transfers between devices with their start and end apart: 6, of which 4 were waited for; matrix products, arithmetic and copies ran while one was open for 0% of the time, Pallas kernels for 19%

profile of v2, /device:TPU:1, one launch (start us, length us, event | category | flops | bytes accessed | tf_op | source)
XLA Modules:
  0.0 40.1 jit_solution(4097771384341212848)
XLA Ops:
  0.0 0.8 %fusion.11 = (f32[1,4,128]{2,1,0:T(4,128)S(1)}, f32[1,4,128]{2,1,0:T(4,128)S(1)}, f32[1,4,128]{2,1,0:T(4,128)S(1)}, f32[1,4,128]{2,1,0:T(4,128)S(1)}) fusion(f32[1,16,128]{2,1,0:T(8,128)} %bitcast.100), kind=kLoop, calls=%fused_computation.44 | loop fusion | bytes 16384 | tf_op jit(solution)/shard_map/slice | solution.py:166
  0.8 0.8 %fusion.8 = (f32[1,1,6,128]{3,2,1,0:T(8,128)S(1)}, f32[1,1,6,128]{3,2,1,0:T(8,128)S(1)}, f32[1,1,6,128]{3,2,1,0:T(8,128)S(1)}, f32[1,1,6,128]{3,2,1,0:T(8,128)S(1)}) fusion(f32[1,16,128]{2,1,0:T(8,128)} %bitcast.99), kind=kLoop, calls=%fused_computation.34 | loop fusion | bytes 28672 | tf_op jit(solution)/shard_map/stack | solution.py:168
  1.7 2.2 %collective-permute-start = (f32[2,1,12,128]{3,2,1,0:T(8,128)S(1)}, f32[2,1,12,128]{3,2,1,0:T(8,128)S(1)}, u32[]{:S(2)}, u32[]{:S(2)}) collective-permute-start(f32[2,1,12,128]{3,2,1,0:T(8,128)S(1)} %select_bitcast_fusion.1), channel_id=1, source_target_pairs={{0,4},{4,0},{8,12},{12,8},{1,5},{5,1},{9,13},{13,9},{2,6},{6,2},{1... | collective-permute-start | bytes 36872 | tf_op jit(solution)/shard_map/ppermute | solution.py:153
  3.8 1.1 %collective-permute-done = f32[2,1,12,128]{3,2,1,0:T(8,128)S(1)} collective-permute-done((f32[2,1,12,128]{3,2,1,0:T(8,128)S(1)}, f32[2,1,12,128]{3,2,1,0:T(8,128)S(1)}, u32[]{:S(2)}, u32[]{:S(2)}) %collective-permute-start) | collective-permute-done | bytes 12320 | tf_op jit(solution)/shard_map/ppermute | solution.py:153
  5.0 2.5 %collective-permute-start.1 = (f32[1,2,12,128]{3,2,1,0:T(8,128)S(1)}, f32[1,2,12,128]{3,2,1,0:T(8,128)S(1)}, u32[]{:S(2)}, u32[]{:S(2)}) collective-permute-start(f32[1,2,12,128]{3,2,1,0:T(8,128)S(1)} %select_bitcast_fusion), channel_id=1, source_target_pairs={{0,8},{4,12},{8,0},{12,4},{1,9},{5,13},{9,1},{13,5},{2,10},{6,14},... | collective-permute-start | bytes 36872 | tf_op jit(solution)/shard_map/ppermute | solution.py:153
  7.6 0.1 broadcast_in_dim.29
  7.7 0.0 copy-start
  7.7 1.6 %copy-done = bf16[64,128,128]{2,1,0:T(8,128)(2,1)S(1)} copy-done((bf16[64,128,128]{2,1,0:T(8,128)(2,1)S(1)}, bf16[64,128,128]{2,1,0:T(8,128)(2,1)}, u32[]{:S(2)}) %copy-start) | copy-done | bytes 2097176
  9.3 1.2 %copy-done.2 = f32[4,256,256]{2,1,0:T(8,128)S(1)} copy-done((f32[4,256,256]{2,1,0:T(8,128)S(1)}, f32[4,256,256]{2,1,0:T(8,128)}, u32[]{:S(2)}) %copy-start.2) | copy-done | bytes 1048600
  10.5 0.7 %copy-done.5 = s32[1,1,1,4,768]{4,3,2,1,0:T(4,128)S(1)} copy-done((s32[1,1,1,4,768]{4,3,2,1,0:T(4,128)S(1)}, s32[1,1,1,4,768]{4,3,2,1,0:T(4,128)}, u32[]{:S(2)}) %copy-start.5) | copy-done | bytes 12312
  11.2 0.7 %copy-done.7 = s32[1,1,1,4,32]{4,3,2,1,0:T(4,128)S(1)} copy-done((s32[1,1,1,4,32]{4,3,2,1,0:T(4,128)S(1)}, s32[1,1,1,4,32]{4,3,2,1,0:T(4,128)}, u32[]{:S(2)}) %copy-start.7) | copy-done | bytes 536
  11.9 0.7 %copy-done.9 = s32[1,1,1,4]{3,2,1,0:T(1,128)S(1)} copy-done((s32[1,1,1,4]{3,2,1,0:T(1,128)S(1)}, s32[1,1,1,4]{3,2,1,0:T(1,128)}, u32[]{:S(2)}) %copy-start.9) | copy-done | bytes 40
  12.5 5.3 %forward.1 = f32[96,128]{1,0:T(8,128)S(1)} custom-call(s32[4]{0:T(128)S(1)} %bitcast.91, s32[4,32]{1,0:T(4,128)S(1)} %bitcast.89, s32[4,768]{1,0:T(4,128)S(1)} %bitcast.87, f32[1024,256]{1,0:T(8,128)S(1)} %bitcast.82, bf16[64,128,128]{2,1,0:T(8,128)(2,1)S(1)} %copy-done), custom_call_target="tpu_custom_call" | custom-call | tf_op jit(solution)/shard_map/forward/pallas_call | solution.py:226
  17.9 0.0 collective-permute-done.1
  17.9 0.1 select_subtract_fusion
  18.0 2.2 %collective-permute-start.2 = (f32[96,128]{1,0:T(8,128)S(1)}, f32[96,128]{1,0:T(8,128)S(1)}, u32[]{:S(2)}, u32[]{:S(2)}) collective-permute-start(f32[96,128]{1,0:T(8,128)S(1)} %select_subtract_fusion), channel_id=1, source_target_pairs={{0,1},{1,0},{2,3},{3,2},{4,5},{5,4},{6,7},{7,6},{8,9},{9,8},{10,11... | collective-permute-start | bytes 147464 | tf_op jit(solution)/shard_map/ppermute | solution.py:153
  20.2 0.9 %collective-permute-done.2 = f32[96,128]{1,0:T(8,128)S(1)} collective-permute-done((f32[96,128]{1,0:T(8,128)S(1)}, f32[96,128]{1,0:T(8,128)S(1)}, u32[]{:S(2)}, u32[]{:S(2)}) %collective-permute-start.2) | collective-permute-done | bytes 49184 | tf_op jit(solution)/shard_map/ppermute | solution.py:153
  21.1 1.3 %collective-permute-start.3 = (f32[120,128]{1,0:T(8,128)S(1)}, f32[120,128]{1,0:T(8,128)S(1)}, u32[]{:S(2)}, u32[]{:S(2)}) collective-permute-start(f32[120,128]{1,0:T(8,128)S(1)} %pad_maximum_fusion), channel_id=1, source_target_pairs={{0,2},{2,0},{1,3},{3,1},{4,6},{6,4},{5,7},{7,5},{8,10},{10,8},{9,1... | collective-permute-start | bytes 184328 | tf_op jit(solution)/shard_map/ppermute | solution.py:153
  22.3 1.9 %collective-permute-done.3 = f32[120,128]{1,0:T(8,128)S(1)} collective-permute-done((f32[120,128]{1,0:T(8,128)S(1)}, f32[120,128]{1,0:T(8,128)S(1)}, u32[]{:S(2)}, u32[]{:S(2)}) %collective-permute-start.3) | collective-permute-done | bytes 61472 | tf_op jit(solution)/shard_map/ppermute | solution.py:153
  24.2 3.2 %collective-permute-start.4 = (f32[32,128]{1,0:T(8,128)S(1)}, f32[32,128]{1,0:T(8,128)S(1)}, u32[]{:S(2)}, u32[]{:S(2)}) collective-permute-start(f32[32,128]{1,0:T(8,128)S(1)} %fusion.2), channel_id=1, source_target_pairs={{4,0},{8,4},{12,8},{1,5},{5,9},{9,13},{6,2},{10,6},{14,10},{3,7},{... | collective-permute-start | bytes 49160 | tf_op jit(solution)/shard_map/ppermute | solution.py:291
  27.5 0.8 %collective-permute-done.4 = f32[32,128]{1,0:T(8,128)S(1)} collective-permute-done((f32[32,128]{1,0:T(8,128)S(1)}, f32[32,128]{1,0:T(8,128)S(1)}, u32[]{:S(2)}, u32[]{:S(2)}) %collective-permute-start.4) | collective-permute-done | bytes 16416 | tf_op jit(solution)/shard_map/ppermute | solution.py:291
  28.3 3.1 %collective-permute-start.5 = (f32[80,128]{1,0:T(8,128)S(1)}, f32[80,128]{1,0:T(8,128)S(1)}, u32[]{:S(2)}, u32[]{:S(2)}) collective-permute-start(f32[80,128]{1,0:T(8,128)S(1)} %pad_maximum_fusion.2), channel_id=1, source_target_pairs={{0,1},{1,0},{2,3},{3,2},{4,5},{5,4},{6,7},{7,6},{8,9},{9,8},{10,11... | collective-permute-start | bytes 122888 | tf_op jit(solution)/shard_map/ppermute | solution.py:153
  31.4 0.0 copy-done.10
  31.4 0.0 copy-done.6
  31.4 2.1 %index.1 = (bf16[512,3072]{1,0:T(8,128)(2,1)S(1)}, bf16[3072,128]{1,0:T(8,128)(2,1)S(1)}) custom-call(s32[4]{0:T(128)S(1)} %bitcast.92, s32[4,768]{1,0:T(4,128)S(1)} %bitcast.88), custom_call_target="tpu_custom_call" | custom-call | tf_op jit(solution)/shard_map/index/pallas_call | solution.py:245
  33.5 0.0 collective-permute-done.5
  33.6 0.0 copy-done.8
  33.6 0.0 copy-done.1
  33.6 0.0 copy-done.3
  33.6 0.0 copy-start.4
  33.7 1.2 %copy-done.4 = f32[4,256,256]{2,1,0:T(8,128)S(1)} copy-done((f32[4,256,256]{2,1,0:T(8,128)S(1)}, f32[4,256,256]{2,1,0:T(8,128)}, u32[]{:S(2)}) %copy-start.4) | copy-done | bytes 1048600
  34.9 5.3 %backward.1 = f32[1024,256]{1,0:T(8,128)} custom-call(s32[4]{0:T(128)S(1)} %bitcast.93, s32[4,32]{1,0:T(4,128)S(1)} %bitcast.90, f32[96,128]{1,0:T(8,128)S(1)} %slice_add_fusion.base, f32[32,128]{1,0:T(8,128)S(1)} %get-tuple-element.14.up, f32[32,128]{1,0:T(8,128)S(1)} %get-tuple-element.13.down, f32[96,128]{1,0:T(8,128)S(1)} %bitcast.86, ...), custom_call_target="tpu_custom_call" | custom-call | tf_op jit(solution)/shard_map/backward/pallas_call | solution.py:306
  (35 shorter events, 0.2 us)
Async XLA Ops:
  0.0 31.4 %copy-start.10 = (s32[1,1,1,4]{3,2,1,0:T(1,128)S(1)}, s32[1,1,1,4]{3,2,1,0:T(1,128)}, u32[]{:S(2)}) copy-start(s32[1,1,1,4]{3,2,1,0:T(1,128)} %param.12) | copy-start | bytes 52
  0.0 31.4 %copy-start.6 = (s32[1,1,1,4,768]{4,3,2,1,0:T(4,128)S(1)}, s32[1,1,1,4,768]{4,3,2,1,0:T(4,128)}, u32[]{:S(2)}) copy-start(s32[1,1,1,4,768]{4,3,2,1,0:T(4,128)} %param.11) | copy-start | bytes 36868
  0.0 33.6 %copy-start.8 = (s32[1,1,1,4,32]{4,3,2,1,0:T(4,128)S(1)}, s32[1,1,1,4,32]{4,3,2,1,0:T(4,128)}, u32[]{:S(2)}) copy-start(s32[1,1,1,4,32]{4,3,2,1,0:T(4,128)} %param.10) | copy-start | bytes 1540
  1.7 3.3 %collective-permute-start = (f32[2,1,12,128]{3,2,1,0:T(8,128)S(1)}, f32[2,1,12,128]{3,2,1,0:T(8,128)S(1)}, u32[]{:S(2)}, u32[]{:S(2)}) collective-permute-start(f32[2,1,12,128]{3,2,1,0:T(8,128)S(1)} %select_bitcast_fusion.1), channel_id=1, source_target_pairs={{0,4},{4,0},{8,12},{12,8},{1,5},{5,1},{9,13},{13,9},{2,6},{6,2},{1... | collective-permute-start | bytes 36872 | tf_op jit(solution)/shard_map/ppermute | solution.py:153
  5.0 12.9 %collective-permute-start.1 = (f32[1,2,12,128]{3,2,1,0:T(8,128)S(1)}, f32[1,2,12,128]{3,2,1,0:T(8,128)S(1)}, u32[]{:S(2)}, u32[]{:S(2)}) collective-permute-start(f32[1,2,12,128]{3,2,1,0:T(8,128)S(1)} %select_bitcast_fusion), channel_id=1, source_target_pairs={{0,8},{4,12},{8,0},{12,4},{1,9},{5,13},{9,1},{13,5},{2,10},{6,14},... | collective-permute-start | bytes 36872 | tf_op jit(solution)/shard_map/ppermute | solution.py:153
  7.7 1.6 %copy-start = (bf16[64,128,128]{2,1,0:T(8,128)(2,1)S(1)}, bf16[64,128,128]{2,1,0:T(8,128)(2,1)}, u32[]{:S(2)}) copy-start(bf16[64,128,128]{2,1,0:T(8,128)(2,1)} %tiles.1) | copy-start | bytes 6291460
  9.3 1.2 %copy-start.2 = (f32[4,256,256]{2,1,0:T(8,128)S(1)}, f32[4,256,256]{2,1,0:T(8,128)}, u32[]{:S(2)}) copy-start(f32[4,256,256]{2,1,0:T(8,128)} %param.8) | copy-start | bytes 3145732
  10.5 0.7 %copy-start.5 = (s32[1,1,1,4,768]{4,3,2,1,0:T(4,128)S(1)}, s32[1,1,1,4,768]{4,3,2,1,0:T(4,128)}, u32[]{:S(2)}) copy-start(s32[1,1,1,4,768]{4,3,2,1,0:T(4,128)} %param.11) | copy-start | bytes 36868
  11.2 0.7 %copy-start.7 = (s32[1,1,1,4,32]{4,3,2,1,0:T(4,128)S(1)}, s32[1,1,1,4,32]{4,3,2,1,0:T(4,128)}, u32[]{:S(2)}) copy-start(s32[1,1,1,4,32]{4,3,2,1,0:T(4,128)} %param.10) | copy-start | bytes 1540
  11.9 0.7 %copy-start.9 = (s32[1,1,1,4]{3,2,1,0:T(1,128)S(1)}, s32[1,1,1,4]{3,2,1,0:T(1,128)}, u32[]{:S(2)}) copy-start(s32[1,1,1,4]{3,2,1,0:T(1,128)} %param.12) | copy-start | bytes 52
  12.5 21.1 %copy-start.1 = (bf16[64,128,128]{2,1,0:T(8,128)(2,1)S(1)}, bf16[64,128,128]{2,1,0:T(8,128)(2,1)}, u32[]{:S(2)}) copy-start(bf16[64,128,128]{2,1,0:T(8,128)(2,1)} %tiles.1) | copy-start | bytes 6291460
  12.5 21.1 %copy-start.3 = (f32[4,256,256]{2,1,0:T(8,128)S(1)}, f32[4,256,256]{2,1,0:T(8,128)}, u32[]{:S(2)}) copy-start(f32[4,256,256]{2,1,0:T(8,128)} %param.8) | copy-start | bytes 3145732
  18.0 3.0 %collective-permute-start.2 = (f32[96,128]{1,0:T(8,128)S(1)}, f32[96,128]{1,0:T(8,128)S(1)}, u32[]{:S(2)}, u32[]{:S(2)}) collective-permute-start(f32[96,128]{1,0:T(8,128)S(1)} %select_subtract_fusion), channel_id=1, source_target_pairs={{0,1},{1,0},{2,3},{3,2},{4,5},{5,4},{6,7},{7,6},{8,9},{9,8},{10,11... | collective-permute-start | bytes 147464 | tf_op jit(solution)/shard_map/ppermute | solution.py:153
  21.1 3.1 %collective-permute-start.3 = (f32[120,128]{1,0:T(8,128)S(1)}, f32[120,128]{1,0:T(8,128)S(1)}, u32[]{:S(2)}, u32[]{:S(2)}) collective-permute-start(f32[120,128]{1,0:T(8,128)S(1)} %pad_maximum_fusion), channel_id=1, source_target_pairs={{0,2},{2,0},{1,3},{3,1},{4,6},{6,4},{5,7},{7,5},{8,10},{10,8},{9,1... | collective-permute-start | bytes 184328 | tf_op jit(solution)/shard_map/ppermute | solution.py:153
  24.2 4.1 %collective-permute-start.4 = (f32[32,128]{1,0:T(8,128)S(1)}, f32[32,128]{1,0:T(8,128)S(1)}, u32[]{:S(2)}, u32[]{:S(2)}) collective-permute-start(f32[32,128]{1,0:T(8,128)S(1)} %fusion.2), channel_id=1, source_target_pairs={{4,0},{8,4},{12,8},{1,5},{5,9},{9,13},{6,2},{10,6},{14,10},{3,7},{... | collective-permute-start | bytes 49160 | tf_op jit(solution)/shard_map/ppermute | solution.py:291
  28.3 5.2 %collective-permute-start.5 = (f32[80,128]{1,0:T(8,128)S(1)}, f32[80,128]{1,0:T(8,128)S(1)}, u32[]{:S(2)}, u32[]{:S(2)}) collective-permute-start(f32[80,128]{1,0:T(8,128)S(1)} %pad_maximum_fusion.2), channel_id=1, source_target_pairs={{0,1},{1,0},{2,3},{3,2},{4,5},{5,4},{6,7},{7,6},{8,9},{9,8},{10,11... | collective-permute-start | bytes 122888 | tf_op jit(solution)/shard_map/ppermute | solution.py:153
  33.6 1.2 %copy-start.4 = (f32[4,256,256]{2,1,0:T(8,128)S(1)}, f32[4,256,256]{2,1,0:T(8,128)}, u32[]{:S(2)}) copy-start(f32[4,256,256]{2,1,0:T(8,128)} %param.15) | copy-start | bytes 3145732

commit v3 on v2

v3 whole, which is shorter than its diff:
```python
import functools
import math

import jax
import jax.numpy as jnp
from jax import lax
from jax.experimental import pallas as pl
from jax.experimental.pallas import tpu as pltpu
from jax.sharding import PartitionSpec as P

ONE_HOT = 256
GROUP = 8
STATIC_ROWS = 4096
VMEM_LIMIT = 16 * 1024 * 1024


def forward_kernel(
    rows, window, live_in, tid_in, bid_in, vol_in, tiles_in, target_in, weight_in, out, sends,
    live, tid, bid, vol, tiles, target, weight, vox, picked, sems,
):
    angles, slots = tid.shape
    tile = tiles.shape[1]
    lines, width = vol.shape
    runs = width // tile
    pairs = (
        (bid_in, bid), (live_in, live), (tid_in, tid), (vol_in, vol),
        (target_in, target), (weight_in, weight), (tiles_in, tiles),
    )
    copies = [pltpu.make_async_copy(a, b, sems.at[i]) for i, (a, b) in enumerate(pairs)]
    for copy in copies:
        copy.start()
    copies[3].wait()
    step = 8
    for run in range(runs):
        for line in range(0, lines, step):
            vox[pl.ds(line * runs + run, step, stride=runs), :] = vol[
                line : line + step, run * tile : (run + 1) * tile
            ]
    for copy in copies[:3] + copies[4:6]:
        copy.wait()
    slabs = sends.shape[0]
    depth = window - 2
    sends[...] = jnp.zeros_like(sends)
    for s in range(slabs):
        low, high = max(s * depth - 1, 0), min(s * depth + depth + 1, slabs * depth)
        skip = low - (s * depth - 1)
        for own in range(target.shape[0]):
            for at, data in ((0, target), (window, weight)):
                sends[s, own, at + skip : at + skip + high - low, :] = data[own, low:high, :]

    def gather(a, at):
        for j in range(slots * rows):
            picked[at + j : at + j + 1, :] = vox[pl.ds(bid[a, j], 1), :]

    def project(a, at):
        count = live[a]
        total = jnp.zeros((rows, tile), jnp.float32)
        for g in range(0, slots, GROUP):
            left, right = [], []
            for k in range(g, g + GROUP):
                part = picked[at + k * rows : at + (k + 1) * rows, :]
                left.append(jnp.where(k < count, part, 0.0).astype(jnp.bfloat16))
                right.append(tiles[tid[a, k]])
            total += lax.dot_general(
                jnp.concatenate(left, axis=1),
                jnp.concatenate(right, axis=1),
                (((1,), (1,)), ((), ())),
                preferred_element_type=jnp.float32,
            )
        return total

    length = slots * rows
    if angles * length <= STATIC_ROWS:
        gather(0, 0)
        copies[6].wait()
        for a in range(angles):

            @pl.when(live[a] >= 0)
            def _():
                if a + 1 < angles:
                    gather(a + 1, (a + 1) % 2 * length)
                out[a * rows : (a + 1) * rows, :] = project(a, a % 2 * length)

    else:
        copies[6].wait()

        def project_angle(a, carry):
            gather(a, 0)
            out[pl.ds(pl.multiple_of(a * rows, 8), rows), :] = project(a, 0)
            return carry

        lax.fori_loop(0, angles, project_angle, 0)


def backward_kernel(
    rows, live, tid, bid, head, middle, tail, target, weight, tiles, vol_in, col_in, out_in,
    res, hot, code, spread, vol, col, out, sems,
):
    angles, slots = tid.shape
    tile = tiles.shape[1]
    lines, width = vol.shape
    runs = width // tile
    high = hot.shape[0]
    length = slots * rows
    reads = [
        pltpu.make_async_copy(vol_in, vol, sems.at[0]),
        pltpu.make_async_copy(col_in, col, sems.at[1]),
    ]
    for copy in reads:
        copy.start()
    for a in range(angles):
        parts = []
        for part in (head, middle, tail):
            size = part.shape[0] // angles
            parts.append(part[a * size : (a + 1) * size, :])
        here = slice(a * rows, (a + 1) * rows)
        error = target[here, :] - jnp.concatenate(parts, axis=0)
        res[a] = (weight[here, :] * error).astype(jnp.bfloat16)

    place = lax.broadcasted_iota(jnp.int32, (high, tile), 0)
    position = lax.broadcasted_iota(jnp.int32, (1, tile), 1)
    for a in range(angles):
        groups = []
        for c in range(0, length, tile):
            block = bid[a : a + 1, c : c + tile]
            line = block // runs
            hot[:, a * length + c : a * length + c + tile] = jnp.where(
                place == line % high, 1.0, 0.0
            ).astype(jnp.bfloat16)
            group = (line // high) * runs + block % runs
            groups.append(jnp.where(position + c < live[a] * rows, group, -1))
        pad = -len(groups) % 8
        groups += [jnp.zeros((1, tile), jnp.int32)] * pad
        turned = jnp.concatenate(groups, axis=0).astype(jnp.float32).T
        for i in range(length // tile):
            wide = jnp.broadcast_to(turned[:, i : i + 1], (tile, tile))
            code[a * length + i * tile : a * length + (i + 1) * tile, :] = wide.astype(
                jnp.bfloat16
            )

    def spread_angle(a, carry):
        values = res[a]

        def group(g, inner):
            for u in range(0, GROUP, 2):
                k = g * GROUP + u
                pair = jnp.concatenate([tiles[tid[a, k]], tiles[tid[a, k + 1]]], axis=1)
                made = jnp.dot(values, pair, preferred_element_type=jnp.float32)
                both = jnp.concatenate([made[:, :tile], made[:, tile:]], axis=0)
                at = pl.multiple_of((a * slots + k) * rows, 16)
                spread[pl.ds(at, 2 * rows), :] = both.astype(jnp.bfloat16)
            return inner

        return lax.fori_loop(0, (live[a] + GROUP - 1) // GROUP, group, carry)

    lax.fori_loop(0, angles, spread_angle, 0)

    writes = []
    for chunk in range(lines // high):
        values = spread[...]
        groups = code[...]
        right = jnp.concatenate(
            [
                jnp.where(groups == jnp.bfloat16(chunk * runs + run), values, jnp.bfloat16(0))
                for run in range(runs)
            ],
            axis=1,
        )
        made = jnp.dot(hot[...], right, preferred_element_type=jnp.float32)
        if chunk == 0:
            for copy in reads:
                copy.wait()
        here = pl.ds(chunk * high, high)
        out[here, :] = vol[here, :] + col[here, :] * made
        copy = pltpu.make_async_copy(out.at[here, :], out_in.at[here, :], sems.at[2 + chunk])
        copy.start()
        writes.append(copy)
    for copy in writes:
        copy.wait()


def swap(values, axis, bit):
    return lax.ppermute(values, axis, [(i, i ^ bit) for i in range(lax.axis_size(axis))])


def swap_many(arrays, axis, bit):
    if len({array.shape[-1] for array in arrays}) > 1:
        return [swap(array, axis, bit) for array in arrays]
    width = arrays[0].shape[-1]
    came = swap(jnp.concatenate([a.reshape(-1, width) for a in arrays], axis=0), axis, bit)
    out, at = [], 0
    for array in arrays:
        count = array.size // width
        out.append(came[at : at + count].reshape(array.shape))
        at += count
    return out


def bits(axis):
    return [1 << i for i in range((lax.axis_size(axis) - 1).bit_length())]


def ordered(mine_high, own, other, axis):
    return jnp.concatenate(
        [jnp.where(mine_high, other, own), jnp.where(mine_high, own, other)], axis=axis
    )


def to_slabs(sends, anchors):
    here = lax.axis_index("gz")
    for bit in bits("gz"):
        high = (here & bit) != 0
        halves = sends.reshape((sends.shape[0] // 2, 2) + sends.shape[1:])
        keep = jnp.where(high, halves[:, 1], halves[:, 0])
        give = jnp.where(high, halves[:, 0], halves[:, 1])
        came = swap(give, "gz", bit)
        if bit in anchors:
            came, _ = lax.optimization_barrier((came, anchors[bit]))
        sends = ordered(high, keep, came, 1)
    return sends[0]


def on_device(volume, tile_table, tile_ids, block_ids, live_slots, measured, row_norm, col_norm):
    slab_depth, column_width, half_width = volume.shape
    tile_size = tile_table.shape[1]
    angle_count, slot_count = tile_ids.shape[3:]
    window = slab_depth + 2
    block_cols = block_ids.shape[4] // (slot_count * window)
    rows = window * block_cols
    rim = 2 * block_cols
    length = slot_count * rows
    lines = slab_depth * column_width
    runs = half_width // tile_size
    high = math.gcd(lines, ONE_HOT)
    slab_count = lax.axis_size("gz")
    own_angles, local_cols, row_total = measured.shape

    def held(array):
        return pltpu.with_memory_space_constraint(array, pltpu.HBM)

    tid = tile_ids.reshape(angle_count, slot_count)
    bid = block_ids.reshape(angle_count, length)
    live = live_slots.reshape(angle_count)
    vol = held(volume.reshape(lines, half_width))
    col = held(col_norm.reshape(lines, half_width))

    smem = pl.BlockSpec(memory_space=pltpu.SMEM)
    vmem = pl.BlockSpec(memory_space=pltpu.VMEM)
    hbm = pl.BlockSpec(memory_space=pltpu.HBM)
    params = pltpu.CompilerParams(vmem_limit_bytes=VMEM_LIMIT)
    buffers = 2 if angle_count * length <= STATIC_ROWS else 1

    partial, sends = pl.pallas_call(
        functools.partial(forward_kernel, rows, window),
        out_shape=(
            jax.ShapeDtypeStruct((angle_count * rows, tile_size), jnp.float32),
            jax.ShapeDtypeStruct((slab_count, own_angles, 2 * window, local_cols), jnp.float32),
        ),
        in_specs=[hbm] * 7,
        out_specs=(vmem, vmem),
        scratch_shapes=[
            pltpu.SMEM((angle_count,), jnp.int32),
            pltpu.SMEM((angle_count, slot_count), jnp.int32),
            pltpu.SMEM((angle_count, length), jnp.int32),
            pltpu.VMEM((lines, half_width), jnp.float32),
            pltpu.VMEM(tile_table.shape, jnp.bfloat16),
            pltpu.VMEM((own_angles, row_total, local_cols), jnp.float32),
            pltpu.VMEM((own_angles, row_total, local_cols), jnp.float32),
            pltpu.VMEM((lines * runs, tile_size), jnp.float32),
            pltpu.VMEM((buffers * length, tile_size), jnp.float32),
            pltpu.SemaphoreType.DMA((7,)),
        ],
        compiler_params=params,
        name="forward",
    )(
        held(live), held(tid), held(bid), vol, held(tile_table),
        held(measured.transpose(0, 2, 1)), held(row_norm.transpose(0, 2, 1)),
    )

    assert lax.axis_size("row") == 2
    upper = lax.axis_index("row") == 1
    total = partial + swap(partial, "row", 1)
    blocks = total.reshape(angle_count, rows, tile_size)
    outer = jnp.where(upper, blocks[:, rows - rim :], blocks[:, :rim])
    middle = blocks[:, rim : rows - rim]
    for bit in bits("gx"):
        came = swap_many([outer, middle], "gx", bit)
        outer, middle = outer + came[0], middle + came[1]
    last = slab_count - 1
    hops = [((z + 1) * 2, z * 2) for z in range(last)]
    hops += [(z * 2 + 1, z * 2 + 3) for z in range(last)]
    rims = lax.ppermute(outer.reshape(angle_count * rim, tile_size), ("gz", "row"), hops)
    outer = outer.reshape(rims.shape)

    columns = to_slabs(sends, {1: total, 2: outer})[None]
    for bit in bits("gx"):
        came = swap(columns, "gx", bit)
        columns = ordered((lax.axis_index("gx") & bit) != 0, columns, came, 0)
    other_outer, other_rims, other_columns = swap_many([outer, rims, columns], "row", 1)
    own_rim = outer + other_rims
    far_rim = other_outer + rims
    head = jnp.where(upper, far_rim, own_rim)
    tail = jnp.where(upper, own_rim, far_rim)
    columns = ordered(upper, columns[:, None], other_columns[:, None], 1)
    columns = columns.reshape(-1, angle_count, 2, window, local_cols)
    columns = columns.transpose(2, 1, 3, 0, 4).reshape(2, angle_count * rows, tile_size)

    made = pl.pallas_call(
        functools.partial(backward_kernel, rows),
        out_shape=jax.ShapeDtypeStruct((lines, half_width), jnp.float32),
        in_specs=[smem, smem] + [vmem] * 7 + [hbm] * 2,
        out_specs=hbm,
        scratch_shapes=[
            pltpu.VMEM((angle_count, rows, tile_size), jnp.bfloat16),
            pltpu.VMEM((high, angle_count * length), jnp.bfloat16),
            pltpu.VMEM((angle_count * length, tile_size), jnp.bfloat16),
            pltpu.VMEM((angle_count * length, tile_size), jnp.bfloat16),
            pltpu.VMEM((lines, half_width), jnp.float32),
            pltpu.VMEM((lines, half_width), jnp.float32),
            pltpu.VMEM((lines, half_width), jnp.float32),
            pltpu.SemaphoreType.DMA((2 + lines // high,)),
        ],
        compiler_params=params,
        name="backward",
    )(
        live, tid, bid, head, middle.reshape(-1, tile_size), tail, columns[0], columns[1],
        tile_table, vol, col,
    )
    return made.reshape(slab_depth, column_width, half_width)


def solution(mesh):
    placed = (
        P(("grp", "gz"), "gx", "row"),
        P(),
        P("gz", "gx", "row", None, None),
        P("gz", "gx", "row", None, None),
        P("gz", "gx", "row", None),
        P(("grp", "gz"), ("gx", "row"), None),
        P("gz", ("gx", "row"), None),
        P("gz", "gx", "row"),
    )

    return jax.shard_map(
        on_device,
        mesh=mesh,
        in_specs=placed,
        out_specs=P(("grp", "gz"), "gx", "row"),
        check_vma=False,
    )
```

time: 40.9 us -> 31.2 us (0.76)
  the two profiles are of different devices: /device:TPU:1 before, /device:TPU:2 now
where the time goes in v3:
time: 31.2 us; the launch traced here: 31.1 us
  Pallas kernels  13.1 us (42%)
  waiting for transfers between devices  9.43 us (30%)
  starting transfers between devices  8.13 us (26%)
    pallas_call x1, Pallas kernels, on_device(): pl.pallas_call(functools.partial(backward_kernel, rows), out_shape=jax.Sh...  8.04 us
    ppermute x6, starting transfers between devices, swap(): lax.ppermute(values, axis, [(i, i ^ bit) for i in range(lax.axis_size(axi...  6.85 us
    ppermute x6, waiting for transfers between devices, swap(): lax.ppermute(values, axis, [(i, i ^ bit) for i in range(lax.axis_size(axi...  5.94 us
    pallas_call x1, Pallas kernels, on_device(): pl.pallas_call(functools.partial(forward_kernel, rows, window), out_shape...  5.05 us
    ppermute x1, waiting for transfers between devices, on_device(): lax.ppermute(outer.reshape(angle_count * rim, tile_size), ('gz', 'row'),...  3.49 us
    ppermute x1, starting transfers between devices, on_device(): lax.ppermute(outer.reshape(angle_count * rim, tile_size), ('gz', 'row'),...  1.28 us
  transfers between devices with their start and end apart: 7, of which 6 were waited for; matrix products, arithmetic and copies ran while one was open for 0% of the time, Pallas kernels for 0%

profile of v3, /device:TPU:2, one launch (start us, length us, event | category | flops | bytes accessed | tf_op | source)
XLA Modules:
  0.0 31.1 jit_solution(564464154209874202)
XLA Ops:
  0.0 5.0 %forward.1 = (f32[96,128]{1,0:T(8,128)S(1)}, f32[4,1,12,128]{3,2,1,0:T(8,128)S(1)}) custom-call(s32[4]{0:T(128)} %bitcast.81, s32[4,32]{1,0:T(4,128)} %bitcast.79, s32[4,768]{1,0:T(4,128)} %bitcast.77, f32[1024,256]{1,0:T(8,128)} %bitcast.83, bf16[64,128,128]{2,1,0:T(8,128)(2,1)} %tiles.1, f32[1,16,128]{2,1,0:T(8,128)} %bitcast.91, f32[1,16,128]{2,1,0:T(8,128)} %bitcast.92), custom_call_target="tpu_custom_call" | custom-call | tf_op jit(solution)/shard_map/forward/pallas_call | solution.py:253
  5.1 0.0 copy-start
  5.1 0.0 copy-start.1
  5.1 0.0 copy-start.2
  5.1 0.0 copy-start.3
  5.1 0.1 collective-permute-start
  5.2 1.6 %collective-permute-start.3 = (f32[2,1,12,128]{3,2,1,0:T(8,128)S(1)}, f32[2,1,12,128]{3,2,1,0:T(8,128)S(1)}, u32[]{:S(2)}, u32[]{:S(2)}) collective-permute-start(f32[2,1,12,128]{3,2,1,0:T(8,128)S(1)} %select_bitcast_fusion.1), channel_id=1, source_target_pairs={{0,4},{4,0},{8,12},{12,8},{1,5},{5,1},{9,13},{13,9},{2,6},{6,2},{1... | collective-permute-start | bytes 36872 | tf_op jit(solution)/shard_map/ppermute | solution.py:183
  6.8 0.0 collective-permute-done
  6.9 2.2 %collective-permute-done.3 = f32[2,1,12,128]{3,2,1,0:T(8,128)S(1)} collective-permute-done((f32[2,1,12,128]{3,2,1,0:T(8,128)S(1)}, f32[2,1,12,128]{3,2,1,0:T(8,128)S(1)}, u32[]{:S(2)}, u32[]{:S(2)}) %collective-permute-start.3) | collective-permute-done | bytes 12320 | tf_op jit(solution)/shard_map/ppermute | solution.py:183
  9.0 0.2 collective-permute-start.1
  9.2 3.1 %collective-permute-start.4 = (f32[1,2,12,128]{3,2,1,0:T(8,128)S(1)}, f32[1,2,12,128]{3,2,1,0:T(8,128)S(1)}, u32[]{:S(2)}, u32[]{:S(2)}) collective-permute-start(f32[1,2,12,128]{3,2,1,0:T(8,128)S(1)} %select_bitcast_fusion), channel_id=1, source_target_pairs={{0,8},{4,12},{8,0},{12,4},{1,9},{5,13},{9,1},{13,5},{2,10},{6,14},... | collective-permute-start | bytes 36872 | tf_op jit(solution)/shard_map/ppermute | solution.py:183
  12.3 0.7 %collective-permute-done.1 = f32[64,128]{1,0:T(8,128)S(1)} collective-permute-done((f32[64,128]{1,0:T(8,128)S(1)}, f32[64,128]{1,0:T(8,128)S(1)}, u32[]{:S(2)}, u32[]{:S(2)}) %collective-permute-start.1) | collective-permute-done | bytes 32800 | tf_op jit(solution)/shard_map/ppermute | solution.py:183
  13.0 1.0 %collective-permute-done.4 = f32[1,2,12,128]{3,2,1,0:T(8,128)S(1)} collective-permute-done((f32[1,2,12,128]{3,2,1,0:T(8,128)S(1)}, f32[1,2,12,128]{3,2,1,0:T(8,128)S(1)}, u32[]{:S(2)}, u32[]{:S(2)}) %collective-permute-start.4) | collective-permute-done | bytes 12320 | tf_op jit(solution)/shard_map/ppermute | solution.py:183
  14.0 1.9 %collective-permute-start.5 = (f32[1,4,12,128]{3,2,1,0:T(8,128)S(1)}, f32[1,4,12,128]{3,2,1,0:T(8,128)S(1)}, u32[]{:S(2)}, u32[]{:S(2)}) collective-permute-start(f32[1,4,12,128]{3,2,1,0:T(8,128)S(1)} %pad_maximum_fusion.5), channel_id=1, source_target_pairs={{0,2},{2,0},{1,3},{3,1},{4,6},{6,4},{5,7},{7,5},{8,10},{10,8},{9,1... | collective-permute-start | bytes 73736 | tf_op jit(solution)/shard_map/ppermute | solution.py:183
  15.9 1.3 %collective-permute-start.2 = (f32[32,128]{1,0:T(8,128)S(1)}, f32[32,128]{1,0:T(8,128)S(1)}, u32[]{:S(2)}, u32[]{:S(2)}) collective-permute-start(f32[32,128]{1,0:T(8,128)S(1)} %get-tuple-element.20), channel_id=1, source_target_pairs={{4,0},{8,4},{12,8},{1,5},{5,9},{9,13},{6,2},{10,6},{14,10},{3,7},{... | collective-permute-start | bytes 49160 | tf_op jit(solution)/shard_map/ppermute | solution.py:292
  17.2 0.8 %collective-permute-done.5 = f32[1,4,12,128]{3,2,1,0:T(8,128)S(1)} collective-permute-done((f32[1,4,12,128]{3,2,1,0:T(8,128)S(1)}, f32[1,4,12,128]{3,2,1,0:T(8,128)S(1)}, u32[]{:S(2)}, u32[]{:S(2)}) %collective-permute-start.5) | collective-permute-done | bytes 24608 | tf_op jit(solution)/shard_map/ppermute | solution.py:183
  18.1 3.5 %collective-permute-done.2 = f32[32,128]{1,0:T(8,128)S(1)} collective-permute-done((f32[32,128]{1,0:T(8,128)S(1)}, f32[32,128]{1,0:T(8,128)S(1)}, u32[]{:S(2)}, u32[]{:S(2)}) %collective-permute-start.2) | collective-permute-done | bytes 16416 | tf_op jit(solution)/shard_map/ppermute | solution.py:292
  21.6 0.0 collective-permute-start.6
  21.6 1.3 %collective-permute-done.6 = f32[160,128]{1,0:T(8,128)S(1)} collective-permute-done((f32[160,128]{1,0:T(8,128)S(1)}, f32[160,128]{1,0:T(8,128)S(1)}, u32[]{:S(2)}, u32[]{:S(2)}) %collective-permute-start.6) | collective-permute-done | bytes 81952 | tf_op jit(solution)/shard_map/ppermute | solution.py:183
  23.0 0.0 copy-done
  23.0 0.0 copy-done.1
  23.0 0.0 copy-done.2
  23.0 0.0 copy-done.3
  23.1 8.0 %backward.1 = f32[1024,256]{1,0:T(8,128)} custom-call(s32[4]{0:T(128)S(1)} %bitcast.82, s32[4,32]{1,0:T(4,128)S(1)} %bitcast.80, s32[4,768]{1,0:T(4,128)S(1)} %bitcast.78, f32[32,128]{1,0:T(8,128)S(1)} %get-tuple-element.16.head, f32[32,128]{1,0:T(8,128)S(1)} %get-tuple-element.19.middle, f32[32,128]{1,0:T(8,128)S(1)} %get-tuple-element.15.tail, ...), custom_call_target="tpu_custom_call" | custom-call | tf_op jit(solution)/shard_map/backward/pallas_call | solution.py:308
  (23 shorter events, 0.2 us)
Async XLA Ops:
  5.1 18.0 %copy-start = (bf16[64,128,128]{2,1,0:T(8,128)(2,1)S(1)}, bf16[64,128,128]{2,1,0:T(8,128)(2,1)}, u32[]{:S(2)}) copy-start(bf16[64,128,128]{2,1,0:T(8,128)(2,1)} %tiles.1) | copy-start | bytes 6291460
  5.1 18.0 %copy-start.1 = (s32[1,1,1,4,768]{4,3,2,1,0:T(4,128)S(1)}, s32[1,1,1,4,768]{4,3,2,1,0:T(4,128)}, u32[]{:S(2)}) copy-start(s32[1,1,1,4,768]{4,3,2,1,0:T(4,128)} %param.11) | copy-start | bytes 36868
  5.1 18.0 %copy-start.2 = (s32[1,1,1,4,32]{4,3,2,1,0:T(4,128)S(1)}, s32[1,1,1,4,32]{4,3,2,1,0:T(4,128)}, u32[]{:S(2)}) copy-start(s32[1,1,1,4,32]{4,3,2,1,0:T(4,128)} %param.10) | copy-start | bytes 1540
  5.1 18.0 %copy-start.3 = (s32[1,1,1,4]{3,2,1,0:T(1,128)S(1)}, s32[1,1,1,4]{3,2,1,0:T(1,128)}, u32[]{:S(2)}) copy-start(s32[1,1,1,4]{3,2,1,0:T(1,128)} %param.12) | copy-start | bytes 52
  5.1 1.7 %collective-permute-start = (f32[96,128]{1,0:T(8,128)S(1)}, f32[96,128]{1,0:T(8,128)S(1)}, u32[]{:S(2)}, u32[]{:S(2)}) collective-permute-start(f32[96,128]{1,0:T(8,128)S(1)} %get-tuple-element.9), channel_id=1, source_target_pairs={{0,1},{1,0},{2,3},{3,2},{4,5},{5,4},{6,7},{7,6},{8,9},{9,8},{10,11... | collective-permute-start | bytes 147464 | tf_op jit(solution)/shard_map/ppermute | solution.py:183
  5.2 3.8 %collective-permute-start.3 = (f32[2,1,12,128]{3,2,1,0:T(8,128)S(1)}, f32[2,1,12,128]{3,2,1,0:T(8,128)S(1)}, u32[]{:S(2)}, u32[]{:S(2)}) collective-permute-start(f32[2,1,12,128]{3,2,1,0:T(8,128)S(1)} %select_bitcast_fusion.1), channel_id=1, source_target_pairs={{0,4},{4,0},{8,12},{12,8},{1,5},{5,1},{9,13},{13,9},{2,6},{6,2},{1... | collective-permute-start | bytes 36872 | tf_op jit(solution)/shard_map/ppermute | solution.py:183
  9.0 4.0 %collective-permute-start.1 = (f32[64,128]{1,0:T(8,128)S(1)}, f32[64,128]{1,0:T(8,128)S(1)}, u32[]{:S(2)}, u32[]{:S(2)}) collective-permute-start(f32[64,128]{1,0:T(8,128)S(1)} %pad_maximum_fusion.4), channel_id=1, source_target_pairs={{0,2},{2,0},{1,3},{3,1},{4,6},{6,4},{5,7},{7,5},{8,10},{10,8},{9,1... | collective-permute-start | bytes 98312 | tf_op jit(solution)/shard_map/ppermute | solution.py:183
  9.2 4.8 %collective-permute-start.4 = (f32[1,2,12,128]{3,2,1,0:T(8,128)S(1)}, f32[1,2,12,128]{3,2,1,0:T(8,128)S(1)}, u32[]{:S(2)}, u32[]{:S(2)}) collective-permute-start(f32[1,2,12,128]{3,2,1,0:T(8,128)S(1)} %select_bitcast_fusion), channel_id=1, source_target_pairs={{0,8},{4,12},{8,0},{12,4},{1,9},{5,13},{9,1},{13,5},{2,10},{6,14},... | collective-permute-start | bytes 36872 | tf_op jit(solution)/shard_map/ppermute | solution.py:183
  14.0 4.0 %collective-permute-start.5 = (f32[1,4,12,128]{3,2,1,0:T(8,128)S(1)}, f32[1,4,12,128]{3,2,1,0:T(8,128)S(1)}, u32[]{:S(2)}, u32[]{:S(2)}) collective-permute-start(f32[1,4,12,128]{3,2,1,0:T(8,128)S(1)} %pad_maximum_fusion.5), channel_id=1, source_target_pairs={{0,2},{2,0},{1,3},{3,1},{4,6},{6,4},{5,7},{7,5},{8,10},{10,8},{9,1... | collective-permute-start | bytes 73736 | tf_op jit(solution)/shard_map/ppermute | solution.py:183
  15.9 5.6 %collective-permute-start.2 = (f32[32,128]{1,0:T(8,128)S(1)}, f32[32,128]{1,0:T(8,128)S(1)}, u32[]{:S(2)}, u32[]{:S(2)}) collective-permute-start(f32[32,128]{1,0:T(8,128)S(1)} %get-tuple-element.20), channel_id=1, source_target_pairs={{4,0},{8,4},{12,8},{1,5},{5,9},{9,13},{6,2},{10,6},{14,10},{3,7},{... | collective-permute-start | bytes 49160 | tf_op jit(solution)/shard_map/ppermute | solution.py:292
  21.6 1.3 %collective-permute-start.6 = (f32[160,128]{1,0:T(8,128)S(1)}, f32[160,128]{1,0:T(8,128)S(1)}, u32[]{:S(2)}, u32[]{:S(2)}) collective-permute-start(f32[160,128]{1,0:T(8,128)S(1)} %pad_maximum_fusion.1), channel_id=1, source_target_pairs={{0,1},{1,0},{2,3},{3,2},{4,5},{5,4},{6,7},{7,6},{8,9},{9,8},{10,11... | collective-permute-start | bytes 245768 | tf_op jit(solution)/shard_map/ppermute | solution.py:183

commit v4 on v3

--- a/solution.py
+++ b/solution.py
@@ -14,18 +14,35 @@
 VMEM_LIMIT = 16 * 1024 * 1024
 
 
+def pack_kernel(window, target_in, weight_in, sends, target, weight, sems):
+    copies = [
+        pltpu.make_async_copy(target_in, target, sems.at[0]),
+        pltpu.make_async_copy(weight_in, weight, sems.at[1]),
+    ]
+    for copy in copies:
+        copy.start()
+    sends[...] = jnp.zeros_like(sends)
+    for copy in copies:
+        copy.wait()
+    slabs = sends.shape[0]
+    depth = window - 2
+    for s in range(slabs):
+        low, high = max(s * depth - 1, 0), min(s * depth + depth + 1, slabs * depth)
+        skip = low - (s * depth - 1)
+        for own in range(target.shape[0]):
+            for at, data in ((0, target), (window, weight)):
+                sends[s, own, at + skip : at + skip + high - low, :] = data[own, low:high, :]
+
+
 def forward_kernel(
-    rows, window, live_in, tid_in, bid_in, vol_in, tiles_in, target_in, weight_in, out, sends,
-    live, tid, bid, vol, tiles, target, weight, vox, picked, sems,
+    rows, live_in, tid_in, bid_in, vol_in, tiles_in, out,
+    live, tid, bid, vol, tiles, vox, picked, sems,
 ):
     angles, slots = tid.shape
     tile = tiles.shape[1]
     lines, width = vol.shape
     runs = width // tile
-    pairs = (
-        (bid_in, bid), (live_in, live), (tid_in, tid), (vol_in, vol),
-        (target_in, target), (weight_in, weight), (tiles_in, tiles),
-    )
+    pairs = ((bid_in, bid), (live_in, live), (tid_in, tid), (vol_in, vol), (tiles_in, tiles))
     copies = [pltpu.make_async_copy(a, b, sems.at[i]) for i, (a, b) in enumerate(pairs)]
     for copy in copies:
         copy.start()
@@ -36,17 +53,8 @@
             vox[pl.ds(line * runs + run, step, stride=runs), :] = vol[
                 line : line + step, run * tile : (run + 1) * tile
             ]
-    for copy in copies[:3] + copies[4:6]:
+    for copy in copies[:3]:
         copy.wait()
-    slabs = sends.shape[0]
-    depth = window - 2
-    sends[...] = jnp.zeros_like(sends)
-    for s in range(slabs):
-        low, high = max(s * depth - 1, 0), min(s * depth + depth + 1, slabs * depth)
-        skip = low - (s * depth - 1)
-        for own in range(target.shape[0]):
-            for at, data in ((0, target), (window, weight)):
-                sends[s, own, at + skip : at + skip + high - low, :] = data[own, low:high, :]
 
     def gather(a, at):
         for j in range(slots * rows):
@@ -72,7 +80,7 @@
     length = slots * rows
     if angles * length <= STATIC_ROWS:
         gather(0, 0)
-        copies[6].wait()
+        copies[4].wait()
         for a in range(angles):
 
             @pl.when(live[a] >= 0)
@@ -82,7 +90,7 @@
                 out[a * rows : (a + 1) * rows, :] = project(a, a % 2 * length)
 
     else:
-        copies[6].wait()
+        copies[4].wait()
 
         def project_angle(a, carry):
             gather(a, 0)
@@ -94,7 +102,7 @@
 
 def backward_kernel(
     rows, live, tid, bid, head, middle, tail, target, weight, tiles, vol_in, col_in, out_in,
-    res, hot, code, spread, vol, col, out, sems,
+    res, hot, code, spread, vol, col, out, total, sems,
 ):
     angles, slots = tid.shape
     tile = tiles.shape[1]
@@ -117,16 +125,17 @@
         error = target[here, :] - jnp.concatenate(parts, axis=0)
         res[a] = (weight[here, :] * error).astype(jnp.bfloat16)
 
-    place = lax.broadcasted_iota(jnp.int32, (high, tile), 0)
+    place = lax.broadcasted_iota(jnp.int32, (high, tile), 0).astype(jnp.bfloat16)
     position = lax.broadcasted_iota(jnp.int32, (1, tile), 1)
     for a in range(angles):
         groups = []
         for c in range(0, length, tile):
             block = bid[a : a + 1, c : c + tile]
             line = block // runs
+            low = (line % high).astype(jnp.bfloat16)
             hot[:, a * length + c : a * length + c + tile] = jnp.where(
-                place == line % high, 1.0, 0.0
-            ).astype(jnp.bfloat16)
+                place == low, jnp.bfloat16(1), jnp.bfloat16(0)
+            )
             group = (line // high) * runs + block % runs
             groups.append(jnp.where(position + c < live[a] * rows, group, -1))
         pad = -len(groups) % 8
@@ -138,43 +147,61 @@
                 jnp.bfloat16
             )
 
-    def spread_angle(a, carry):
-        values = res[a]
-
-        def group(g, inner):
-            for u in range(0, GROUP, 2):
-                k = g * GROUP + u
-                pair = jnp.concatenate([tiles[tid[a, k]], tiles[tid[a, k + 1]]], axis=1)
-                made = jnp.dot(values, pair, preferred_element_type=jnp.float32)
-                both = jnp.concatenate([made[:, :tile], made[:, tile:]], axis=0)
-                at = pl.multiple_of((a * slots + k) * rows, 16)
-                spread[pl.ds(at, 2 * rows), :] = both.astype(jnp.bfloat16)
-            return inner
-
-        return lax.fori_loop(0, (live[a] + GROUP - 1) // GROUP, group, carry)
-
-    lax.fori_loop(0, angles, spread_angle, 0)
-
-    writes = []
-    for chunk in range(lines // high):
-        values = spread[...]
-        groups = code[...]
+    def spread_pair(values, a, k, at):
+        pair = jnp.concatenate([tiles[tid[a, k]], tiles[tid[a, k + 1]]], axis=1)
+        made = jnp.dot(values, pair, preferred_element_type=jnp.float32)
+        both = jnp.concatenate([made[:, :tile], made[:, tile:]], axis=0)
+        spread[pl.ds(at, 2 * rows), :] = both.astype(jnp.bfloat16)
+
+    def add_part(at, size, first, count):
+        values = spread[pl.ds(at, size), :]
+        groups = code[pl.ds(at, size), :]
         right = jnp.concatenate(
             [
-                jnp.where(groups == jnp.bfloat16(chunk * runs + run), values, jnp.bfloat16(0))
-                for run in range(runs)
+                jnp.where(groups == jnp.bfloat16(g), values, jnp.bfloat16(0))
+                for g in range(first * runs, (first + count) * runs)
             ],
             axis=1,
         )
-        made = jnp.dot(hot[...], right, preferred_element_type=jnp.float32)
-        if chunk == 0:
-            for copy in reads:
-                copy.wait()
-        here = pl.ds(chunk * high, high)
-        out[here, :] = vol[here, :] + col[here, :] * made
-        copy = pltpu.make_async_copy(out.at[here, :], out_in.at[here, :], sems.at[2 + chunk])
-        copy.start()
-        writes.append(copy)
+        return jnp.dot(hot[:, pl.ds(at, size)], right, preferred_element_type=jnp.float32)
+
+    chunks = lines // high
+    writes = []
+
+    def finish(first, count, made):
+        for i in range(count):
+            here = pl.ds((first + i) * high, high)
+            out[here, :] = vol[here, :] + col[here, :] * made[:, i * width : (i + 1) * width]
+            copy = pltpu.make_async_copy(
+                out.at[here, :], out_in.at[here, :], sems.at[2 + first + i]
+            )
+            copy.start()
+            writes.append(copy)
+
+    if angles * length <= STATIC_ROWS:
+        for a in range(angles):
+            values = res[a]
+            for k in range(0, slots, 2):
+                spread_pair(values, a, k, (a * slots + k) * rows)
+        made = add_part(0, angles * length, 0, chunks)
+        for copy in reads:
+            copy.wait()
+        finish(0, chunks, made)
+    else:
+
+        def step(a, carry):
+            values = res[a]
+            base = pl.multiple_of(a * length, 256)
+            for k in range(0, slots, 2):
+                spread_pair(values, a, k, base + k * rows)
+            total[...] += add_part(base, length, 0, chunks)
+            return carry
+
+        total[...] = jnp.zeros_like(total)
+        lax.fori_loop(0, angles, step, 0)
+        for copy in reads:
+            copy.wait()
+        finish(0, chunks, total[...])
     for copy in writes:
         copy.wait()
 
@@ -206,18 +233,16 @@
     )
 
 
-def to_slabs(sends, anchors):
-    here = lax.axis_index("gz")
-    for bit in bits("gz"):
-        high = (here & bit) != 0
-        halves = sends.reshape((sends.shape[0] // 2, 2) + sends.shape[1:])
-        keep = jnp.where(high, halves[:, 1], halves[:, 0])
-        give = jnp.where(high, halves[:, 0], halves[:, 1])
-        came = swap(give, "gz", bit)
-        if bit in anchors:
-            came, _ = lax.optimization_barrier((came, anchors[bit]))
-        sends = ordered(high, keep, came, 1)
-    return sends[0]
+def exchange_slabs(parts, bit):
+    high = (lax.axis_index("gz") & bit) != 0
+    count = parts.shape[0] // 2
+    halves = parts.reshape((2, count) + parts.shape[1:])
+    keep = jnp.where(high, halves[1], halves[0])
+    give = jnp.where(high, halves[0], halves[1])
+    came = swap(give, "gz", bit)
+    low, up = jnp.where(high, came, keep), jnp.where(high, keep, came)
+    both = jnp.stack([low, up], axis=2)
+    return both.reshape((count, parts.shape[1] * 2) + parts.shape[2:])
 
 
 def on_device(volume, tile_table, tile_ids, block_ids, live_slots, measured, row_norm, col_norm):
@@ -250,32 +275,43 @@
     params = pltpu.CompilerParams(vmem_limit_bytes=VMEM_LIMIT)
     buffers = 2 if angle_count * length <= STATIC_ROWS else 1
 
-    partial, sends = pl.pallas_call(
-        functools.partial(forward_kernel, rows, window),
-        out_shape=(
-            jax.ShapeDtypeStruct((angle_count * rows, tile_size), jnp.float32),
-            jax.ShapeDtypeStruct((slab_count, own_angles, 2 * window, local_cols), jnp.float32),
+    sends = pl.pallas_call(
+        functools.partial(pack_kernel, window),
+        out_shape=jax.ShapeDtypeStruct(
+            (slab_count, own_angles, 2 * window, local_cols), jnp.float32
         ),
-        in_specs=[hbm] * 7,
-        out_specs=(vmem, vmem),
+        in_specs=[hbm] * 2,
+        out_specs=vmem,
+        scratch_shapes=[
+            pltpu.VMEM((own_angles, row_total, local_cols), jnp.float32),
+            pltpu.VMEM((own_angles, row_total, local_cols), jnp.float32),
+            pltpu.SemaphoreType.DMA((2,)),
+        ],
+        compiler_params=params,
+        name="pack",
+    )(held(measured.transpose(0, 2, 1)), held(row_norm.transpose(0, 2, 1)))
+    columns = sends[:, None]
+    for bit in bits("gz")[:0:-1]:
+        columns = exchange_slabs(columns, bit)
+
+    partial = pl.pallas_call(
+        functools.partial(forward_kernel, rows),
+        out_shape=jax.ShapeDtypeStruct((angle_count * rows, tile_size), jnp.float32),
+        in_specs=[hbm] * 5,
+        out_specs=vmem,
         scratch_shapes=[
             pltpu.SMEM((angle_count,), jnp.int32),
             pltpu.SMEM((angle_count, slot_count), jnp.int32),
             pltpu.SMEM((angle_count, length), jnp.int32),
             pltpu.VMEM((lines, half_width), jnp.float32),
             pltpu.VMEM(tile_table.shape, jnp.bfloat16),
-            pltpu.VMEM((own_angles, row_total, local_cols), jnp.float32),
-            pltpu.VMEM((own_angles, row_total, local_cols), jnp.float32),
             pltpu.VMEM((lines * runs, tile_size), jnp.float32),
             pltpu.VMEM((buffers * length, tile_size), jnp.float32),
-            pltpu.SemaphoreType.DMA((7,)),
+            pltpu.SemaphoreType.DMA((5,)),
         ],
         compiler_params=params,
         name="forward",
-    )(
-        held(live), held(tid), held(bid), vol, held(tile_table),
-        held(measured.transpose(0, 2, 1)), held(row_norm.transpose(0, 2, 1)),
-    )
+    )(held(live), held(tid), held(bid), vol, held(tile_table))
 
     assert lax.axis_size("row") == 2
     upper = lax.axis_index("row") == 1
@@ -283,19 +319,18 @@
     blocks = total.reshape(angle_count, rows, tile_size)
     outer = jnp.where(upper, blocks[:, rows - rim :], blocks[:, :rim])
     middle = blocks[:, rim : rows - rim]
+    columns = columns[None]
     for bit in bits("gx"):
-        came = swap_many([outer, middle], "gx", bit)
+        came = swap_many([outer, middle, columns], "gx", bit)
         outer, middle = outer + came[0], middle + came[1]
+        columns = ordered((lax.axis_index("gx") & bit) != 0, columns, came[2], 0)
     last = slab_count - 1
     hops = [((z + 1) * 2, z * 2) for z in range(last)]
     hops += [(z * 2 + 1, z * 2 + 3) for z in range(last)]
     rims = lax.ppermute(outer.reshape(angle_count * rim, tile_size), ("gz", "row"), hops)
     outer = outer.reshape(rims.shape)
 
-    columns = to_slabs(sends, {1: total, 2: outer})[None]
-    for bit in bits("gx"):
-        came = swap(columns, "gx", bit)
-        columns = ordered((lax.axis_index("gx") & bit) != 0, columns, came, 0)
+    columns = exchange_slabs(columns.transpose(1, 2, 0, 3, 4, 5), 1)[0].transpose(1, 0, 2, 3, 4)
     other_outer, other_rims, other_columns = swap_many([outer, rims, columns], "row", 1)
     own_rim = outer + other_rims
     far_rim = other_outer + rims
@@ -318,6 +353,7 @@
             pltpu.VMEM((lines, half_width), jnp.float32),
             pltpu.VMEM((lines, half_width), jnp.float32),
             pltpu.VMEM((lines, half_width), jnp.float32),
+            pltpu.VMEM((high, lines // high * half_width), jnp.float32),
             pltpu.SemaphoreType.DMA((2 + lines // high,)),
         ],
         compiler_params=params,

time: 31.2 us -> 29.3 us (0.939)
  the two profiles are of different devices: /device:TPU:2 before, /device:TPU:0 now
where the time goes in v4:
time: 29.3 us; the launch traced here: 29 us
  Pallas kernels  10.3 us (35%)
  waiting for transfers between devices  9.32 us (32%)
  starting transfers between devices  8.69 us (30%)
    ppermute x5, starting transfers between devices, swap(): lax.ppermute(values, axis, [(i, i ^ bit) for i in range(lax.axis_size(axi...  7.41 us
    ppermute x5, waiting for transfers between devices, swap(): lax.ppermute(values, axis, [(i, i ^ bit) for i in range(lax.axis_size(axi...  6.14 us
    pallas_call x1, Pallas kernels, on_device(): pl.pallas_call(functools.partial(forward_kernel, rows), out_shape=jax.Sha...  4.99 us
    pallas_call x1, Pallas kernels, on_device(): pl.pallas_call(functools.partial(backward_kernel, rows), out_shape=jax.Sh...  4.6 us
    ppermute x1, waiting for transfers between devices, on_device(): lax.ppermute(outer.reshape(angle_count * rim, tile_size), ('gz', 'row'),...  3.18 us
    ppermute x1, starting transfers between devices, on_device(): lax.ppermute(outer.reshape(angle_count * rim, tile_size), ('gz', 'row'),...  1.28 us
    pallas_call x1, Pallas kernels, on_device(): pl.pallas_call(functools.partial(pack_kernel, window), out_shape=jax.Shap...  0.73 us
  transfers between devices with their start and end apart: 6, of which 5 were waited for; matrix products, arithmetic and copies ran while one was open for 0% of the time, Pallas kernels for 17%

profile of v4, /device:TPU:0, one launch (start us, length us, event | category | flops | bytes accessed | tf_op | source)
XLA Modules:
  0.0 29.0 jit_solution(14952660697533207889)
XLA Ops:
  0.0 0.7 %pack.1 = f32[4,1,12,128]{3,2,1,0:T(8,128)S(1)} custom-call(f32[1,16,128]{2,1,0:T(8,128)} %bitcast.121, f32[1,16,128]{2,1,0:T(8,128)} %bitcast.122), custom_call_target="tpu_custom_call" | custom-call | tf_op jit(solution)/shard_map/pack/pallas_call | solution.py:278
  0.8 4.1 %collective-permute-start.1 = (f32[2,1,1,12,128]{4,3,0,2,1:T(8,128)S(1)}, f32[2,1,1,12,128]{4,3,0,2,1:T(8,128)S(1)}, u32[]{:S(2)}, u32[]{:S(2)}) collective-permute-start(f32[2,1,1,12,128]{4,3,0,2,1:T(8,128)S(1)} %fusion.8), channel_id=1, source_target_pairs={{0,8},{4,12},{8,0},{12,4},{1,9},{5,13},{9,1},{13,5},{2,10},{6,14},... | collective-permute-start | bytes 36872 | tf_op jit(solution)/shard_map/ppermute | solution.py:210
  4.9 5.0 %forward.1 = f32[96,128]{1,0:T(8,128)S(1)} custom-call(s32[4]{0:T(128)} %bitcast.111, s32[4,32]{1,0:T(4,128)} %bitcast.109, s32[4,768]{1,0:T(4,128)} %bitcast.107, f32[1024,256]{1,0:T(8,128)} %bitcast.113, bf16[64,128,128]{2,1,0:T(8,128)(2,1)} %tiles.1), custom_call_target="tpu_custom_call" | custom-call | tf_op jit(solution)/shard_map/forward/pallas_call | solution.py:297
  9.9 0.0 copy-start
  9.9 0.0 copy-start.1
  9.9 0.0 copy-start.2
  9.9 0.0 copy-start.3
  9.9 0.1 collective-permute-start
  10.0 0.0 collective-permute-done.1
  10.1 1.1 %collective-permute-done = f32[96,128]{1,0:T(8,128)S(1)} collective-permute-done((f32[96,128]{1,0:T(8,128)S(1)}, f32[96,128]{1,0:T(8,128)S(1)}, u32[]{:S(2)}, u32[]{:S(2)}) %collective-permute-start) | collective-permute-done | bytes 49184 | tf_op jit(solution)/shard_map/ppermute | solution.py:210
  11.3 1.6 %collective-permute-start.2 = (f32[112,128]{1,0:T(8,128)S(1)}, f32[112,128]{1,0:T(8,128)S(1)}, u32[]{:S(2)}, u32[]{:S(2)}) collective-permute-start(f32[112,128]{1,0:T(8,128)S(1)} %pad_maximum_fusion.3), channel_id=1, source_target_pairs={{0,2},{2,0},{1,3},{3,1},{4,6},{6,4},{5,7},{7,5},{8,10},{10,8},{9,1... | collective-permute-start | bytes 172040 | tf_op jit(solution)/shard_map/ppermute | solution.py:210
  12.8 2.7 %collective-permute-done.2 = f32[112,128]{1,0:T(8,128)S(1)} collective-permute-done((f32[112,128]{1,0:T(8,128)S(1)}, f32[112,128]{1,0:T(8,128)S(1)}, u32[]{:S(2)}, u32[]{:S(2)}) %collective-permute-start.2) | collective-permute-done | bytes 57376 | tf_op jit(solution)/shard_map/ppermute | solution.py:210
  15.6 1.6 %collective-permute-start.4 = (f32[1,2,2,1,12,128]{5,4,1,2,3,0:T(8,128)S(1)}, f32[1,2,2,1,12,128]{5,4,1,2,3,0:T(8,128)S(1)}, u32[]{:S(2)}, u32[]{:S(2)}) collective-permute-start(f32[1,2,2,1,12,128]{5,4,1,2,3,0:T(8,128)S(1)} %bitcast_select_fusion.2), channel_id=1, source_target_pairs={{0,4},{4,0},{8,12},{12,8},{1,5},{5,1},{9,13},{13,9},{2,6},{6,2},{1... | collective-permute-start | bytes 73736 | tf_op jit(solution)/shard_map/ppermute | solution.py:210
  17.2 1.3 %collective-permute-start.3 = (f32[32,128]{1,0:T(8,128)S(1)}, f32[32,128]{1,0:T(8,128)S(1)}, u32[]{:S(2)}, u32[]{:S(2)}) collective-permute-start(f32[32,128]{1,0:T(8,128)S(1)} %get-tuple-element.10), channel_id=1, source_target_pairs={{4,0},{8,4},{12,8},{1,5},{5,9},{9,13},{6,2},{10,6},{14,10},{3,7},{... | collective-permute-start | bytes 49160 | tf_op jit(solution)/shard_map/ppermute | solution.py:330
  18.5 1.0 %collective-permute-done.4 = f32[1,2,2,1,12,128]{5,4,1,2,3,0:T(8,128)S(1)} collective-permute-done((f32[1,2,2,1,12,128]{5,4,1,2,3,0:T(8,128)S(1)}, f32[1,2,2,1,12,128]{5,4,1,2,3,0:T(8,128)S(1)}, u32[]{:S(2)}, u32[]{:S(2)}) %collective-permute-start.4) | collective-permute-done | bytes 24608 | tf_op jit(solution)/shard_map/ppermute | solution.py:210
  19.7 3.2 %collective-permute-done.3 = f32[32,128]{1,0:T(8,128)S(1)} collective-permute-done((f32[32,128]{1,0:T(8,128)S(1)}, f32[32,128]{1,0:T(8,128)S(1)}, u32[]{:S(2)}, u32[]{:S(2)}) %collective-permute-start.3) | collective-permute-done | bytes 16416 | tf_op jit(solution)/shard_map/ppermute | solution.py:330
  22.8 0.0 collective-permute-start.5
  22.8 1.3 %collective-permute-done.5 = f32[160,128]{1,0:T(8,128)S(1)} collective-permute-done((f32[160,128]{1,0:T(8,128)S(1)}, f32[160,128]{1,0:T(8,128)S(1)}, u32[]{:S(2)}, u32[]{:S(2)}) %collective-permute-start.5) | collective-permute-done | bytes 81952 | tf_op jit(solution)/shard_map/ppermute | solution.py:210
  24.1 0.1 broadcast_select_fusion.1
  24.4 0.0 copy-done
  24.4 0.0 copy-done.1
  24.4 0.0 copy-done.2
  24.4 0.0 copy-done.3
  24.4 4.6 %backward.1 = f32[1024,256]{1,0:T(8,128)} custom-call(s32[4]{0:T(128)S(1)} %bitcast.112, s32[4,32]{1,0:T(4,128)S(1)} %bitcast.110, s32[4,768]{1,0:T(4,128)S(1)} %bitcast.108, f32[32,128]{1,0:T(8,128)S(1)} %get-tuple-element.8.head, f32[32,128]{1,0:T(8,128)S(1)} %get-tuple-element.9.middle, f32[32,128]{1,0:T(8,128)S(1)} %get-tuple-element.7.tail, ...), custom_call_target="tpu_custom_call" | custom-call | tf_op jit(solution)/shard_map/backward/pallas_call | solution.py:343
  (29 shorter events, 0.3 us)
Async XLA Ops:
  0.8 9.3 %collective-permute-start.1 = (f32[2,1,1,12,128]{4,3,0,2,1:T(8,128)S(1)}, f32[2,1,1,12,128]{4,3,0,2,1:T(8,128)S(1)}, u32[]{:S(2)}, u32[]{:S(2)}) collective-permute-start(f32[2,1,1,12,128]{4,3,0,2,1:T(8,128)S(1)} %fusion.8), channel_id=1, source_target_pairs={{0,8},{4,12},{8,0},{12,4},{1,9},{5,13},{9,1},{13,5},{2,10},{6,14},... | collective-permute-start | bytes 36872 | tf_op jit(solution)/shard_map/ppermute | solution.py:210
  9.9 14.5 %copy-start = (bf16[64,128,128]{2,1,0:T(8,128)(2,1)S(1)}, bf16[64,128,128]{2,1,0:T(8,128)(2,1)}, u32[]{:S(2)}) copy-start(bf16[64,128,128]{2,1,0:T(8,128)(2,1)} %tiles.1) | copy-start | bytes 6291460
  9.9 14.5 %copy-start.1 = (s32[1,1,1,4,768]{4,3,2,1,0:T(4,128)S(1)}, s32[1,1,1,4,768]{4,3,2,1,0:T(4,128)}, u32[]{:S(2)}) copy-start(s32[1,1,1,4,768]{4,3,2,1,0:T(4,128)} %param.11) | copy-start | bytes 36868
  9.9 14.5 %copy-start.2 = (s32[1,1,1,4,32]{4,3,2,1,0:T(4,128)S(1)}, s32[1,1,1,4,32]{4,3,2,1,0:T(4,128)}, u32[]{:S(2)}) copy-start(s32[1,1,1,4,32]{4,3,2,1,0:T(4,128)} %param.10) | copy-start | bytes 1540
  9.9 14.5 %copy-start.3 = (s32[1,1,1,4]{3,2,1,0:T(1,128)S(1)}, s32[1,1,1,4]{3,2,1,0:T(1,128)}, u32[]{:S(2)}) copy-start(s32[1,1,1,4]{3,2,1,0:T(1,128)} %param.12) | copy-start | bytes 52
  9.9 1.3 %collective-permute-start = (f32[96,128]{1,0:T(8,128)S(1)}, f32[96,128]{1,0:T(8,128)S(1)}, u32[]{:S(2)}, u32[]{:S(2)}) collective-permute-start(f32[96,128]{1,0:T(8,128)S(1)} %forward.1), channel_id=1, source_target_pairs={{0,1},{1,0},{2,3},{3,2},{4,5},{5,4},{6,7},{7,6},{8,9},{9,8},{10,11... | collective-permute-start | bytes 147464 | tf_op jit(solution)/shard_map/ppermute | solution.py:210
  11.3 4.2 %collective-permute-start.2 = (f32[112,128]{1,0:T(8,128)S(1)}, f32[112,128]{1,0:T(8,128)S(1)}, u32[]{:S(2)}, u32[]{:S(2)}) collective-permute-start(f32[112,128]{1,0:T(8,128)S(1)} %pad_maximum_fusion.3), channel_id=1, source_target_pairs={{0,2},{2,0},{1,3},{3,1},{4,6},{6,4},{5,7},{7,5},{8,10},{10,8},{9,1... | collective-permute-start | bytes 172040 | tf_op jit(solution)/shard_map/ppermute | solution.py:210
  15.6 4.0 %collective-permute-start.4 = (f32[1,2,2,1,12,128]{5,4,1,2,3,0:T(8,128)S(1)}, f32[1,2,2,1,12,128]{5,4,1,2,3,0:T(8,128)S(1)}, u32[]{:S(2)}, u32[]{:S(2)}) collective-permute-start(f32[1,2,2,1,12,128]{5,4,1,2,3,0:T(8,128)S(1)} %bitcast_select_fusion.2), channel_id=1, source_target_pairs={{0,4},{4,0},{8,12},{12,8},{1,5},{5,1},{9,13},{13,9},{2,6},{6,2},{1... | collective-permute-start | bytes 73736 | tf_op jit(solution)/shard_map/ppermute | solution.py:210
  17.2 5.6 %collective-permute-start.3 = (f32[32,128]{1,0:T(8,128)S(1)}, f32[32,128]{1,0:T(8,128)S(1)}, u32[]{:S(2)}, u32[]{:S(2)}) collective-permute-start(f32[32,128]{1,0:T(8,128)S(1)} %get-tuple-element.10), channel_id=1, source_target_pairs={{4,0},{8,4},{12,8},{1,5},{5,9},{9,13},{6,2},{10,6},{14,10},{3,7},{... | collective-permute-start | bytes 49160 | tf_op jit(solution)/shard_map/ppermute | solution.py:330
  22.8 1.3 %collective-permute-start.5 = (f32[160,128]{1,0:T(8,128)S(1)}, f32[160,128]{1,0:T(8,128)S(1)}, u32[]{:S(2)}, u32[]{:S(2)}) collective-permute-start(f32[160,128]{1,0:T(8,128)S(1)} %pad_maximum_fusion.1), channel_id=1, source_target_pairs={{0,1},{1,0},{2,3},{3,2},{4,5},{5,4},{6,7},{7,6},{8,9},{9,8},{10,11... | collective-permute-start | bytes 245768 | tf_op jit(solution)/shard_map/ppermute | solution.py:210

commit v5 on v4

--- a/solution.py
+++ b/solution.py
@@ -101,8 +101,8 @@
 
 
 def backward_kernel(
-    rows, live, tid, bid, head, middle, tail, target, weight, tiles, vol_in, col_in, out_in,
-    res, hot, code, spread, vol, col, out, total, sems,
+    rows, joined, live, tid, bid, head, middle, tail, columns, tiles, vol_in, col_in, out_in,
+    target, weight, res, hot, code, spread, vol, col, out, total, sems,
 ):
     angles, slots = tid.shape
     tile = tiles.shape[1]
@@ -116,6 +116,18 @@
     ]
     for copy in reads:
         copy.start()
+    if joined:
+        count = columns.shape[0]
+        window = rows // count
+        for q in range(count):
+            for a in range(angles):
+                there = pl.ds(a * rows + q, window, stride=count)
+                at = a * 2 * window
+                target[there, :] = columns[q, at : at + window, :]
+                weight[there, :] = columns[q, at + window : at + 2 * window, :]
+    else:
+        target[...] = columns[0]
+        weight[...] = columns[1]
     for a in range(angles):
         parts = []
         for part in (head, middle, tail):
@@ -210,11 +222,12 @@
     return lax.ppermute(values, axis, [(i, i ^ bit) for i in range(lax.axis_size(axis))])
 
 
-def swap_many(arrays, axis, bit):
+def move_many(arrays, axis, hops):
     if len({array.shape[-1] for array in arrays}) > 1:
-        return [swap(array, axis, bit) for array in arrays]
+        return [lax.ppermute(array, axis, hops) for array in arrays]
     width = arrays[0].shape[-1]
-    came = swap(jnp.concatenate([a.reshape(-1, width) for a in arrays], axis=0), axis, bit)
+    joined = jnp.concatenate([a.reshape(-1, width) for a in arrays], axis=0)
+    came = lax.ppermute(joined, axis, hops)
     out, at = [], 0
     for array in arrays:
         count = array.size // width
@@ -223,6 +236,10 @@
     return out
 
 
+def swap_many(arrays, axis, bit):
+    return move_many(arrays, axis, [(i, i ^ bit) for i in range(lax.axis_size(axis))])
+
+
 def bits(axis):
     return [1 << i for i in range((lax.axis_size(axis) - 1).bit_length())]
 
@@ -239,7 +256,8 @@
     halves = parts.reshape((2, count) + parts.shape[1:])
     keep = jnp.where(high, halves[1], halves[0])
     give = jnp.where(high, halves[0], halves[1])
-    came = swap(give, "gz", bit)
+    with jax.named_scope(f"slab{bit}"):
+        came = swap(give, "gz", bit)
     low, up = jnp.where(high, came, keep), jnp.where(high, keep, came)
     both = jnp.stack([low, up], axis=2)
     return both.reshape((count, parts.shape[1] * 2) + parts.shape[2:])
@@ -315,37 +333,51 @@
 
     assert lax.axis_size("row") == 2
     upper = lax.axis_index("row") == 1
-    total = partial + swap(partial, "row", 1)
+    odd = (lax.axis_index("gz") & 1) == 1
+    faces = upper != odd
+    keep = jnp.where(odd, columns[1], columns[0])
+    give = jnp.where(odd, columns[0], columns[1])
+    columns = jnp.where(faces, give, keep)
+    with jax.named_scope("rowsum"):
+        came = swap_many([partial, jnp.where(faces, keep, give)], "row", 1)
+    total = partial + came[0]
+    columns = ordered(upper, columns[None], came[1][None], 0)[None]
     blocks = total.reshape(angle_count, rows, tile_size)
     outer = jnp.where(upper, blocks[:, rows - rim :], blocks[:, :rim])
     middle = blocks[:, rim : rows - rim]
-    columns = columns[None]
     for bit in bits("gx"):
-        came = swap_many([outer, middle, columns], "gx", bit)
+        with jax.named_scope(f"gxsum{bit}"):
+            came = swap_many([outer, middle, columns], "gx", bit)
         outer, middle = outer + came[0], middle + came[1]
         columns = ordered((lax.axis_index("gx") & bit) != 0, columns, came[2], 0)
     last = slab_count - 1
     hops = [((z + 1) * 2, z * 2) for z in range(last)]
     hops += [(z * 2 + 1, z * 2 + 3) for z in range(last)]
-    rims = lax.ppermute(outer.reshape(angle_count * rim, tile_size), ("gz", "row"), hops)
-    outer = outer.reshape(rims.shape)
-
-    columns = exchange_slabs(columns.transpose(1, 2, 0, 3, 4, 5), 1)[0].transpose(1, 0, 2, 3, 4)
-    other_outer, other_rims, other_columns = swap_many([outer, rims, columns], "row", 1)
-    own_rim = outer + other_rims
-    far_rim = other_outer + rims
-    head = jnp.where(upper, far_rim, own_rim)
-    tail = jnp.where(upper, own_rim, far_rim)
-    columns = ordered(upper, columns[:, None], other_columns[:, None], 1)
-    columns = columns.reshape(-1, angle_count, 2, window, local_cols)
-    columns = columns.transpose(2, 1, 3, 0, 4).reshape(2, angle_count * rows, tile_size)
+    with jax.named_scope("rims"):
+        rims, came = move_many([outer, columns], ("gz", "row"), hops)
+    columns = jnp.stack([jnp.where(odd, came, columns), jnp.where(odd, columns, came)], axis=3)
+    with jax.named_scope("finish"):
+        came = swap_many([outer, rims, columns], "row", 1)
+    own_rim = outer + came[1]
+    far_rim = came[0] + rims
+    head = jnp.where(upper, far_rim, own_rim).reshape(-1, tile_size)
+    tail = jnp.where(upper, own_rim, far_rim).reshape(-1, tile_size)
+    columns = jnp.where(faces, came[2], columns)
+    joined = local_cols == tile_size
+    if joined:
+        columns = columns.reshape(block_cols, angle_count * 2 * window, tile_size)
+    else:
+        columns = columns.reshape(-1, angle_count, 2, window, local_cols)
+        columns = columns.transpose(2, 1, 3, 0, 4).reshape(2, angle_count * rows, tile_size)
 
     made = pl.pallas_call(
-        functools.partial(backward_kernel, rows),
+        functools.partial(backward_kernel, rows, joined),
         out_shape=jax.ShapeDtypeStruct((lines, half_width), jnp.float32),
-        in_specs=[smem, smem] + [vmem] * 7 + [hbm] * 2,
+        in_specs=[smem, smem] + [vmem] * 6 + [hbm] * 2,
         out_specs=hbm,
         scratch_shapes=[
+            pltpu.VMEM((angle_count * rows, tile_size), jnp.float32),
+            pltpu.VMEM((angle_count * rows, tile_size), jnp.float32),
             pltpu.VMEM((angle_count, rows, tile_size), jnp.bfloat16),
             pltpu.VMEM((high, angle_count * length), jnp.bfloat16),
             pltpu.VMEM((angle_count * length, tile_size), jnp.bfloat16),
@@ -359,8 +391,7 @@
         compiler_params=params,
         name="backward",
     )(
-        live, tid, bid, head, middle.reshape(-1, tile_size), tail, columns[0], columns[1],
-        tile_table, vol, col,
+        live, tid, bid, head, middle.reshape(-1, tile_size), tail, columns, tile_table, vol, col,
     )
     return made.reshape(slab_depth, column_width, half_width)
 

time: 29.3 us -> 28.4 us (0.969)
  starting transfers between devices: 8.69 us -> 7.13 us
  waiting for transfers between devices: 9.32 us -> 10 us
    ppermute x1 -> x4, waiting for transfers between devices: 3.18 us -> 10 us  [move_many(): came = lax.ppermute(joined, axis, hops)]
    ppermute x5 -> x1, waiting for transfers between devices: 6.14 us -> 0.01 us  [swap(): lax.ppermute(values, axis, [(i, i ^ bit) for i in range(lax.axis_size(axi...]
    ppermute x5 -> x1, starting transfers between devices: 7.41 us -> 4.13 us  [swap(): lax.ppermute(values, axis, [(i, i ^ bit) for i in range(lax.axis_size(axi...]
    ppermute x1 -> x4, starting transfers between devices: 1.28 us -> 3 us  [move_many(): came = lax.ppermute(joined, axis, hops)]
  transfers between devices with their start and end apart: 6 -> 5, of which waited for: 5 -> 4; matrix products, arithmetic and copies ran while one was open for 0% -> 0% of each run, Pallas kernels for 17% -> 18%
where the time goes in v5:
time: 28.4 us; the launch traced here: 28.1 us
  Pallas kernels  10.3 us (36%)
  waiting for transfers between devices  10 us (35%)
  starting transfers between devices  7.13 us (25%)
  between operations  0.31 us (1%)
    ppermute x4, waiting for transfers between devices, move_many(): came = lax.ppermute(joined, axis, hops)  10 us
    pallas_call x1, Pallas kernels, on_device(): pl.pallas_call(functools.partial(forward_kernel, rows), out_shape=jax.Sha...  4.99 us
    pallas_call x1, Pallas kernels, on_device(): pl.pallas_call(functools.partial(backward_kernel, rows, joined), out_shap...  4.62 us
    ppermute x1, starting transfers between devices, swap(): lax.ppermute(values, axis, [(i, i ^ bit) for i in range(lax.axis_size(axi...  4.13 us
    ppermute x4, starting transfers between devices, move_many(): came = lax.ppermute(joined, axis, hops)  3 us
    pallas_call x1, Pallas kernels, on_device(): pl.pallas_call(functools.partial(pack_kernel, window), out_shape=jax.Shap...  0.73 us
  transfers between devices with their start and end apart: 5, of which 4 were waited for; matrix products, arithmetic and copies ran while one was open for 0% of the time, Pallas kernels for 18%

profile of v5, /device:TPU:0, one launch (start us, length us, event | category | flops | bytes accessed | tf_op | source)
XLA Modules:
  0.0 28.1 jit_solution(8959534270353607965)
XLA Ops:
  0.0 0.7 %pack.1 = f32[4,1,12,128]{3,2,1,0:T(8,128)S(1)} custom-call(f32[1,16,128]{2,1,0:T(8,128)} %bitcast.128, f32[1,16,128]{2,1,0:T(8,128)} %bitcast.129), custom_call_target="tpu_custom_call" | custom-call | tf_op jit(solution)/shard_map/pack/pallas_call | solution.py:296
  0.8 4.1 %collective-permute-start = (f32[2,1,1,12,128]{4,3,0,2,1:T(8,128)S(1)}, f32[2,1,1,12,128]{4,3,0,2,1:T(8,128)S(1)}, u32[]{:S(2)}, u32[]{:S(2)}) collective-permute-start(f32[2,1,1,12,128]{4,3,0,2,1:T(8,128)S(1)} %fusion.10), channel_id=1, source_target_pairs={{0,8},{4,12},{8,0},{12,4},{1,9},{5,13},{9,1},{13,5},{2,10},{6,14},... | collective-permute-start | bytes 36872 | tf_op jit(solution)/shard_map/slab2/ppermute | solution.py:222
  4.9 5.0 %forward.1 = f32[96,128]{1,0:T(8,128)S(1)} custom-call(s32[4]{0:T(128)} %bitcast.118, s32[4,32]{1,0:T(4,128)} %bitcast.116, s32[4,768]{1,0:T(4,128)} %bitcast.114, f32[1024,256]{1,0:T(8,128)} %bitcast.120, bf16[64,128,128]{2,1,0:T(8,128)(2,1)} %tiles.1), custom_call_target="tpu_custom_call" | custom-call | tf_op jit(solution)/shard_map/forward/pallas_call | solution.py:315
  9.9 0.0 collective-permute-done
  9.9 0.0 copy-start
  9.9 0.0 copy-start.1
  9.9 0.0 copy-start.2
  9.9 0.0 copy-start.3
  10.0 0.1 collective-permute-start.1
  10.1 1.2 %collective-permute-done.1 = f32[120,128]{1,0:T(8,128)S(1)} collective-permute-done((f32[120,128]{1,0:T(8,128)S(1)}, f32[120,128]{1,0:T(8,128)S(1)}, u32[]{:S(2)}, u32[]{:S(2)}) %collective-permute-start.1) | collective-permute-done | bytes 61472 | tf_op jit(solution)/shard_map/rowsum/ppermute | solution.py:230
  11.4 1.6 %collective-permute-start.2 = (f32[112,128]{1,0:T(8,128)S(1)}, f32[112,128]{1,0:T(8,128)S(1)}, u32[]{:S(2)}, u32[]{:S(2)}) collective-permute-start(f32[112,128]{1,0:T(8,128)S(1)} %pad_maximum_fusion.6), channel_id=1, source_target_pairs={{0,2},{2,0},{1,3},{3,1},{4,6},{6,4},{5,7},{7,5},{8,10},{10,8},{9,1... | collective-permute-start | bytes 172040 | tf_op jit(solution)/shard_map/gxsum1/ppermute | solution.py:230
  13.0 2.7 %collective-permute-done.2 = f32[112,128]{1,0:T(8,128)S(1)} collective-permute-done((f32[112,128]{1,0:T(8,128)S(1)}, f32[112,128]{1,0:T(8,128)S(1)}, u32[]{:S(2)}, u32[]{:S(2)}) %collective-permute-start.2) | collective-permute-done | bytes 57376 | tf_op jit(solution)/shard_map/gxsum1/ppermute | solution.py:230
  15.7 1.3 %collective-permute-start.3 = (f32[128,128]{1,0:T(8,128)S(1)}, f32[128,128]{1,0:T(8,128)S(1)}, u32[]{:S(2)}, u32[]{:S(2)}) collective-permute-start(f32[128,128]{1,0:T(8,128)S(1)} %pad_maximum_fusion.3), channel_id=1, source_target_pairs={{4,0},{8,4},{12,8},{1,5},{5,9},{9,13},{6,2},{10,6},{14,10},{3,7},{... | collective-permute-start | bytes 196616 | tf_op jit(solution)/shard_map/rims/ppermute | solution.py:230
  17.1 4.8 %collective-permute-done.3 = f32[128,128]{1,0:T(8,128)S(1)} collective-permute-done((f32[128,128]{1,0:T(8,128)S(1)}, f32[128,128]{1,0:T(8,128)S(1)}, u32[]{:S(2)}, u32[]{:S(2)}) %collective-permute-start.3) | collective-permute-done | bytes 65568 | tf_op jit(solution)/shard_map/rims/ppermute | solution.py:230
  22.0 0.1 collective-permute-start.4
  22.1 0.1 copy.21
  22.2 1.2 %collective-permute-done.4 = f32[256,128]{1,0:T(8,128)S(1)} collective-permute-done((f32[256,128]{1,0:T(8,128)S(1)}, f32[256,128]{1,0:T(8,128)S(1)}, u32[]{:S(2)}, u32[]{:S(2)}) %collective-permute-start.4) | collective-permute-done | bytes 131104 | tf_op jit(solution)/shard_map/finish/ppermute | solution.py:230
  23.5 0.0 copy-done
  23.5 0.0 copy-done.1
  23.5 0.0 copy-done.2
  23.5 0.0 copy-done.3
  23.5 4.6 %backward.1 = f32[1024,256]{1,0:T(8,128)} custom-call(s32[4]{0:T(128)S(1)} %bitcast.119, s32[4,32]{1,0:T(4,128)S(1)} %bitcast.117, s32[4,768]{1,0:T(4,128)S(1)} %bitcast.115, f32[32,128]{1,0:T(8,128)S(1)} %get-tuple-element.9.head, f32[32,128]{1,0:T(8,128)S(1)} %get-tuple-element.18.middle, f32[32,128]{1,0:T(8,128)S(1)} %get-tuple-element.8.tail, ...), custom_call_target="tpu_custom_call" | custom-call | tf_op jit(solution)/shard_map/backward/pallas_call | solution.py:373
  (33 shorter events, 0.2 us)
Async XLA Ops:
  0.8 9.1 %collective-permute-start = (f32[2,1,1,12,128]{4,3,0,2,1:T(8,128)S(1)}, f32[2,1,1,12,128]{4,3,0,2,1:T(8,128)S(1)}, u32[]{:S(2)}, u32[]{:S(2)}) collective-permute-start(f32[2,1,1,12,128]{4,3,0,2,1:T(8,128)S(1)} %fusion.10), channel_id=1, source_target_pairs={{0,8},{4,12},{8,0},{12,4},{1,9},{5,13},{9,1},{13,5},{2,10},{6,14},... | collective-permute-start | bytes 36872 | tf_op jit(solution)/shard_map/slab2/ppermute | solution.py:222
  9.9 13.6 %copy-start = (bf16[64,128,128]{2,1,0:T(8,128)(2,1)S(1)}, bf16[64,128,128]{2,1,0:T(8,128)(2,1)}, u32[]{:S(2)}) copy-start(bf16[64,128,128]{2,1,0:T(8,128)(2,1)} %tiles.1) | copy-start | bytes 6291460
  9.9 13.6 %copy-start.1 = (s32[1,1,1,4,768]{4,3,2,1,0:T(4,128)S(1)}, s32[1,1,1,4,768]{4,3,2,1,0:T(4,128)}, u32[]{:S(2)}) copy-start(s32[1,1,1,4,768]{4,3,2,1,0:T(4,128)} %param.11) | copy-start | bytes 36868
  9.9 13.6 %copy-start.2 = (s32[1,1,1,4,32]{4,3,2,1,0:T(4,128)S(1)}, s32[1,1,1,4,32]{4,3,2,1,0:T(4,128)}, u32[]{:S(2)}) copy-start(s32[1,1,1,4,32]{4,3,2,1,0:T(4,128)} %param.10) | copy-start | bytes 1540
  9.9 13.6 %copy-start.3 = (s32[1,1,1,4]{3,2,1,0:T(1,128)S(1)}, s32[1,1,1,4]{3,2,1,0:T(1,128)}, u32[]{:S(2)}) copy-start(s32[1,1,1,4]{3,2,1,0:T(1,128)} %param.12) | copy-start | bytes 52
  10.0 1.3 %collective-permute-start.1 = (f32[120,128]{1,0:T(8,128)S(1)}, f32[120,128]{1,0:T(8,128)S(1)}, u32[]{:S(2)}, u32[]{:S(2)}) collective-permute-start(f32[120,128]{1,0:T(8,128)S(1)} %pad_maximum_fusion.5), channel_id=1, source_target_pairs={{0,1},{1,0},{2,3},{3,2},{4,5},{5,4},{6,7},{7,6},{8,9},{9,8},{10,11... | collective-permute-start | bytes 184328 | tf_op jit(solution)/shard_map/rowsum/ppermute | solution.py:230
  11.4 4.2 %collective-permute-start.2 = (f32[112,128]{1,0:T(8,128)S(1)}, f32[112,128]{1,0:T(8,128)S(1)}, u32[]{:S(2)}, u32[]{:S(2)}) collective-permute-start(f32[112,128]{1,0:T(8,128)S(1)} %pad_maximum_fusion.6), channel_id=1, source_target_pairs={{0,2},{2,0},{1,3},{3,1},{4,6},{6,4},{5,7},{7,5},{8,10},{10,8},{9,1... | collective-permute-start | bytes 172040 | tf_op jit(solution)/shard_map/gxsum1/ppermute | solution.py:230
  15.7 6.2 %collective-permute-start.3 = (f32[128,128]{1,0:T(8,128)S(1)}, f32[128,128]{1,0:T(8,128)S(1)}, u32[]{:S(2)}, u32[]{:S(2)}) collective-permute-start(f32[128,128]{1,0:T(8,128)S(1)} %pad_maximum_fusion.3), channel_id=1, source_target_pairs={{4,0},{8,4},{12,8},{1,5},{5,9},{9,13},{6,2},{10,6},{14,10},{3,7},{... | collective-permute-start | bytes 196616 | tf_op jit(solution)/shard_map/rims/ppermute | solution.py:230
  22.0 1.4 %collective-permute-start.4 = (f32[256,128]{1,0:T(8,128)S(1)}, f32[256,128]{1,0:T(8,128)S(1)}, u32[]{:S(2)}, u32[]{:S(2)}) collective-permute-start(f32[256,128]{1,0:T(8,128)S(1)} %pad_maximum_fusion.1), channel_id=1, source_target_pairs={{0,1},{1,0},{2,3},{3,2},{4,5},{5,4},{6,7},{7,6},{8,9},{9,8},{10,11... | collective-permute-start | bytes 393224 | tf_op jit(solution)/shard_map/finish/ppermute | solution.py:230

commit v6 on v5

--- a/solution.py
+++ b/solution.py
@@ -139,6 +139,8 @@
 
     place = lax.broadcasted_iota(jnp.int32, (high, tile), 0).astype(jnp.bfloat16)
     position = lax.broadcasted_iota(jnp.int32, (1, tile), 1)
+    static = angles * length <= STATIC_ROWS
+    codes = []
     for a in range(angles):
         groups = []
         for c in range(0, length, tile):
@@ -155,27 +157,27 @@
         turned = jnp.concatenate(groups, axis=0).astype(jnp.float32).T
         for i in range(length // tile):
             wide = jnp.broadcast_to(turned[:, i : i + 1], (tile, tile))
-            code[a * length + i * tile : a * length + (i + 1) * tile, :] = wide.astype(
-                jnp.bfloat16
-            )
-
-    def spread_pair(values, a, k, at):
+            if static:
+                codes.append(wide.astype(jnp.bfloat16))
+            else:
+                here = slice(a * length + i * tile, a * length + (i + 1) * tile)
+                code[here, :] = wide.astype(jnp.bfloat16)
+
+    def spread_pair(values, a, k):
         pair = jnp.concatenate([tiles[tid[a, k]], tiles[tid[a, k + 1]]], axis=1)
         made = jnp.dot(values, pair, preferred_element_type=jnp.float32)
         both = jnp.concatenate([made[:, :tile], made[:, tile:]], axis=0)
-        spread[pl.ds(at, 2 * rows), :] = both.astype(jnp.bfloat16)
-
-    def add_part(at, size, first, count):
-        values = spread[pl.ds(at, size), :]
-        groups = code[pl.ds(at, size), :]
+        return both.astype(jnp.bfloat16)
+
+    def add_part(values, groups, chosen):
         right = jnp.concatenate(
             [
                 jnp.where(groups == jnp.bfloat16(g), values, jnp.bfloat16(0))
-                for g in range(first * runs, (first + count) * runs)
+                for g in range(chunks * runs)
             ],
             axis=1,
         )
-        return jnp.dot(hot[:, pl.ds(at, size)], right, preferred_element_type=jnp.float32)
+        return jnp.dot(chosen, right, preferred_element_type=jnp.float32)
 
     chunks = lines // high
     writes = []
@@ -190,12 +192,14 @@
             copy.start()
             writes.append(copy)
 
-    if angles * length <= STATIC_ROWS:
+    if static:
+        values = []
         for a in range(angles):
-            values = res[a]
             for k in range(0, slots, 2):
-                spread_pair(values, a, k, (a * slots + k) * rows)
-        made = add_part(0, angles * length, 0, chunks)
+                values.append(spread_pair(res[a], a, k))
+        made = add_part(
+            jnp.concatenate(values, axis=0), jnp.concatenate(codes, axis=0), hot[...]
+        )
         for copy in reads:
             copy.wait()
         finish(0, chunks, made)
@@ -205,8 +209,10 @@
             values = res[a]
             base = pl.multiple_of(a * length, 256)
             for k in range(0, slots, 2):
-                spread_pair(values, a, k, base + k * rows)
-            total[...] += add_part(base, length, 0, chunks)
+                spread[k * rows : (k + 2) * rows, :] = spread_pair(values, a, k)
+            total[...] += add_part(
+                spread[...], code[pl.ds(base, length), :], hot[:, pl.ds(base, length)]
+            )
             return carry
 
         total[...] = jnp.zeros_like(total)
@@ -334,35 +340,34 @@
     assert lax.axis_size("row") == 2
     upper = lax.axis_index("row") == 1
     odd = (lax.axis_index("gz") & 1) == 1
-    faces = upper != odd
+    top = upper != odd
     keep = jnp.where(odd, columns[1], columns[0])
     give = jnp.where(odd, columns[0], columns[1])
-    columns = jnp.where(faces, give, keep)
+    columns = jnp.where(upper, give, keep)
     with jax.named_scope("rowsum"):
-        came = swap_many([partial, jnp.where(faces, keep, give)], "row", 1)
+        came = swap_many([partial, jnp.where(upper, keep, give)], "row", 1)
     total = partial + came[0]
     columns = ordered(upper, columns[None], came[1][None], 0)[None]
     blocks = total.reshape(angle_count, rows, tile_size)
-    outer = jnp.where(upper, blocks[:, rows - rim :], blocks[:, :rim])
+    outer = jnp.where(top, blocks[:, rows - rim :], blocks[:, :rim])
     middle = blocks[:, rim : rows - rim]
     for bit in bits("gx"):
         with jax.named_scope(f"gxsum{bit}"):
             came = swap_many([outer, middle, columns], "gx", bit)
         outer, middle = outer + came[0], middle + came[1]
         columns = ordered((lax.axis_index("gx") & bit) != 0, columns, came[2], 0)
-    last = slab_count - 1
-    hops = [((z + 1) * 2, z * 2) for z in range(last)]
-    hops += [(z * 2 + 1, z * 2 + 3) for z in range(last)]
+    hops = [(z * 2 + 1, (z ^ 1) * 2 + 1) for z in range(slab_count)]
+    hops += [(z * 2, ((z + 1 ^ 1) - 1) * 2) for z in range(1, slab_count - 1)]
     with jax.named_scope("rims"):
-        rims, came = move_many([outer, columns], ("gz", "row"), hops)
-    columns = jnp.stack([jnp.where(odd, came, columns), jnp.where(odd, columns, came)], axis=3)
+        came = move_many([outer, columns], ("gz", "row"), hops)
+    outer = outer + came[0]
+    columns = jnp.where(upper, came[1], columns)
     with jax.named_scope("finish"):
-        came = swap_many([outer, rims, columns], "row", 1)
-    own_rim = outer + came[1]
-    far_rim = came[0] + rims
-    head = jnp.where(upper, far_rim, own_rim).reshape(-1, tile_size)
-    tail = jnp.where(upper, own_rim, far_rim).reshape(-1, tile_size)
-    columns = jnp.where(faces, came[2], columns)
+        came = swap_many([outer, columns], "row", 1)
+    head = jnp.where(top, came[0], outer).reshape(-1, tile_size)
+    tail = jnp.where(top, outer, came[0]).reshape(-1, tile_size)
+    low, up = jnp.where(top, came[1], columns), jnp.where(top, columns, came[1])
+    columns = jnp.stack([low, up], axis=3)
     joined = local_cols == tile_size
     if joined:
         columns = columns.reshape(block_cols, angle_count * 2 * window, tile_size)
@@ -381,7 +386,7 @@
             pltpu.VMEM((angle_count, rows, tile_size), jnp.bfloat16),
             pltpu.VMEM((high, angle_count * length), jnp.bfloat16),
             pltpu.VMEM((angle_count * length, tile_size), jnp.bfloat16),
-            pltpu.VMEM((angle_count * length, tile_size), jnp.bfloat16),
+            pltpu.VMEM((length, tile_size), jnp.bfloat16),
             pltpu.VMEM((lines, half_width), jnp.float32),
             pltpu.VMEM((lines, half_width), jnp.float32),
             pltpu.VMEM((lines, half_width), jnp.float32),

time: 28.4 us -> 26.8 us (0.944)
  the two profiles are of different devices: /device:TPU:0 before, /device:TPU:9 now
where the time goes in v6:
time: 26.8 us; the launch traced here: 26.6 us
  Pallas kernels  9.97 us (37%)
  starting transfers between devices  9.47 us (35%)
  waiting for transfers between devices  6.49 us (24%)
  between operations  0.28 us (1%)
    ppermute x4, starting transfers between devices, move_many(): came = lax.ppermute(joined, axis, hops)  7.1 us
    ppermute x4, waiting for transfers between devices, move_many(): came = lax.ppermute(joined, axis, hops)  6.49 us
    pallas_call x1, Pallas kernels, on_device(): pl.pallas_call(functools.partial(forward_kernel, rows), out_shape=jax.Sha...  5 us
    pallas_call x1, Pallas kernels, on_device(): pl.pallas_call(functools.partial(backward_kernel, rows, joined), out_shap...  4.24 us
    ppermute x1, starting transfers between devices, swap(): lax.ppermute(values, axis, [(i, i ^ bit) for i in range(lax.axis_size(axi...  2.37 us
    pallas_call x1, Pallas kernels, on_device(): pl.pallas_call(functools.partial(pack_kernel, window), out_shape=jax.Shap...  0.73 us
  transfers between devices with their start and end apart: 5, of which 4 were waited for; matrix products, arithmetic and copies ran while one was open for 0% of the time, Pallas kernels for 19%

profile of v6, /device:TPU:9, one launch (start us, length us, event | category | flops | bytes accessed | tf_op | source)
XLA Modules:
  0.0 26.6 jit_solution(16885333225677342880)
XLA Ops:
  0.0 0.7 %pack.1 = f32[4,1,12,128]{3,2,1,0:T(8,128)S(1)} custom-call(f32[1,16,128]{2,1,0:T(8,128)} %bitcast.124, f32[1,16,128]{2,1,0:T(8,128)} %bitcast.125), custom_call_target="tpu_custom_call" | custom-call | tf_op jit(solution)/shard_map/pack/pallas_call | solution.py:302
  0.8 2.4 %collective-permute-start = (f32[2,1,1,12,128]{4,3,0,2,1:T(8,128)S(1)}, f32[2,1,1,12,128]{4,3,0,2,1:T(8,128)S(1)}, u32[]{:S(2)}, u32[]{:S(2)}) collective-permute-start(f32[2,1,1,12,128]{4,3,0,2,1:T(8,128)S(1)} %fusion.9), channel_id=1, source_target_pairs={{0,8},{4,12},{8,0},{12,4},{1,9},{5,13},{9,1},{13,5},{2,10},{6,14},... | collective-permute-start | bytes 36872 | tf_op jit(solution)/shard_map/slab2/ppermute | solution.py:228
  3.1 5.0 %forward.1 = f32[96,128]{1,0:T(8,128)S(1)} custom-call(s32[4]{0:T(128)} %bitcast.114, s32[4,32]{1,0:T(4,128)} %bitcast.112, s32[4,768]{1,0:T(4,128)} %bitcast.110, f32[1024,256]{1,0:T(8,128)} %bitcast.116, bf16[64,128,128]{2,1,0:T(8,128)(2,1)} %tiles.1), custom_call_target="tpu_custom_call" | custom-call | tf_op jit(solution)/shard_map/forward/pallas_call | solution.py:321
  8.1 0.0 copy-start
  8.1 0.0 copy-start.1
  8.2 0.0 copy-start.2
  8.2 0.0 copy-start.3
  8.2 0.0 collective-permute-done
  8.3 1.0 %collective-permute-start.1 = (f32[120,128]{1,0:T(8,128)S(1)}, f32[120,128]{1,0:T(8,128)S(1)}, u32[]{:S(2)}, u32[]{:S(2)}) collective-permute-start(f32[120,128]{1,0:T(8,128)S(1)} %pad_maximum_fusion.4), channel_id=1, source_target_pairs={{0,1},{1,0},{2,3},{3,2},{4,5},{5,4},{6,7},{7,6},{8,9},{9,8},{10,11... | collective-permute-start | bytes 184328 | tf_op jit(solution)/shard_map/rowsum/ppermute | solution.py:236
  9.3 0.9 %collective-permute-done.1 = f32[120,128]{1,0:T(8,128)S(1)} collective-permute-done((f32[120,128]{1,0:T(8,128)S(1)}, f32[120,128]{1,0:T(8,128)S(1)}, u32[]{:S(2)}, u32[]{:S(2)}) %collective-permute-start.1) | collective-permute-done | bytes 61472 | tf_op jit(solution)/shard_map/rowsum/ppermute | solution.py:236
  10.3 1.3 %collective-permute-start.2 = (f32[112,128]{1,0:T(8,128)S(1)}, f32[112,128]{1,0:T(8,128)S(1)}, u32[]{:S(2)}, u32[]{:S(2)}) collective-permute-start(f32[112,128]{1,0:T(8,128)S(1)} %pad_maximum_fusion.5), channel_id=1, source_target_pairs={{0,2},{2,0},{1,3},{3,1},{4,6},{6,4},{5,7},{7,5},{8,10},{10,8},{9,1... | collective-permute-start | bytes 172040 | tf_op jit(solution)/shard_map/gxsum1/ppermute | solution.py:236
  11.5 1.8 %collective-permute-done.2 = f32[112,128]{1,0:T(8,128)S(1)} collective-permute-done((f32[112,128]{1,0:T(8,128)S(1)}, f32[112,128]{1,0:T(8,128)S(1)}, u32[]{:S(2)}, u32[]{:S(2)}) %collective-permute-start.2) | collective-permute-done | bytes 57376 | tf_op jit(solution)/shard_map/gxsum1/ppermute | solution.py:236
  13.4 2.1 %collective-permute-start.3 = (f32[128,128]{1,0:T(8,128)S(1)}, f32[128,128]{1,0:T(8,128)S(1)}, u32[]{:S(2)}, u32[]{:S(2)}) collective-permute-start(f32[128,128]{1,0:T(8,128)S(1)} %pad_maximum_fusion.2), channel_id=1, source_target_pairs={{1,5},{5,1},{9,13},{13,9},{4,8},{8,4},{3,7},{7,3},{11,15},{15,11},... | collective-permute-start | bytes 196616 | tf_op jit(solution)/shard_map/rims/ppermute | solution.py:236
  15.5 2.9 %collective-permute-done.3 = f32[128,128]{1,0:T(8,128)S(1)} collective-permute-done((f32[128,128]{1,0:T(8,128)S(1)}, f32[128,128]{1,0:T(8,128)S(1)}, u32[]{:S(2)}, u32[]{:S(2)}) %collective-permute-start.3) | collective-permute-done | bytes 65568 | tf_op jit(solution)/shard_map/rims/ppermute | solution.py:236
  18.5 2.7 %collective-permute-start.4 = (f32[128,128]{1,0:T(8,128)S(1)}, f32[128,128]{1,0:T(8,128)S(1)}, u32[]{:S(2)}, u32[]{:S(2)}) collective-permute-start(f32[128,128]{1,0:T(8,128)S(1)} %pad_maximum_fusion.3), channel_id=1, source_target_pairs={{0,1},{1,0},{2,3},{3,2},{4,5},{5,4},{6,7},{7,6},{8,9},{9,8},{10,11... | collective-permute-start | bytes 196616 | tf_op jit(solution)/shard_map/finish/ppermute | solution.py:236
  21.2 0.9 %collective-permute-done.4 = f32[128,128]{1,0:T(8,128)S(1)} collective-permute-done((f32[128,128]{1,0:T(8,128)S(1)}, f32[128,128]{1,0:T(8,128)S(1)}, u32[]{:S(2)}, u32[]{:S(2)}) %collective-permute-start.4) | collective-permute-done | bytes 65568 | tf_op jit(solution)/shard_map/finish/ppermute | solution.py:236
  22.2 0.1 copy.21
  22.3 0.0 copy-done
  22.3 0.0 copy-done.1
  22.3 0.0 copy-done.2
  22.3 0.0 copy-done.3
  22.3 4.2 %backward.1 = f32[1024,256]{1,0:T(8,128)} custom-call(s32[4]{0:T(128)S(1)} %bitcast.115, s32[4,32]{1,0:T(4,128)S(1)} %bitcast.113, s32[4,768]{1,0:T(4,128)S(1)} %bitcast.111, f32[32,128]{1,0:T(8,128)S(1)} %get-tuple-element.11.head, f32[32,128]{1,0:T(8,128)S(1)} %get-tuple-element.20.middle, f32[32,128]{1,0:T(8,128)S(1)} %get-tuple-element.10.tail, ...), custom_call_target="tpu_custom_call" | custom-call | tf_op jit(solution)/shard_map/backward/pallas_call | solution.py:378
  (32 shorter events, 0.2 us)
Async XLA Ops:
  0.8 7.4 %collective-permute-start = (f32[2,1,1,12,128]{4,3,0,2,1:T(8,128)S(1)}, f32[2,1,1,12,128]{4,3,0,2,1:T(8,128)S(1)}, u32[]{:S(2)}, u32[]{:S(2)}) collective-permute-start(f32[2,1,1,12,128]{4,3,0,2,1:T(8,128)S(1)} %fusion.9), channel_id=1, source_target_pairs={{0,8},{4,12},{8,0},{12,4},{1,9},{5,13},{9,1},{13,5},{2,10},{6,14},... | collective-permute-start | bytes 36872 | tf_op jit(solution)/shard_map/slab2/ppermute | solution.py:228
  8.1 14.1 %copy-start = (bf16[64,128,128]{2,1,0:T(8,128)(2,1)S(1)}, bf16[64,128,128]{2,1,0:T(8,128)(2,1)}, u32[]{:S(2)}) copy-start(bf16[64,128,128]{2,1,0:T(8,128)(2,1)} %tiles.1) | copy-start | bytes 6291460
  8.1 14.1 %copy-start.1 = (s32[1,1,1,4,768]{4,3,2,1,0:T(4,128)S(1)}, s32[1,1,1,4,768]{4,3,2,1,0:T(4,128)}, u32[]{:S(2)}) copy-start(s32[1,1,1,4,768]{4,3,2,1,0:T(4,128)} %param.11) | copy-start | bytes 36868
  8.2 14.1 %copy-start.2 = (s32[1,1,1,4,32]{4,3,2,1,0:T(4,128)S(1)}, s32[1,1,1,4,32]{4,3,2,1,0:T(4,128)}, u32[]{:S(2)}) copy-start(s32[1,1,1,4,32]{4,3,2,1,0:T(4,128)} %param.10) | copy-start | bytes 1540
  8.2 14.1 %copy-start.3 = (s32[1,1,1,4]{3,2,1,0:T(1,128)S(1)}, s32[1,1,1,4]{3,2,1,0:T(1,128)}, u32[]{:S(2)}) copy-start(s32[1,1,1,4]{3,2,1,0:T(1,128)} %param.12) | copy-start | bytes 52
  8.3 1.9 %collective-permute-start.1 = (f32[120,128]{1,0:T(8,128)S(1)}, f32[120,128]{1,0:T(8,128)S(1)}, u32[]{:S(2)}, u32[]{:S(2)}) collective-permute-start(f32[120,128]{1,0:T(8,128)S(1)} %pad_maximum_fusion.4), channel_id=1, source_target_pairs={{0,1},{1,0},{2,3},{3,2},{4,5},{5,4},{6,7},{7,6},{8,9},{9,8},{10,11... | collective-permute-start | bytes 184328 | tf_op jit(solution)/shard_map/rowsum/ppermute | solution.py:236
  10.3 3.1 %collective-permute-start.2 = (f32[112,128]{1,0:T(8,128)S(1)}, f32[112,128]{1,0:T(8,128)S(1)}, u32[]{:S(2)}, u32[]{:S(2)}) collective-permute-start(f32[112,128]{1,0:T(8,128)S(1)} %pad_maximum_fusion.5), channel_id=1, source_target_pairs={{0,2},{2,0},{1,3},{3,1},{4,6},{6,4},{5,7},{7,5},{8,10},{10,8},{9,1... | collective-permute-start | bytes 172040 | tf_op jit(solution)/shard_map/gxsum1/ppermute | solution.py:236
  13.4 5.0 %collective-permute-start.3 = (f32[128,128]{1,0:T(8,128)S(1)}, f32[128,128]{1,0:T(8,128)S(1)}, u32[]{:S(2)}, u32[]{:S(2)}) collective-permute-start(f32[128,128]{1,0:T(8,128)S(1)} %pad_maximum_fusion.2), channel_id=1, source_target_pairs={{1,5},{5,1},{9,13},{13,9},{4,8},{8,4},{3,7},{7,3},{11,15},{15,11},... | collective-permute-start | bytes 196616 | tf_op jit(solution)/shard_map/rims/ppermute | solution.py:236
  18.5 3.6 %collective-permute-start.4 = (f32[128,128]{1,0:T(8,128)S(1)}, f32[128,128]{1,0:T(8,128)S(1)}, u32[]{:S(2)}, u32[]{:S(2)}) collective-permute-start(f32[128,128]{1,0:T(8,128)S(1)} %pad_maximum_fusion.3), channel_id=1, source_target_pairs={{0,1},{1,0},{2,3},{3,2},{4,5},{5,4},{6,7},{7,6},{8,9},{9,8},{10,11... | collective-permute-start | bytes 196616 | tf_op jit(solution)/shard_map/finish/ppermute | solution.py:236

commit v7 on v6

--- a/solution.py
+++ b/solution.py
@@ -14,14 +14,14 @@
 VMEM_LIMIT = 16 * 1024 * 1024
 
 
-def pack_kernel(window, target_in, weight_in, sends, target, weight, sems):
+def pack_kernel(window, target_in, weight_in, sends, target, weight, made, sems):
     copies = [
         pltpu.make_async_copy(target_in, target, sems.at[0]),
         pltpu.make_async_copy(weight_in, weight, sems.at[1]),
     ]
     for copy in copies:
         copy.start()
-    sends[...] = jnp.zeros_like(sends)
+    made[...] = jnp.zeros_like(made)
     for copy in copies:
         copy.wait()
     slabs = sends.shape[0]
@@ -30,8 +30,9 @@
         low, high = max(s * depth - 1, 0), min(s * depth + depth + 1, slabs * depth)
         skip = low - (s * depth - 1)
         for own in range(target.shape[0]):
-            for at, data in ((0, target), (window, weight)):
-                sends[s, own, at + skip : at + skip + high - low, :] = data[own, low:high, :]
+            for at, data in ((0, target), (made.shape[2] // 2, weight)):
+                made[s, own, at + skip : at + skip + high - low, :] = data[own, low:high, :]
+    sends[...] = made[...].astype(sends.dtype)
 
 
 def forward_kernel(
@@ -119,15 +120,17 @@
     if joined:
         count = columns.shape[0]
         window = rows // count
+        padded = columns.shape[1] // angles // 2
         for q in range(count):
             for a in range(angles):
                 there = pl.ds(a * rows + q, window, stride=count)
-                at = a * 2 * window
-                target[there, :] = columns[q, at : at + window, :]
-                weight[there, :] = columns[q, at + window : at + 2 * window, :]
+                at = a * 2 * padded
+                both = columns[q, at : at + 2 * padded, :].astype(jnp.float32)
+                target[there, :] = both[:window]
+                weight[there, :] = both[padded : padded + window]
     else:
-        target[...] = columns[0]
-        weight[...] = columns[1]
+        target[...] = columns[0].astype(jnp.float32)
+        weight[...] = columns[1].astype(jnp.float32)
     for a in range(angles):
         parts = []
         for part in (head, middle, tail):
@@ -277,6 +280,7 @@
     block_cols = block_ids.shape[4] // (slot_count * window)
     rows = window * block_cols
     rim = 2 * block_cols
+    padded = -(-window // 8) * 8
     length = slot_count * rows
     lines = slab_depth * column_width
     runs = half_width // tile_size
@@ -302,13 +306,14 @@
     sends = pl.pallas_call(
         functools.partial(pack_kernel, window),
         out_shape=jax.ShapeDtypeStruct(
-            (slab_count, own_angles, 2 * window, local_cols), jnp.float32
+            (slab_count, own_angles, 2 * padded, local_cols), jnp.bfloat16
         ),
         in_specs=[hbm] * 2,
         out_specs=vmem,
         scratch_shapes=[
             pltpu.VMEM((own_angles, row_total, local_cols), jnp.float32),
             pltpu.VMEM((own_angles, row_total, local_cols), jnp.float32),
+            pltpu.VMEM((slab_count, own_angles, 2 * padded, local_cols), jnp.float32),
             pltpu.SemaphoreType.DMA((2,)),
         ],
         compiler_params=params,
@@ -345,34 +350,38 @@
     give = jnp.where(odd, columns[0], columns[1])
     columns = jnp.where(upper, give, keep)
     with jax.named_scope("rowsum"):
-        came = swap_many([partial, jnp.where(upper, keep, give)], "row", 1)
+        passed = jnp.where(upper, keep, give).astype(jnp.float32)
+        came = swap_many([partial, passed], "row", 1)
     total = partial + came[0]
-    columns = ordered(upper, columns[None], came[1][None], 0)[None]
+    columns = ordered(upper, columns[None], came[1][None].astype(jnp.bfloat16), 0)[None]
     blocks = total.reshape(angle_count, rows, tile_size)
     outer = jnp.where(top, blocks[:, rows - rim :], blocks[:, :rim])
     middle = blocks[:, rim : rows - rim]
     for bit in bits("gx"):
         with jax.named_scope(f"gxsum{bit}"):
-            came = swap_many([outer, middle, columns], "gx", bit)
-        outer, middle = outer + came[0], middle + came[1]
+            parts = [outer.astype(jnp.bfloat16), middle.astype(jnp.bfloat16), columns]
+            came = swap_many(parts, "gx", bit)
+        outer = outer + came[0].astype(jnp.float32)
+        middle = middle + came[1].astype(jnp.float32)
         columns = ordered((lax.axis_index("gx") & bit) != 0, columns, came[2], 0)
     hops = [(z * 2 + 1, (z ^ 1) * 2 + 1) for z in range(slab_count)]
     hops += [(z * 2, ((z + 1 ^ 1) - 1) * 2) for z in range(1, slab_count - 1)]
     with jax.named_scope("rims"):
-        came = move_many([outer, columns], ("gz", "row"), hops)
-    outer = outer + came[0]
+        came = move_many([outer.astype(jnp.bfloat16), columns], ("gz", "row"), hops)
+    outer = outer + came[0].astype(jnp.float32)
     columns = jnp.where(upper, came[1], columns)
     with jax.named_scope("finish"):
-        came = swap_many([outer, columns], "row", 1)
-    head = jnp.where(top, came[0], outer).reshape(-1, tile_size)
-    tail = jnp.where(top, outer, came[0]).reshape(-1, tile_size)
+        came = swap_many([outer.astype(jnp.bfloat16), columns], "row", 1)
+    far = came[0].astype(jnp.float32)
+    head = jnp.where(top, far, outer).reshape(-1, tile_size)
+    tail = jnp.where(top, outer, far).reshape(-1, tile_size)
     low, up = jnp.where(top, came[1], columns), jnp.where(top, columns, came[1])
     columns = jnp.stack([low, up], axis=3)
     joined = local_cols == tile_size
     if joined:
-        columns = columns.reshape(block_cols, angle_count * 2 * window, tile_size)
+        columns = columns.reshape(block_cols, angle_count * 2 * padded, tile_size)
     else:
-        columns = columns.reshape(-1, angle_count, 2, window, local_cols)
+        columns = columns.reshape(-1, angle_count, 2, padded, local_cols)[:, :, :, :window]
         columns = columns.transpose(2, 1, 3, 0, 4).reshape(2, angle_count * rows, tile_size)
 
     made = pl.pallas_call(

time: 26.8 us -> 26.2 us (0.978)
  waiting for transfers between devices: 6.49 us -> 5.98 us
    ppermute x4, waiting for transfers between devices: 6.49 us -> 5.98 us  [move_many(): came = lax.ppermute(joined, axis, hops)]
  transfers between devices with their start and end apart: 5 -> 5, of which waited for: 4 -> 4; matrix products, arithmetic and copies ran while one was open for 0% -> 0% of each run, Pallas kernels for 19% -> 20%
where the time goes in v7:
time: 26.2 us; the launch traced here: 26 us
  Pallas kernels  10.1 us (39%)
  starting transfers between devices  9.47 us (36%)
  waiting for transfers between devices  5.98 us (23%)
    ppermute x4, starting transfers between devices, move_many(): came = lax.ppermute(joined, axis, hops)  7.09 us
    ppermute x4, waiting for transfers between devices, move_many(): came = lax.ppermute(joined, axis, hops)  5.98 us
    pallas_call x1, Pallas kernels, on_device(): pl.pallas_call(functools.partial(forward_kernel, rows), out_shape=jax.Sha...  5.13 us
    pallas_call x1, Pallas kernels, on_device(): pl.pallas_call(functools.partial(backward_kernel, rows, joined), out_shap...  4.24 us
    ppermute x1, starting transfers between devices, swap(): lax.ppermute(values, axis, [(i, i ^ bit) for i in range(lax.axis_size(axi...  2.37 us
    pallas_call x1, Pallas kernels, on_device(): pl.pallas_call(functools.partial(pack_kernel, window), out_shape=jax.Shap...  0.74 us
  transfers between devices with their start and end apart: 5, of which 4 were waited for; matrix products, arithmetic and copies ran while one was open for 0% of the time, Pallas kernels for 20%

profile of v7, /device:TPU:9, one launch (start us, length us, event | category | flops | bytes accessed | tf_op | source)
XLA Modules:
  0.0 26.0 jit_solution(16457220619795567586)
XLA Ops:
  0.0 0.7 %pack.1 = bf16[4,1,16,128]{3,2,1,0:T(8,128)(2,1)S(1)} custom-call(f32[1,16,128]{2,1,0:T(8,128)} %bitcast.141, f32[1,16,128]{2,1,0:T(8,128)} %bitcast.142), custom_call_target="tpu_custom_call" | custom-call | tf_op jit(solution)/shard_map/pack/pallas_call | solution.py:306
  0.8 2.4 %collective-permute-start = (bf16[2,1,1,16,128]{4,3,0,2,1:T(8,128)(2,1)S(1)}, bf16[2,1,1,16,128]{4,3,0,2,1:T(8,128)(2,1)S(1)}, u32[]{:S(2)}, u32[]{:S(2)}) collective-permute-start(bf16[2,1,1,16,128]{4,3,0,2,1:T(8,128)(2,1)S(1)} %fusion.10), channel_id=1, source_target_pairs={{0,8},{4,12},{8,0},{12,4},{1,9},{5,13},{9,1},{13,5},{2,10},{6,14},... | collective-permute-start | bytes 24584 | tf_op jit(solution)/shard_map/slab2/ppermute | solution.py:231
  3.1 0.0 copy-start
  3.1 0.0 copy-start.1
  3.1 0.0 copy-start.2
  3.1 0.0 copy-start.3
  3.1 5.1 %forward.1 = f32[96,128]{1,0:T(8,128)S(1)} custom-call(s32[4]{0:T(128)} %bitcast.126, s32[4,32]{1,0:T(4,128)} %bitcast.124, s32[4,768]{1,0:T(4,128)} %bitcast.122, f32[1024,256]{1,0:T(8,128)} %bitcast.128, bf16[64,128,128]{2,1,0:T(8,128)(2,1)} %tiles.1), custom_call_target="tpu_custom_call" | custom-call | tf_op jit(solution)/shard_map/forward/pallas_call | solution.py:326
  8.3 0.0 collective-permute-done
  8.4 1.0 %collective-permute-start.1 = (f32[128,128]{1,0:T(8,128)S(1)}, f32[128,128]{1,0:T(8,128)S(1)}, u32[]{:S(2)}, u32[]{:S(2)}) collective-permute-start(f32[128,128]{1,0:T(8,128)S(1)} %pad_maximum_fusion), channel_id=1, source_target_pairs={{0,1},{1,0},{2,3},{3,2},{4,5},{5,4},{6,7},{7,6},{8,9},{9,8},{10,11... | collective-permute-start | bytes 196616 | tf_op jit(solution)/shard_map/rowsum/ppermute | solution.py:239
  9.4 0.9 %collective-permute-done.1 = f32[128,128]{1,0:T(8,128)S(1)} collective-permute-done((f32[128,128]{1,0:T(8,128)S(1)}, f32[128,128]{1,0:T(8,128)S(1)}, u32[]{:S(2)}, u32[]{:S(2)}) %collective-permute-start.1) | collective-permute-done | bytes 65568 | tf_op jit(solution)/shard_map/rowsum/ppermute | solution.py:239
  10.4 1.3 %collective-permute-start.2 = (bf16[128,128]{1,0:T(8,128)(2,1)S(1)}, bf16[128,128]{1,0:T(8,128)(2,1)S(1)}, u32[]{:S(2)}, u32[]{:S(2)}) collective-permute-start(bf16[128,128]{1,0:T(8,128)(2,1)S(1)} %pad_maximum_fusion.4), channel_id=1, source_target_pairs={{0,2},{2,0},{1,3},{3,1},{4,6},{6,4},{5,7},{7,5},{8,10},{10,8},{9,1... | collective-permute-start | bytes 98312 | tf_op jit(solution)/shard_map/gxsum1/ppermute | solution.py:239
  11.6 1.6 %collective-permute-done.2 = bf16[128,128]{1,0:T(8,128)(2,1)S(1)} collective-permute-done((bf16[128,128]{1,0:T(8,128)(2,1)S(1)}, bf16[128,128]{1,0:T(8,128)(2,1)S(1)}, u32[]{:S(2)}, u32[]{:S(2)}) %collective-permute-start.2) | collective-permute-done | bytes 32800 | tf_op jit(solution)/shard_map/gxsum1/ppermute | solution.py:239
  13.3 2.1 %collective-permute-start.3 = (bf16[160,128]{1,0:T(8,128)(2,1)S(1)}, bf16[160,128]{1,0:T(8,128)(2,1)S(1)}, u32[]{:S(2)}, u32[]{:S(2)}) collective-permute-start(bf16[160,128]{1,0:T(8,128)(2,1)S(1)} %pad_maximum_fusion.2), channel_id=1, source_target_pairs={{1,5},{5,1},{9,13},{13,9},{4,8},{8,4},{3,7},{7,3},{11,15},{15,11},... | collective-permute-start | bytes 122888 | tf_op jit(solution)/shard_map/rims/ppermute | solution.py:239
  15.3 2.7 %collective-permute-done.3 = bf16[160,128]{1,0:T(8,128)(2,1)S(1)} collective-permute-done((bf16[160,128]{1,0:T(8,128)(2,1)S(1)}, bf16[160,128]{1,0:T(8,128)(2,1)S(1)}, u32[]{:S(2)}, u32[]{:S(2)}) %collective-permute-start.3) | collective-permute-done | bytes 40992 | tf_op jit(solution)/shard_map/rims/ppermute | solution.py:239
  18.0 2.7 %collective-permute-start.4 = (bf16[160,128]{1,0:T(8,128)(2,1)S(1)}, bf16[160,128]{1,0:T(8,128)(2,1)S(1)}, u32[]{:S(2)}, u32[]{:S(2)}) collective-permute-start(bf16[160,128]{1,0:T(8,128)(2,1)S(1)} %pad_maximum_fusion.3), channel_id=1, source_target_pairs={{0,1},{1,0},{2,3},{3,2},{4,5},{5,4},{6,7},{7,6},{8,9},{9,8},{10,11... | collective-permute-start | bytes 122888 | tf_op jit(solution)/shard_map/finish/ppermute | solution.py:239
  20.8 0.9 %collective-permute-done.4 = bf16[160,128]{1,0:T(8,128)(2,1)S(1)} collective-permute-done((bf16[160,128]{1,0:T(8,128)(2,1)S(1)}, bf16[160,128]{1,0:T(8,128)(2,1)S(1)}, u32[]{:S(2)}, u32[]{:S(2)}) %collective-permute-start.4) | collective-permute-done | bytes 40992 | tf_op jit(solution)/shard_map/finish/ppermute | solution.py:239
  21.7 0.0 copy-done
  21.7 0.0 copy-done.1
  21.7 0.0 copy-done.2
  21.7 0.0 copy-done.3
  21.7 4.2 %backward.1 = f32[1024,256]{1,0:T(8,128)} custom-call(s32[4]{0:T(128)S(1)} %bitcast.127, s32[4,32]{1,0:T(4,128)S(1)} %bitcast.125, s32[4,768]{1,0:T(4,128)S(1)} %bitcast.123, f32[32,128]{1,0:T(8,128)S(1)} %get-tuple-element.11.head, f32[32,128]{1,0:T(8,128)S(1)} %get-tuple-element.20.middle, f32[32,128]{1,0:T(8,128)S(1)} %get-tuple-element.10.tail, ...), custom_call_target="tpu_custom_call" | custom-call | tf_op jit(solution)/shard_map/backward/pallas_call | solution.py:387
  (26 shorter events, 0.2 us)
Async XLA Ops:
  0.8 7.5 %collective-permute-start = (bf16[2,1,1,16,128]{4,3,0,2,1:T(8,128)(2,1)S(1)}, bf16[2,1,1,16,128]{4,3,0,2,1:T(8,128)(2,1)S(1)}, u32[]{:S(2)}, u32[]{:S(2)}) collective-permute-start(bf16[2,1,1,16,128]{4,3,0,2,1:T(8,128)(2,1)S(1)} %fusion.10), channel_id=1, source_target_pairs={{0,8},{4,12},{8,0},{12,4},{1,9},{5,13},{9,1},{13,5},{2,10},{6,14},... | collective-permute-start | bytes 24584 | tf_op jit(solution)/shard_map/slab2/ppermute | solution.py:231
  3.1 18.6 %copy-start = (bf16[64,128,128]{2,1,0:T(8,128)(2,1)S(1)}, bf16[64,128,128]{2,1,0:T(8,128)(2,1)}, u32[]{:S(2)}) copy-start(bf16[64,128,128]{2,1,0:T(8,128)(2,1)} %tiles.1) | copy-start | bytes 6291460
  3.1 18.6 %copy-start.1 = (s32[1,1,1,4,768]{4,3,2,1,0:T(4,128)S(1)}, s32[1,1,1,4,768]{4,3,2,1,0:T(4,128)}, u32[]{:S(2)}) copy-start(s32[1,1,1,4,768]{4,3,2,1,0:T(4,128)} %param.11) | copy-start | bytes 36868
  3.1 18.6 %copy-start.2 = (s32[1,1,1,4,32]{4,3,2,1,0:T(4,128)S(1)}, s32[1,1,1,4,32]{4,3,2,1,0:T(4,128)}, u32[]{:S(2)}) copy-start(s32[1,1,1,4,32]{4,3,2,1,0:T(4,128)} %param.10) | copy-start | bytes 1540
  3.1 18.6 %copy-start.3 = (s32[1,1,1,4]{3,2,1,0:T(1,128)S(1)}, s32[1,1,1,4]{3,2,1,0:T(1,128)}, u32[]{:S(2)}) copy-start(s32[1,1,1,4]{3,2,1,0:T(1,128)} %param.12) | copy-start | bytes 52
  8.4 1.9 %collective-permute-start.1 = (f32[128,128]{1,0:T(8,128)S(1)}, f32[128,128]{1,0:T(8,128)S(1)}, u32[]{:S(2)}, u32[]{:S(2)}) collective-permute-start(f32[128,128]{1,0:T(8,128)S(1)} %pad_maximum_fusion), channel_id=1, source_target_pairs={{0,1},{1,0},{2,3},{3,2},{4,5},{5,4},{6,7},{7,6},{8,9},{9,8},{10,11... | collective-permute-start | bytes 196616 | tf_op jit(solution)/shard_map/rowsum/ppermute | solution.py:239
  10.4 2.8 %collective-permute-start.2 = (bf16[128,128]{1,0:T(8,128)(2,1)S(1)}, bf16[128,128]{1,0:T(8,128)(2,1)S(1)}, u32[]{:S(2)}, u32[]{:S(2)}) collective-permute-start(bf16[128,128]{1,0:T(8,128)(2,1)S(1)} %pad_maximum_fusion.4), channel_id=1, source_target_pairs={{0,2},{2,0},{1,3},{3,1},{4,6},{6,4},{5,7},{7,5},{8,10},{10,8},{9,1... | collective-permute-start | bytes 98312 | tf_op jit(solution)/shard_map/gxsum1/ppermute | solution.py:239
  13.3 4.7 %collective-permute-start.3 = (bf16[160,128]{1,0:T(8,128)(2,1)S(1)}, bf16[160,128]{1,0:T(8,128)(2,1)S(1)}, u32[]{:S(2)}, u32[]{:S(2)}) collective-permute-start(bf16[160,128]{1,0:T(8,128)(2,1)S(1)} %pad_maximum_fusion.2), channel_id=1, source_target_pairs={{1,5},{5,1},{9,13},{13,9},{4,8},{8,4},{3,7},{7,3},{11,15},{15,11},... | collective-permute-start | bytes 122888 | tf_op jit(solution)/shard_map/rims/ppermute | solution.py:239
  18.0 3.6 %collective-permute-start.4 = (bf16[160,128]{1,0:T(8,128)(2,1)S(1)}, bf16[160,128]{1,0:T(8,128)(2,1)S(1)}, u32[]{:S(2)}, u32[]{:S(2)}) collective-permute-start(bf16[160,128]{1,0:T(8,128)(2,1)S(1)} %pad_maximum_fusion.3), channel_id=1, source_target_pairs={{0,1},{1,0},{2,3},{3,2},{4,5},{5,4},{6,7},{7,6},{8,9},{9,8},{10,11... | collective-permute-start | bytes 122888 | tf_op jit(solution)/shard_map/finish/ppermute | solution.py:239

commit v8 on v7

--- a/solution.py
+++ b/solution.py
@@ -14,15 +14,15 @@
 VMEM_LIMIT = 16 * 1024 * 1024
 
 
-def pack_kernel(window, target_in, weight_in, sends, target, weight, made, sems):
-    copies = [
-        pltpu.make_async_copy(target_in, target, sems.at[0]),
-        pltpu.make_async_copy(weight_in, weight, sems.at[1]),
-    ]
+def pack_kernel(
+    window, target_in, weight_in, bid_in, vol_in, sends, bid, vox, target, weight, made, vol, sems
+):
+    pairs = ((vol_in, vol), (target_in, target), (weight_in, weight), (bid_in, bid))
+    copies = [pltpu.make_async_copy(a, b, sems.at[i]) for i, (a, b) in enumerate(pairs)]
     for copy in copies:
         copy.start()
     made[...] = jnp.zeros_like(made)
-    for copy in copies:
+    for copy in copies[1:]:
         copy.wait()
     slabs = sends.shape[0]
     depth = window - 2
@@ -33,29 +33,28 @@
             for at, data in ((0, target), (made.shape[2] // 2, weight)):
                 made[s, own, at + skip : at + skip + high - low, :] = data[own, low:high, :]
     sends[...] = made[...].astype(sends.dtype)
-
-
-def forward_kernel(
-    rows, live_in, tid_in, bid_in, vol_in, tiles_in, out,
-    live, tid, bid, vol, tiles, vox, picked, sems,
-):
-    angles, slots = tid.shape
-    tile = tiles.shape[1]
+    copies[0].wait()
     lines, width = vol.shape
+    tile = vox.shape[1]
     runs = width // tile
-    pairs = ((bid_in, bid), (live_in, live), (tid_in, tid), (vol_in, vol), (tiles_in, tiles))
-    copies = [pltpu.make_async_copy(a, b, sems.at[i]) for i, (a, b) in enumerate(pairs)]
-    for copy in copies:
-        copy.start()
-    copies[3].wait()
     step = 8
     for run in range(runs):
         for line in range(0, lines, step):
             vox[pl.ds(line * runs + run, step, stride=runs), :] = vol[
                 line : line + step, run * tile : (run + 1) * tile
             ]
-    for copy in copies[:3]:
-        copy.wait()
+
+
+def forward_kernel(
+    rows, live_in, tid_in, bid_in, vox, tiles_in, out, live, tid, bid, tiles, picked, sems
+):
+    angles, slots = tid.shape
+    tile = tiles.shape[1]
+    pairs = ((bid_in, bid), (tiles_in, tiles), (live_in, live), (tid_in, tid))
+    copies = [pltpu.make_async_copy(a, b, sems.at[i]) for i, (a, b) in enumerate(pairs)]
+    for copy in copies:
+        copy.start()
+    copies[0].wait()
 
     def gather(a, at):
         for j in range(slots * rows):
@@ -80,18 +79,27 @@
 
     length = slots * rows
     if angles * length <= STATIC_ROWS:
+        ahead = min(2, angles)
         gather(0, 0)
-        copies[4].wait()
+        if ahead > 1:
+
+            @pl.when(bid[0, 0] >= 0)
+            def _():
+                gather(1, length)
+
+        for copy in copies[1:]:
+            copy.wait()
         for a in range(angles):
 
             @pl.when(live[a] >= 0)
             def _():
-                if a + 1 < angles:
-                    gather(a + 1, (a + 1) % 2 * length)
-                out[a * rows : (a + 1) * rows, :] = project(a, a % 2 * length)
+                if a + ahead < angles:
+                    gather(a + ahead, (a + ahead) % 3 * length)
+                out[a * rows : (a + 1) * rows, :] = project(a, a % 3 * length)
 
     else:
-        copies[4].wait()
+        for copy in copies[1:]:
+            copy.wait()
 
         def project_angle(a, carry):
             gather(a, 0)
@@ -301,24 +309,27 @@
     vmem = pl.BlockSpec(memory_space=pltpu.VMEM)
     hbm = pl.BlockSpec(memory_space=pltpu.HBM)
     params = pltpu.CompilerParams(vmem_limit_bytes=VMEM_LIMIT)
-    buffers = 2 if angle_count * length <= STATIC_ROWS else 1
-
-    sends = pl.pallas_call(
+    buffers = 3 if angle_count * length <= STATIC_ROWS else 1
+
+    sends, held_bid, vox = pl.pallas_call(
         functools.partial(pack_kernel, window),
-        out_shape=jax.ShapeDtypeStruct(
-            (slab_count, own_angles, 2 * padded, local_cols), jnp.bfloat16
+        out_shape=(
+            jax.ShapeDtypeStruct((slab_count, own_angles, 2 * padded, local_cols), jnp.bfloat16),
+            jax.ShapeDtypeStruct((angle_count, length), jnp.int32),
+            jax.ShapeDtypeStruct((lines * runs, tile_size), jnp.float32),
         ),
-        in_specs=[hbm] * 2,
-        out_specs=vmem,
+        in_specs=[hbm] * 4,
+        out_specs=(vmem, vmem, vmem),
         scratch_shapes=[
             pltpu.VMEM((own_angles, row_total, local_cols), jnp.float32),
             pltpu.VMEM((own_angles, row_total, local_cols), jnp.float32),
             pltpu.VMEM((slab_count, own_angles, 2 * padded, local_cols), jnp.float32),
-            pltpu.SemaphoreType.DMA((2,)),
+            pltpu.VMEM((lines, half_width), jnp.float32),
+            pltpu.SemaphoreType.DMA((4,)),
         ],
         compiler_params=params,
         name="pack",
-    )(held(measured.transpose(0, 2, 1)), held(row_norm.transpose(0, 2, 1)))
+    )(held(measured.transpose(0, 2, 1)), held(row_norm.transpose(0, 2, 1)), held(bid), vol)
     columns = sends[:, None]
     for bit in bits("gz")[:0:-1]:
         columns = exchange_slabs(columns, bit)
@@ -326,21 +337,19 @@
     partial = pl.pallas_call(
         functools.partial(forward_kernel, rows),
         out_shape=jax.ShapeDtypeStruct((angle_count * rows, tile_size), jnp.float32),
-        in_specs=[hbm] * 5,
+        in_specs=[hbm, hbm, vmem, vmem, hbm],
         out_specs=vmem,
         scratch_shapes=[
             pltpu.SMEM((angle_count,), jnp.int32),
             pltpu.SMEM((angle_count, slot_count), jnp.int32),
             pltpu.SMEM((angle_count, length), jnp.int32),
-            pltpu.VMEM((lines, half_width), jnp.float32),
             pltpu.VMEM(tile_table.shape, jnp.bfloat16),
-            pltpu.VMEM((lines * runs, tile_size), jnp.float32),
             pltpu.VMEM((buffers * length, tile_size), jnp.float32),
-            pltpu.SemaphoreType.DMA((5,)),
+            pltpu.SemaphoreType.DMA((4,)),
         ],
         compiler_params=params,
         name="forward",
-    )(held(live), held(tid), held(bid), vol, held(tile_table))
+    )(held(live), held(tid), held_bid, vox, held(tile_table))
 
     assert lax.axis_size("row") == 2
     upper = lax.axis_index("row") == 1

time: 26.2 us -> 26.1 us (level)
    pallas_call x1, Pallas kernels: 5.13 us -> 4.42 us  [on_device(): pl.pallas_call(functools.partial(forward_kernel, rows), out_shape=jax.Sha...]
    pallas_call x1, Pallas kernels: 0.74 us -> 1.33 us  [on_device(): pl.pallas_call(functools.partial(pack_kernel, window), out_shape=(jax.Sha...]
  transfers between devices with their start and end apart: 5 -> 5, of which waited for: 4 -> 4; matrix products, arithmetic and copies ran while one was open for 0% -> 0% of each run, Pallas kernels for 20% -> 17%
where the time goes in v8:
time: 26.1 us; the launch traced here: 25.9 us
  Pallas kernels  9.99 us (38%)
  starting transfers between devices  9.47 us (36%)
  waiting for transfers between devices  5.98 us (23%)
    ppermute x4, starting transfers between devices, move_many(): came = lax.ppermute(joined, axis, hops)  7.09 us
    ppermute x4, waiting for transfers between devices, move_many(): came = lax.ppermute(joined, axis, hops)  5.98 us
    pallas_call x1, Pallas kernels, on_device(): pl.pallas_call(functools.partial(forward_kernel, rows), out_shape=jax.Sha...  4.42 us
    pallas_call x1, Pallas kernels, on_device(): pl.pallas_call(functools.partial(backward_kernel, rows, joined), out_shap...  4.24 us
    ppermute x1, starting transfers between devices, swap(): lax.ppermute(values, axis, [(i, i ^ bit) for i in range(lax.axis_size(axi...  2.37 us
    pallas_call x1, Pallas kernels, on_device(): pl.pallas_call(functools.partial(pack_kernel, window), out_shape=(jax.Sha...  1.33 us
  transfers between devices with their start and end apart: 5, of which 4 were waited for; matrix products, arithmetic and copies ran while one was open for 0% of the time, Pallas kernels for 17%

profile of v8, /device:TPU:9, one launch (start us, length us, event | category | flops | bytes accessed | tf_op | source)
XLA Modules:
  0.0 25.9 jit_solution(17831641389161900450)
XLA Ops:
  0.0 1.3 %pack.1 = (bf16[4,1,16,128]{3,2,1,0:T(8,128)(2,1)S(1)}, s32[4,768]{1,0:T(4,128)S(1)}, f32[2048,128]{1,0:T(8,128)S(1)}) custom-call(f32[1,16,128]{2,1,0:T(8,128)} %bitcast.141, f32[1,16,128]{2,1,0:T(8,128)} %bitcast.142, s32[4,768]{1,0:T(4,128)} %bitcast.122, f32[1024,256]{1,0:T(8,128)} %bitcast.128), custom_call_target="tpu_custom_call" | custom-call | tf_op jit(solution)/shard_map/pack/pallas_call | solution.py:314
  1.3 2.4 %collective-permute-start = (bf16[2,1,1,16,128]{4,3,0,2,1:T(8,128)(2,1)S(1)}, bf16[2,1,1,16,128]{4,3,0,2,1:T(8,128)(2,1)S(1)}, u32[]{:S(2)}, u32[]{:S(2)}) collective-permute-start(bf16[2,1,1,16,128]{4,3,0,2,1:T(8,128)(2,1)S(1)} %fusion.10), channel_id=1, source_target_pairs={{0,8},{4,12},{8,0},{12,4},{1,9},{5,13},{9,1},{13,5},{2,10},{6,14},... | collective-permute-start | bytes 24584 | tf_op jit(solution)/shard_map/slab2/ppermute | solution.py:239
  3.7 0.0 copy-start
  3.7 0.0 copy-start.1
  3.7 0.0 copy-start.2
  3.7 0.0 copy-start.3
  3.7 4.4 %forward.1 = f32[96,128]{1,0:T(8,128)S(1)} custom-call(s32[4]{0:T(128)} %bitcast.126, s32[4,32]{1,0:T(4,128)} %bitcast.124, s32[4,768]{1,0:T(4,128)S(1)} %get-tuple-element.8.bid_in, f32[2048,128]{1,0:T(8,128)S(1)} %get-tuple-element.9.vox, bf16[64,128,128]{2,1,0:T(8,128)(2,1)} %tiles.1), custom_call_target="tpu_custom_call" | custom-call | tf_op jit(solution)/shard_map/forward/pallas_call | solution.py:337
  8.2 0.0 collective-permute-done
  8.2 1.0 %collective-permute-start.1 = (f32[128,128]{1,0:T(8,128)S(1)}, f32[128,128]{1,0:T(8,128)S(1)}, u32[]{:S(2)}, u32[]{:S(2)}) collective-permute-start(f32[128,128]{1,0:T(8,128)S(1)} %pad_maximum_fusion), channel_id=1, source_target_pairs={{0,1},{1,0},{2,3},{3,2},{4,5},{5,4},{6,7},{7,6},{8,9},{9,8},{10,11... | collective-permute-start | bytes 196616 | tf_op jit(solution)/shard_map/rowsum/ppermute | solution.py:247
  9.3 0.9 %collective-permute-done.1 = f32[128,128]{1,0:T(8,128)S(1)} collective-permute-done((f32[128,128]{1,0:T(8,128)S(1)}, f32[128,128]{1,0:T(8,128)S(1)}, u32[]{:S(2)}, u32[]{:S(2)}) %collective-permute-start.1) | collective-permute-done | bytes 65568 | tf_op jit(solution)/shard_map/rowsum/ppermute | solution.py:247
  10.2 1.3 %collective-permute-start.2 = (bf16[128,128]{1,0:T(8,128)(2,1)S(1)}, bf16[128,128]{1,0:T(8,128)(2,1)S(1)}, u32[]{:S(2)}, u32[]{:S(2)}) collective-permute-start(bf16[128,128]{1,0:T(8,128)(2,1)S(1)} %pad_maximum_fusion.4), channel_id=1, source_target_pairs={{0,2},{2,0},{1,3},{3,1},{4,6},{6,4},{5,7},{7,5},{8,10},{10,8},{9,1... | collective-permute-start | bytes 98312 | tf_op jit(solution)/shard_map/gxsum1/ppermute | solution.py:247
  11.5 1.6 %collective-permute-done.2 = bf16[128,128]{1,0:T(8,128)(2,1)S(1)} collective-permute-done((bf16[128,128]{1,0:T(8,128)(2,1)S(1)}, bf16[128,128]{1,0:T(8,128)(2,1)S(1)}, u32[]{:S(2)}, u32[]{:S(2)}) %collective-permute-start.2) | collective-permute-done | bytes 32800 | tf_op jit(solution)/shard_map/gxsum1/ppermute | solution.py:247
  13.1 2.1 %collective-permute-start.3 = (bf16[160,128]{1,0:T(8,128)(2,1)S(1)}, bf16[160,128]{1,0:T(8,128)(2,1)S(1)}, u32[]{:S(2)}, u32[]{:S(2)}) collective-permute-start(bf16[160,128]{1,0:T(8,128)(2,1)S(1)} %pad_maximum_fusion.2), channel_id=1, source_target_pairs={{1,5},{5,1},{9,13},{13,9},{4,8},{8,4},{3,7},{7,3},{11,15},{15,11},... | collective-permute-start | bytes 122888 | tf_op jit(solution)/shard_map/rims/ppermute | solution.py:247
  15.2 2.7 %collective-permute-done.3 = bf16[160,128]{1,0:T(8,128)(2,1)S(1)} collective-permute-done((bf16[160,128]{1,0:T(8,128)(2,1)S(1)}, bf16[160,128]{1,0:T(8,128)(2,1)S(1)}, u32[]{:S(2)}, u32[]{:S(2)}) %collective-permute-start.3) | collective-permute-done | bytes 40992 | tf_op jit(solution)/shard_map/rims/ppermute | solution.py:247
  17.9 2.7 %collective-permute-start.4 = (bf16[160,128]{1,0:T(8,128)(2,1)S(1)}, bf16[160,128]{1,0:T(8,128)(2,1)S(1)}, u32[]{:S(2)}, u32[]{:S(2)}) collective-permute-start(bf16[160,128]{1,0:T(8,128)(2,1)S(1)} %pad_maximum_fusion.3), channel_id=1, source_target_pairs={{0,1},{1,0},{2,3},{3,2},{4,5},{5,4},{6,7},{7,6},{8,9},{9,8},{10,11... | collective-permute-start | bytes 122888 | tf_op jit(solution)/shard_map/finish/ppermute | solution.py:247
  20.6 0.9 %collective-permute-done.4 = bf16[160,128]{1,0:T(8,128)(2,1)S(1)} collective-permute-done((bf16[160,128]{1,0:T(8,128)(2,1)S(1)}, bf16[160,128]{1,0:T(8,128)(2,1)S(1)}, u32[]{:S(2)}, u32[]{:S(2)}) %collective-permute-start.4) | collective-permute-done | bytes 40992 | tf_op jit(solution)/shard_map/finish/ppermute | solution.py:247
  21.6 0.0 copy-done
  21.6 0.0 copy-done.1
  21.6 0.0 copy-done.2
  21.6 0.0 copy-done.3
  21.6 4.2 %backward.1 = f32[1024,256]{1,0:T(8,128)} custom-call(s32[4]{0:T(128)S(1)} %bitcast.127, s32[4,32]{1,0:T(4,128)S(1)} %bitcast.125, s32[4,768]{1,0:T(4,128)S(1)} %bitcast.123, f32[32,128]{1,0:T(8,128)S(1)} %get-tuple-element.17.head, f32[32,128]{1,0:T(8,128)S(1)} %get-tuple-element.26.middle, f32[32,128]{1,0:T(8,128)S(1)} %get-tuple-element.16.tail, ...), custom_call_target="tpu_custom_call" | custom-call | tf_op jit(solution)/shard_map/backward/pallas_call | solution.py:396
  (26 shorter events, 0.2 us)
Async XLA Ops:
  1.3 6.8 %collective-permute-start = (bf16[2,1,1,16,128]{4,3,0,2,1:T(8,128)(2,1)S(1)}, bf16[2,1,1,16,128]{4,3,0,2,1:T(8,128)(2,1)S(1)}, u32[]{:S(2)}, u32[]{:S(2)}) collective-permute-start(bf16[2,1,1,16,128]{4,3,0,2,1:T(8,128)(2,1)S(1)} %fusion.10), channel_id=1, source_target_pairs={{0,8},{4,12},{8,0},{12,4},{1,9},{5,13},{9,1},{13,5},{2,10},{6,14},... | collective-permute-start | bytes 24584 | tf_op jit(solution)/shard_map/slab2/ppermute | solution.py:239
  3.7 17.9 %copy-start = (bf16[64,128,128]{2,1,0:T(8,128)(2,1)S(1)}, bf16[64,128,128]{2,1,0:T(8,128)(2,1)}, u32[]{:S(2)}) copy-start(bf16[64,128,128]{2,1,0:T(8,128)(2,1)} %tiles.1) | copy-start | bytes 6291460
  3.7 17.9 %copy-start.1 = (s32[1,1,1,4,768]{4,3,2,1,0:T(4,128)S(1)}, s32[1,1,1,4,768]{4,3,2,1,0:T(4,128)}, u32[]{:S(2)}) copy-start(s32[1,1,1,4,768]{4,3,2,1,0:T(4,128)} %param.11) | copy-start | bytes 36868
  3.7 17.9 %copy-start.2 = (s32[1,1,1,4,32]{4,3,2,1,0:T(4,128)S(1)}, s32[1,1,1,4,32]{4,3,2,1,0:T(4,128)}, u32[]{:S(2)}) copy-start(s32[1,1,1,4,32]{4,3,2,1,0:T(4,128)} %param.10) | copy-start | bytes 1540
  3.7 17.9 %copy-start.3 = (s32[1,1,1,4]{3,2,1,0:T(1,128)S(1)}, s32[1,1,1,4]{3,2,1,0:T(1,128)}, u32[]{:S(2)}) copy-start(s32[1,1,1,4]{3,2,1,0:T(1,128)} %param.12) | copy-start | bytes 52
  8.2 1.9 %collective-permute-start.1 = (f32[128,128]{1,0:T(8,128)S(1)}, f32[128,128]{1,0:T(8,128)S(1)}, u32[]{:S(2)}, u32[]{:S(2)}) collective-permute-start(f32[128,128]{1,0:T(8,128)S(1)} %pad_maximum_fusion), channel_id=1, source_target_pairs={{0,1},{1,0},{2,3},{3,2},{4,5},{5,4},{6,7},{7,6},{8,9},{9,8},{10,11... | collective-permute-start | bytes 196616 | tf_op jit(solution)/shard_map/rowsum/ppermute | solution.py:247
  10.2 2.8 %collective-permute-start.2 = (bf16[128,128]{1,0:T(8,128)(2,1)S(1)}, bf16[128,128]{1,0:T(8,128)(2,1)S(1)}, u32[]{:S(2)}, u32[]{:S(2)}) collective-permute-start(bf16[128,128]{1,0:T(8,128)(2,1)S(1)} %pad_maximum_fusion.4), channel_id=1, source_target_pairs={{0,2},{2,0},{1,3},{3,1},{4,6},{6,4},{5,7},{7,5},{8,10},{10,8},{9,1... | collective-permute-start | bytes 98312 | tf_op jit(solution)/shard_map/gxsum1/ppermute | solution.py:247
  13.1 4.7 %collective-permute-start.3 = (bf16[160,128]{1,0:T(8,128)(2,1)S(1)}, bf16[160,128]{1,0:T(8,128)(2,1)S(1)}, u32[]{:S(2)}, u32[]{:S(2)}) collective-permute-start(bf16[160,128]{1,0:T(8,128)(2,1)S(1)} %pad_maximum_fusion.2), channel_id=1, source_target_pairs={{1,5},{5,1},{9,13},{13,9},{4,8},{8,4},{3,7},{7,3},{11,15},{15,11},... | collective-permute-start | bytes 122888 | tf_op jit(solution)/shard_map/rims/ppermute | solution.py:247
  17.9 3.6 %collective-permute-start.4 = (bf16[160,128]{1,0:T(8,128)(2,1)S(1)}, bf16[160,128]{1,0:T(8,128)(2,1)S(1)}, u32[]{:S(2)}, u32[]{:S(2)}) collective-permute-start(bf16[160,128]{1,0:T(8,128)(2,1)S(1)} %pad_maximum_fusion.3), channel_id=1, source_target_pairs={{0,1},{1,0},{2,3},{3,2},{4,5},{5,4},{6,7},{7,6},{8,9},{9,8},{10,11... | collective-permute-start | bytes 122888 | tf_op jit(solution)/shard_map/finish/ppermute | solution.py:247

commit v9 on v8

--- a/solution.py
+++ b/solution.py
@@ -46,7 +46,7 @@
 
 
 def forward_kernel(
-    rows, live_in, tid_in, bid_in, vox, tiles_in, out, live, tid, bid, tiles, picked, sems
+    rows, live_in, tid_in, bid_in, vox, tiles_in, out, tiles, live, tid, bid, picked, sems
 ):
     angles, slots = tid.shape
     tile = tiles.shape[1]
@@ -334,16 +334,18 @@
     for bit in bits("gz")[:0:-1]:
         columns = exchange_slabs(columns, bit)
 
-    partial = pl.pallas_call(
+    partial, held_tiles = pl.pallas_call(
         functools.partial(forward_kernel, rows),
-        out_shape=jax.ShapeDtypeStruct((angle_count * rows, tile_size), jnp.float32),
+        out_shape=(
+            jax.ShapeDtypeStruct((angle_count * rows, tile_size), jnp.float32),
+            jax.ShapeDtypeStruct(tile_table.shape, tile_table.dtype),
+        ),
         in_specs=[hbm, hbm, vmem, vmem, hbm],
-        out_specs=vmem,
+        out_specs=(vmem, vmem),
         scratch_shapes=[
             pltpu.SMEM((angle_count,), jnp.int32),
             pltpu.SMEM((angle_count, slot_count), jnp.int32),
             pltpu.SMEM((angle_count, length), jnp.int32),
-            pltpu.VMEM(tile_table.shape, jnp.bfloat16),
             pltpu.VMEM((buffers * length, tile_size), jnp.float32),
             pltpu.SemaphoreType.DMA((4,)),
         ],
@@ -414,7 +416,7 @@
         compiler_params=params,
         name="backward",
     )(
-        live, tid, bid, head, middle.reshape(-1, tile_size), tail, columns, tile_table, vol, col,
+        live, tid, bid, head, middle.reshape(-1, tile_size), tail, columns, held_tiles, vol, col,
     )
     return made.reshape(slab_depth, column_width, half_width)
 

time: 26.1 us -> 25.9 us (level)
  no operation moved by 1% of the time
where the time goes in v9:
time: 25.9 us; the launch traced here: 25.7 us
  Pallas kernels  9.89 us (38%)
  starting transfers between devices  9.46 us (37%)
  waiting for transfers between devices  5.98 us (23%)
    ppermute x4, starting transfers between devices, move_many(): came = lax.ppermute(joined, axis, hops)  7.09 us
    ppermute x4, waiting for transfers between devices, move_many(): came = lax.ppermute(joined, axis, hops)  5.98 us
    pallas_call x1, Pallas kernels, on_device(): pl.pallas_call(functools.partial(forward_kernel, rows), out_shape=(jax.Sh...  4.31 us
    pallas_call x1, Pallas kernels, on_device(): pl.pallas_call(functools.partial(backward_kernel, rows, joined), out_shap...  4.25 us
    ppermute x1, starting transfers between devices, swap(): lax.ppermute(values, axis, [(i, i ^ bit) for i in range(lax.axis_size(axi...  2.37 us
    pallas_call x1, Pallas kernels, on_device(): pl.pallas_call(functools.partial(pack_kernel, window), out_shape=(jax.Sha...  1.33 us
  transfers between devices with their start and end apart: 5, of which 4 were waited for; matrix products, arithmetic and copies ran while one was open for 0% of the time, Pallas kernels for 17%

profile of v9, /device:TPU:9, one launch (start us, length us, event | category | flops | bytes accessed | tf_op | source)
XLA Modules:
  0.0 25.7 jit_solution(5516149787104969026)
XLA Ops:
  0.0 1.3 %pack.1 = (bf16[4,1,16,128]{3,2,1,0:T(8,128)(2,1)S(1)}, s32[4,768]{1,0:T(4,128)S(1)}, f32[2048,128]{1,0:T(8,128)S(1)}) custom-call(f32[1,16,128]{2,1,0:T(8,128)} %bitcast.141, f32[1,16,128]{2,1,0:T(8,128)} %bitcast.142, s32[4,768]{1,0:T(4,128)} %bitcast.122, f32[1024,256]{1,0:T(8,128)} %bitcast.128), custom_call_target="tpu_custom_call" | custom-call | tf_op jit(solution)/shard_map/pack/pallas_call | solution.py:314
  1.3 2.4 %collective-permute-start = (bf16[2,1,1,16,128]{4,3,0,2,1:T(8,128)(2,1)S(1)}, bf16[2,1,1,16,128]{4,3,0,2,1:T(8,128)(2,1)S(1)}, u32[]{:S(2)}, u32[]{:S(2)}) collective-permute-start(bf16[2,1,1,16,128]{4,3,0,2,1:T(8,128)(2,1)S(1)} %fusion.10), channel_id=1, source_target_pairs={{0,8},{4,12},{8,0},{12,4},{1,9},{5,13},{9,1},{13,5},{2,10},{6,14},... | collective-permute-start | bytes 24584 | tf_op jit(solution)/shard_map/slab2/ppermute | solution.py:239
  3.7 0.0 copy-start
  3.7 0.0 copy-start.1
  3.7 0.0 copy-start.2
  3.7 4.3 %forward.1 = (f32[96,128]{1,0:T(8,128)S(1)}, bf16[64,128,128]{2,1,0:T(8,128)(2,1)S(1)}) custom-call(s32[4]{0:T(128)} %bitcast.126, s32[4,32]{1,0:T(4,128)} %bitcast.124, s32[4,768]{1,0:T(4,128)S(1)} %get-tuple-element.10.bid_in, f32[2048,128]{1,0:T(8,128)S(1)} %get-tuple-element.11.vox, bf16[64,128,128]{2,1,0:T(8,128)(2,1)} %tiles_in.1), custom_call_target="tpu_custom_call" | custom-call | tf_op jit(solution)/shard_map/forward/pallas_call | solution.py:337
  8.1 0.0 collective-permute-done
  8.1 1.0 %collective-permute-start.1 = (f32[128,128]{1,0:T(8,128)S(1)}, f32[128,128]{1,0:T(8,128)S(1)}, u32[]{:S(2)}, u32[]{:S(2)}) collective-permute-start(f32[128,128]{1,0:T(8,128)S(1)} %pad_maximum_fusion), channel_id=1, source_target_pairs={{0,1},{1,0},{2,3},{3,2},{4,5},{5,4},{6,7},{7,6},{8,9},{9,8},{10,11... | collective-permute-start | bytes 196616 | tf_op jit(solution)/shard_map/rowsum/ppermute | solution.py:247
  9.1 0.9 %collective-permute-done.1 = f32[128,128]{1,0:T(8,128)S(1)} collective-permute-done((f32[128,128]{1,0:T(8,128)S(1)}, f32[128,128]{1,0:T(8,128)S(1)}, u32[]{:S(2)}, u32[]{:S(2)}) %collective-permute-start.1) | collective-permute-done | bytes 65568 | tf_op jit(solution)/shard_map/rowsum/ppermute | solution.py:247
  10.1 1.3 %collective-permute-start.2 = (bf16[128,128]{1,0:T(8,128)(2,1)S(1)}, bf16[128,128]{1,0:T(8,128)(2,1)S(1)}, u32[]{:S(2)}, u32[]{:S(2)}) collective-permute-start(bf16[128,128]{1,0:T(8,128)(2,1)S(1)} %pad_maximum_fusion.4), channel_id=1, source_target_pairs={{0,2},{2,0},{1,3},{3,1},{4,6},{6,4},{5,7},{7,5},{8,10},{10,8},{9,1... | collective-permute-start | bytes 98312 | tf_op jit(solution)/shard_map/gxsum1/ppermute | solution.py:247
  11.4 1.6 %collective-permute-done.2 = bf16[128,128]{1,0:T(8,128)(2,1)S(1)} collective-permute-done((bf16[128,128]{1,0:T(8,128)(2,1)S(1)}, bf16[128,128]{1,0:T(8,128)(2,1)S(1)}, u32[]{:S(2)}, u32[]{:S(2)}) %collective-permute-start.2) | collective-permute-done | bytes 32800 | tf_op jit(solution)/shard_map/gxsum1/ppermute | solution.py:247
  13.0 2.1 %collective-permute-start.3 = (bf16[160,128]{1,0:T(8,128)(2,1)S(1)}, bf16[160,128]{1,0:T(8,128)(2,1)S(1)}, u32[]{:S(2)}, u32[]{:S(2)}) collective-permute-start(bf16[160,128]{1,0:T(8,128)(2,1)S(1)} %pad_maximum_fusion.2), channel_id=1, source_target_pairs={{1,5},{5,1},{9,13},{13,9},{4,8},{8,4},{3,7},{7,3},{11,15},{15,11},... | collective-permute-start | bytes 122888 | tf_op jit(solution)/shard_map/rims/ppermute | solution.py:247
  15.1 2.7 %collective-permute-done.3 = bf16[160,128]{1,0:T(8,128)(2,1)S(1)} collective-permute-done((bf16[160,128]{1,0:T(8,128)(2,1)S(1)}, bf16[160,128]{1,0:T(8,128)(2,1)S(1)}, u32[]{:S(2)}, u32[]{:S(2)}) %collective-permute-start.3) | collective-permute-done | bytes 40992 | tf_op jit(solution)/shard_map/rims/ppermute | solution.py:247
  17.8 2.7 %collective-permute-start.4 = (bf16[160,128]{1,0:T(8,128)(2,1)S(1)}, bf16[160,128]{1,0:T(8,128)(2,1)S(1)}, u32[]{:S(2)}, u32[]{:S(2)}) collective-permute-start(bf16[160,128]{1,0:T(8,128)(2,1)S(1)} %pad_maximum_fusion.3), channel_id=1, source_target_pairs={{0,1},{1,0},{2,3},{3,2},{4,5},{5,4},{6,7},{7,6},{8,9},{9,8},{10,11... | collective-permute-start | bytes 122888 | tf_op jit(solution)/shard_map/finish/ppermute | solution.py:247
  20.5 0.9 %collective-permute-done.4 = bf16[160,128]{1,0:T(8,128)(2,1)S(1)} collective-permute-done((bf16[160,128]{1,0:T(8,128)(2,1)S(1)}, bf16[160,128]{1,0:T(8,128)(2,1)S(1)}, u32[]{:S(2)}, u32[]{:S(2)}) %collective-permute-start.4) | collective-permute-done | bytes 40992 | tf_op jit(solution)/shard_map/finish/ppermute | solution.py:247
  21.5 0.0 copy-done
  21.5 0.0 copy-done.1
  21.5 0.0 copy-done.2
  21.5 4.2 %backward.1 = f32[1024,256]{1,0:T(8,128)} custom-call(s32[4]{0:T(128)S(1)} %bitcast.127, s32[4,32]{1,0:T(4,128)S(1)} %bitcast.125, s32[4,768]{1,0:T(4,128)S(1)} %bitcast.123, f32[32,128]{1,0:T(8,128)S(1)} %get-tuple-element.21.head, f32[32,128]{1,0:T(8,128)S(1)} %get-tuple-element.30.middle, f32[32,128]{1,0:T(8,128)S(1)} %get-tuple-element.20.tail, ...), custom_call_target="tpu_custom_call" | custom-call | tf_op jit(solution)/shard_map/backward/pallas_call | solution.py:398
  (26 shorter events, 0.2 us)
Async XLA Ops:
  1.3 6.7 %collective-permute-start = (bf16[2,1,1,16,128]{4,3,0,2,1:T(8,128)(2,1)S(1)}, bf16[2,1,1,16,128]{4,3,0,2,1:T(8,128)(2,1)S(1)}, u32[]{:S(2)}, u32[]{:S(2)}) collective-permute-start(bf16[2,1,1,16,128]{4,3,0,2,1:T(8,128)(2,1)S(1)} %fusion.10), channel_id=1, source_target_pairs={{0,8},{4,12},{8,0},{12,4},{1,9},{5,13},{9,1},{13,5},{2,10},{6,14},... | collective-permute-start | bytes 24584 | tf_op jit(solution)/shard_map/slab2/ppermute | solution.py:239
  3.7 17.7 %copy-start = (s32[1,1,1,4,768]{4,3,2,1,0:T(4,128)S(1)}, s32[1,1,1,4,768]{4,3,2,1,0:T(4,128)}, u32[]{:S(2)}) copy-start(s32[1,1,1,4,768]{4,3,2,1,0:T(4,128)} %param.11) | copy-start | bytes 36868
  3.7 17.7 %copy-start.1 = (s32[1,1,1,4,32]{4,3,2,1,0:T(4,128)S(1)}, s32[1,1,1,4,32]{4,3,2,1,0:T(4,128)}, u32[]{:S(2)}) copy-start(s32[1,1,1,4,32]{4,3,2,1,0:T(4,128)} %param.10) | copy-start | bytes 1540
  3.7 17.7 %copy-start.2 = (s32[1,1,1,4]{3,2,1,0:T(1,128)S(1)}, s32[1,1,1,4]{3,2,1,0:T(1,128)}, u32[]{:S(2)}) copy-start(s32[1,1,1,4]{3,2,1,0:T(1,128)} %param.12) | copy-start | bytes 52
  8.1 1.9 %collective-permute-start.1 = (f32[128,128]{1,0:T(8,128)S(1)}, f32[128,128]{1,0:T(8,128)S(1)}, u32[]{:S(2)}, u32[]{:S(2)}) collective-permute-start(f32[128,128]{1,0:T(8,128)S(1)} %pad_maximum_fusion), channel_id=1, source_target_pairs={{0,1},{1,0},{2,3},{3,2},{4,5},{5,4},{6,7},{7,6},{8,9},{9,8},{10,11... | collective-permute-start | bytes 196616 | tf_op jit(solution)/shard_map/rowsum/ppermute | solution.py:247
  10.1 2.8 %collective-permute-start.2 = (bf16[128,128]{1,0:T(8,128)(2,1)S(1)}, bf16[128,128]{1,0:T(8,128)(2,1)S(1)}, u32[]{:S(2)}, u32[]{:S(2)}) collective-permute-start(bf16[128,128]{1,0:T(8,128)(2,1)S(1)} %pad_maximum_fusion.4), channel_id=1, source_target_pairs={{0,2},{2,0},{1,3},{3,1},{4,6},{6,4},{5,7},{7,5},{8,10},{10,8},{9,1... | collective-permute-start | bytes 98312 | tf_op jit(solution)/shard_map/gxsum1/ppermute | solution.py:247
  13.0 4.7 %collective-permute-start.3 = (bf16[160,128]{1,0:T(8,128)(2,1)S(1)}, bf16[160,128]{1,0:T(8,128)(2,1)S(1)}, u32[]{:S(2)}, u32[]{:S(2)}) collective-permute-start(bf16[160,128]{1,0:T(8,128)(2,1)S(1)} %pad_maximum_fusion.2), channel_id=1, source_target_pairs={{1,5},{5,1},{9,13},{13,9},{4,8},{8,4},{3,7},{7,3},{11,15},{15,11},... | collective-permute-start | bytes 122888 | tf_op jit(solution)/shard_map/rims/ppermute | solution.py:247
  17.8 3.6 %collective-permute-start.4 = (bf16[160,128]{1,0:T(8,128)(2,1)S(1)}, bf16[160,128]{1,0:T(8,128)(2,1)S(1)}, u32[]{:S(2)}, u32[]{:S(2)}) collective-permute-start(bf16[160,128]{1,0:T(8,128)(2,1)S(1)} %pad_maximum_fusion.3), channel_id=1, source_target_pairs={{0,1},{1,0},{2,3},{3,2},{4,5},{5,4},{6,7},{7,6},{8,9},{9,8},{10,11... | collective-permute-start | bytes 122888 | tf_op jit(solution)/shard_map/finish/ppermute | solution.py:247

commit v10 on v9

--- a/solution.py
+++ b/solution.py
@@ -89,12 +89,16 @@
 
         for copy in copies[1:]:
             copy.wait()
-        for a in range(angles):
+        for a in range(angles - ahead):
 
             @pl.when(live[a] >= 0)
             def _():
-                if a + ahead < angles:
-                    gather(a + ahead, (a + ahead) % 3 * length)
+                gather(a + ahead, (a + ahead) % 3 * length)
+                out[a * rows : (a + 1) * rows, :] = project(a, a % 3 * length)
+
+        @pl.when(live[0] >= 0)
+        def _():
+            for a in range(angles - ahead, angles):
                 out[a * rows : (a + 1) * rows, :] = project(a, a % 3 * length)
 
     else:

time: 25.9 us -> 25.8 us (level)
  transfers between devices with their start and end apart: 5 -> 5, of which waited for: 4 -> 4; matrix products, arithmetic and copies ran while one was open for 0% -> 0% of each run, Pallas kernels for 17% -> 16%
where the time goes in v10:
time: 25.8 us; the launch traced here: 25.6 us
  Pallas kernels  9.76 us (38%)
  starting transfers between devices  9.47 us (37%)
  waiting for transfers between devices  5.98 us (23%)
    ppermute x4, starting transfers between devices, move_many(): came = lax.ppermute(joined, axis, hops)  7.09 us
    ppermute x4, waiting for transfers between devices, move_many(): came = lax.ppermute(joined, axis, hops)  5.97 us
    pallas_call x1, Pallas kernels, on_device(): pl.pallas_call(functools.partial(backward_kernel, rows, joined), out_shap...  4.24 us
    pallas_call x1, Pallas kernels, on_device(): pl.pallas_call(functools.partial(forward_kernel, rows), out_shape=(jax.Sh...  4.2 us
    ppermute x1, starting transfers between devices, swap(): lax.ppermute(values, axis, [(i, i ^ bit) for i in range(lax.axis_size(axi...  2.37 us
    pallas_call x1, Pallas kernels, on_device(): pl.pallas_call(functools.partial(pack_kernel, window), out_shape=(jax.Sha...  1.33 us
  transfers between devices with their start and end apart: 5, of which 4 were waited for; matrix products, arithmetic and copies ran while one was open for 0% of the time, Pallas kernels for 16%

profile of v10, /device:TPU:9, one launch (start us, length us, event | category | flops | bytes accessed | tf_op | source)
XLA Modules:
  0.0 25.6 jit_solution(453875187826326184)
XLA Ops:
  0.0 1.3 %pack.1 = (bf16[4,1,16,128]{3,2,1,0:T(8,128)(2,1)S(1)}, s32[4,768]{1,0:T(4,128)S(1)}, f32[2048,128]{1,0:T(8,128)S(1)}) custom-call(f32[1,16,128]{2,1,0:T(8,128)} %bitcast.141, f32[1,16,128]{2,1,0:T(8,128)} %bitcast.142, s32[4,768]{1,0:T(4,128)} %bitcast.122, f32[1024,256]{1,0:T(8,128)} %bitcast.128), custom_call_target="tpu_custom_call" | custom-call | tf_op jit(solution)/shard_map/pack/pallas_call | solution.py:318
  1.3 2.4 %collective-permute-start = (bf16[2,1,1,16,128]{4,3,0,2,1:T(8,128)(2,1)S(1)}, bf16[2,1,1,16,128]{4,3,0,2,1:T(8,128)(2,1)S(1)}, u32[]{:S(2)}, u32[]{:S(2)}) collective-permute-start(bf16[2,1,1,16,128]{4,3,0,2,1:T(8,128)(2,1)S(1)} %fusion.10), channel_id=1, source_target_pairs={{0,8},{4,12},{8,0},{12,4},{1,9},{5,13},{9,1},{13,5},{2,10},{6,14},... | collective-permute-start | bytes 24584 | tf_op jit(solution)/shard_map/slab2/ppermute | solution.py:243
  3.7 0.0 copy-start
  3.7 0.0 copy-start.1
  3.7 0.0 copy-start.2
  3.7 4.2 %forward.1 = (f32[96,128]{1,0:T(8,128)S(1)}, bf16[64,128,128]{2,1,0:T(8,128)(2,1)S(1)}) custom-call(s32[4]{0:T(128)} %bitcast.126, s32[4,32]{1,0:T(4,128)} %bitcast.124, s32[4,768]{1,0:T(4,128)S(1)} %get-tuple-element.10.bid_in, f32[2048,128]{1,0:T(8,128)S(1)} %get-tuple-element.11.vox, bf16[64,128,128]{2,1,0:T(8,128)(2,1)} %tiles_in.1), custom_call_target="tpu_custom_call" | custom-call | tf_op jit(solution)/shard_map/forward/pallas_call | solution.py:341
  7.9 0.0 collective-permute-done
  8.0 1.0 %collective-permute-start.1 = (f32[128,128]{1,0:T(8,128)S(1)}, f32[128,128]{1,0:T(8,128)S(1)}, u32[]{:S(2)}, u32[]{:S(2)}) collective-permute-start(f32[128,128]{1,0:T(8,128)S(1)} %pad_maximum_fusion), channel_id=1, source_target_pairs={{0,1},{1,0},{2,3},{3,2},{4,5},{5,4},{6,7},{7,6},{8,9},{9,8},{10,11... | collective-permute-start | bytes 196616 | tf_op jit(solution)/shard_map/rowsum/ppermute | solution.py:251
  9.0 0.9 %collective-permute-done.1 = f32[128,128]{1,0:T(8,128)S(1)} collective-permute-done((f32[128,128]{1,0:T(8,128)S(1)}, f32[128,128]{1,0:T(8,128)S(1)}, u32[]{:S(2)}, u32[]{:S(2)}) %collective-permute-start.1) | collective-permute-done | bytes 65568 | tf_op jit(solution)/shard_map/rowsum/ppermute | solution.py:251
  10.0 1.3 %collective-permute-start.2 = (bf16[128,128]{1,0:T(8,128)(2,1)S(1)}, bf16[128,128]{1,0:T(8,128)(2,1)S(1)}, u32[]{:S(2)}, u32[]{:S(2)}) collective-permute-start(bf16[128,128]{1,0:T(8,128)(2,1)S(1)} %pad_maximum_fusion.4), channel_id=1, source_target_pairs={{0,2},{2,0},{1,3},{3,1},{4,6},{6,4},{5,7},{7,5},{8,10},{10,8},{9,1... | collective-permute-start | bytes 98312 | tf_op jit(solution)/shard_map/gxsum1/ppermute | solution.py:251
  11.3 1.6 %collective-permute-done.2 = bf16[128,128]{1,0:T(8,128)(2,1)S(1)} collective-permute-done((bf16[128,128]{1,0:T(8,128)(2,1)S(1)}, bf16[128,128]{1,0:T(8,128)(2,1)S(1)}, u32[]{:S(2)}, u32[]{:S(2)}) %collective-permute-start.2) | collective-permute-done | bytes 32800 | tf_op jit(solution)/shard_map/gxsum1/ppermute | solution.py:251
  12.9 2.1 %collective-permute-start.3 = (bf16[160,128]{1,0:T(8,128)(2,1)S(1)}, bf16[160,128]{1,0:T(8,128)(2,1)S(1)}, u32[]{:S(2)}, u32[]{:S(2)}) collective-permute-start(bf16[160,128]{1,0:T(8,128)(2,1)S(1)} %pad_maximum_fusion.2), channel_id=1, source_target_pairs={{1,5},{5,1},{9,13},{13,9},{4,8},{8,4},{3,7},{7,3},{11,15},{15,11},... | collective-permute-start | bytes 122888 | tf_op jit(solution)/shard_map/rims/ppermute | solution.py:251
  15.0 2.7 %collective-permute-done.3 = bf16[160,128]{1,0:T(8,128)(2,1)S(1)} collective-permute-done((bf16[160,128]{1,0:T(8,128)(2,1)S(1)}, bf16[160,128]{1,0:T(8,128)(2,1)S(1)}, u32[]{:S(2)}, u32[]{:S(2)}) %collective-permute-start.3) | collective-permute-done | bytes 40992 | tf_op jit(solution)/shard_map/rims/ppermute | solution.py:251
  17.7 2.7 %collective-permute-start.4 = (bf16[160,128]{1,0:T(8,128)(2,1)S(1)}, bf16[160,128]{1,0:T(8,128)(2,1)S(1)}, u32[]{:S(2)}, u32[]{:S(2)}) collective-permute-start(bf16[160,128]{1,0:T(8,128)(2,1)S(1)} %pad_maximum_fusion.3), channel_id=1, source_target_pairs={{0,1},{1,0},{2,3},{3,2},{4,5},{5,4},{6,7},{7,6},{8,9},{9,8},{10,11... | collective-permute-start | bytes 122888 | tf_op jit(solution)/shard_map/finish/ppermute | solution.py:251
  20.4 0.9 %collective-permute-done.4 = bf16[160,128]{1,0:T(8,128)(2,1)S(1)} collective-permute-done((bf16[160,128]{1,0:T(8,128)(2,1)S(1)}, bf16[160,128]{1,0:T(8,128)(2,1)S(1)}, u32[]{:S(2)}, u32[]{:S(2)}) %collective-permute-start.4) | collective-permute-done | bytes 40992 | tf_op jit(solution)/shard_map/finish/ppermute | solution.py:251
  21.3 0.0 copy-done
  21.3 0.0 copy-done.1
  21.4 0.0 copy-done.2
  21.4 4.2 %backward.1 = f32[1024,256]{1,0:T(8,128)} custom-call(s32[4]{0:T(128)S(1)} %bitcast.127, s32[4,32]{1,0:T(4,128)S(1)} %bitcast.125, s32[4,768]{1,0:T(4,128)S(1)} %bitcast.123, f32[32,128]{1,0:T(8,128)S(1)} %get-tuple-element.21.head, f32[32,128]{1,0:T(8,128)S(1)} %get-tuple-element.30.middle, f32[32,128]{1,0:T(8,128)S(1)} %get-tuple-element.20.tail, ...), custom_call_target="tpu_custom_call" | custom-call | tf_op jit(solution)/shard_map/backward/pallas_call | solution.py:402
  (26 shorter events, 0.2 us)
Async XLA Ops:
  1.3 6.6 %collective-permute-start = (bf16[2,1,1,16,128]{4,3,0,2,1:T(8,128)(2,1)S(1)}, bf16[2,1,1,16,128]{4,3,0,2,1:T(8,128)(2,1)S(1)}, u32[]{:S(2)}, u32[]{:S(2)}) collective-permute-start(bf16[2,1,1,16,128]{4,3,0,2,1:T(8,128)(2,1)S(1)} %fusion.10), channel_id=1, source_target_pairs={{0,8},{4,12},{8,0},{12,4},{1,9},{5,13},{9,1},{13,5},{2,10},{6,14},... | collective-permute-start | bytes 24584 | tf_op jit(solution)/shard_map/slab2/ppermute | solution.py:243
  3.7 17.6 %copy-start = (s32[1,1,1,4,768]{4,3,2,1,0:T(4,128)S(1)}, s32[1,1,1,4,768]{4,3,2,1,0:T(4,128)}, u32[]{:S(2)}) copy-start(s32[1,1,1,4,768]{4,3,2,1,0:T(4,128)} %param.11) | copy-start | bytes 36868
  3.7 17.6 %copy-start.1 = (s32[1,1,1,4,32]{4,3,2,1,0:T(4,128)S(1)}, s32[1,1,1,4,32]{4,3,2,1,0:T(4,128)}, u32[]{:S(2)}) copy-start(s32[1,1,1,4,32]{4,3,2,1,0:T(4,128)} %param.10) | copy-start | bytes 1540
  3.7 17.6 %copy-start.2 = (s32[1,1,1,4]{3,2,1,0:T(1,128)S(1)}, s32[1,1,1,4]{3,2,1,0:T(1,128)}, u32[]{:S(2)}) copy-start(s32[1,1,1,4]{3,2,1,0:T(1,128)} %param.12) | copy-start | bytes 52
  8.0 1.9 %collective-permute-start.1 = (f32[128,128]{1,0:T(8,128)S(1)}, f32[128,128]{1,0:T(8,128)S(1)}, u32[]{:S(2)}, u32[]{:S(2)}) collective-permute-start(f32[128,128]{1,0:T(8,128)S(1)} %pad_maximum_fusion), channel_id=1, source_target_pairs={{0,1},{1,0},{2,3},{3,2},{4,5},{5,4},{6,7},{7,6},{8,9},{9,8},{10,11... | collective-permute-start | bytes 196616 | tf_op jit(solution)/shard_map/rowsum/ppermute | solution.py:251
  10.0 2.8 %collective-permute-start.2 = (bf16[128,128]{1,0:T(8,128)(2,1)S(1)}, bf16[128,128]{1,0:T(8,128)(2,1)S(1)}, u32[]{:S(2)}, u32[]{:S(2)}) collective-permute-start(bf16[128,128]{1,0:T(8,128)(2,1)S(1)} %pad_maximum_fusion.4), channel_id=1, source_target_pairs={{0,2},{2,0},{1,3},{3,1},{4,6},{6,4},{5,7},{7,5},{8,10},{10,8},{9,1... | collective-permute-start | bytes 98312 | tf_op jit(solution)/shard_map/gxsum1/ppermute | solution.py:251
  12.9 4.7 %collective-permute-start.3 = (bf16[160,128]{1,0:T(8,128)(2,1)S(1)}, bf16[160,128]{1,0:T(8,128)(2,1)S(1)}, u32[]{:S(2)}, u32[]{:S(2)}) collective-permute-start(bf16[160,128]{1,0:T(8,128)(2,1)S(1)} %pad_maximum_fusion.2), channel_id=1, source_target_pairs={{1,5},{5,1},{9,13},{13,9},{4,8},{8,4},{3,7},{7,3},{11,15},{15,11},... | collective-permute-start | bytes 122888 | tf_op jit(solution)/shard_map/rims/ppermute | solution.py:251
  17.7 3.6 %collective-permute-start.4 = (bf16[160,128]{1,0:T(8,128)(2,1)S(1)}, bf16[160,128]{1,0:T(8,128)(2,1)S(1)}, u32[]{:S(2)}, u32[]{:S(2)}) collective-permute-start(bf16[160,128]{1,0:T(8,128)(2,1)S(1)} %pad_maximum_fusion.3), channel_id=1, source_target_pairs={{0,1},{1,0},{2,3},{3,2},{4,5},{5,4},{6,7},{7,6},{8,9},{9,8},{10,11... | collective-permute-start | bytes 122888 | tf_op jit(solution)/shard_map/finish/ppermute | solution.py:251
